TPU v7x, 256 devices: a whole 4x4x8 slice. The times are simulated.
256 devices in a mesh: seq: 64 (over z, y_lo, x), head: 4 (over y_hi, core).
Axes of the slice: x: 4, y: 4 (y_hi: 2, y_lo: 2; y = y_hi * 2 + y_lo), z: 8, core: 2. Of those that a mesh axis runs over, the one named last changes fastest.
Arguments:
- queries: bfloat16 [16384, 32, 128], P('seq', 'head'), may hold values from -6 to 6
- key_vectors: bfloat16 [16384, 4, 128], P(('seq', 'head')), may hold values from -6 to 6
- value_vectors: bfloat16 [16384, 4, 128], P(('seq', 'head')), may hold values from -6 to 6
- out_grad: bfloat16 [16384, 32, 128], P('seq', 'head'), may hold values from -6 to 6
Outputs:
- attended: bfloat16 [16384, 32, 128], P('seq', 'head')
- query_grad: bfloat16 [16384, 32, 128], P('seq', 'head')
- key_grad: bfloat16 [16384, 4, 128], P(('seq', 'head'))
- value_grad: bfloat16 [16384, 4, 128], P(('seq', 'head'))
All inputs are finite; a program needn't handle non-finite values.
Results may differ from a plain program's by a relative error of at most 0.035.
Values may be sent and summed in bfloat16 or wider, within the bound.
No kernel may reach another device: no remote copies, remote signals or barrier semaphores. Data moves between devices by JAX's collectives and lax.ppermute only.
A program may use at most 64 MiB of HBM per device.

v0:
```python
import math

import jax
import jax.numpy as jnp
from jax import lax
from jax.sharding import PartitionSpec as P

GROUPS = 4


def in_one_piece(arrays, axis, split_dim, concat_dim, along):
    both = jnp.concatenate(arrays, axis=along)
    whole, at, done = (
        lax.all_to_all(both, axis, split_axis=split_dim, concat_axis=concat_dim, tiled=True),
        0,
        [],
    )
    for a in arrays:
        done.append(lax.slice_in_dim(whole, at, at + a.shape[along], axis=along))
        at += a.shape[along]
    return tuple(done)


def shifted(value, axis, by):
    size = lax.axis_size(axis)
    return lax.ppermute(value, axis, [(i, (i + by) % size) for i in range(size)])


def visible(query_pos, key_pos, group_len, offset, tok_total):
    query_aligned = (query_pos - offset) % tok_total
    key_aligned = (key_pos - offset) % tok_total
    same_group = query_aligned[:, None] // group_len == key_aligned[None, :] // group_len
    return same_group & (key_aligned[None, :] <= query_aligned[:, None])


def per_device(queries, key_vectors, value_vectors, out_grad):
    key_home, value_home = in_one_piece((key_vectors, value_vectors), "head", 1, 0, 2)
    key_home = key_home[:, 0, :]
    value_home = value_home[:, 0, :]
    tok_rows = queries.shape[0]
    half_heads = queries.shape[1] // 2
    head_dim = queries.shape[2]
    score_scale = 1.0 / math.sqrt(head_dim)
    devices = lax.axis_size("seq")
    group_span = devices // GROUPS
    tok_total = devices * tok_rows
    group_len = tok_total // GROUPS
    offsets = (0, group_len // 2)
    my_index = lax.axis_index("seq")
    local_pos = jnp.arange(tok_rows, dtype=jnp.int32)
    query_pos = my_index * tok_rows + local_pos
    q_parts = (queries[:, :half_heads], queries[:, half_heads:])
    grad_parts = (out_grad[:, :half_heads], out_grad[:, half_heads:])

    def key_positions(distance):
        return (my_index - distance) % devices * tok_rows + local_pos

    def scores_of(which_half, key_blk, allowed):
        scores = (
            jnp.einsum(
                "ihd,td->hit", q_parts[which_half], key_blk, preferred_element_type=jnp.float32
            )
            * score_scale
        )
        return jnp.where(allowed[None], scores, -jnp.inf)

    def forward_tile(states, key_blk, value_blk, distance):
        key_pos = key_positions(distance)
        updated = []
        for which_half in range(2):
            allowed = visible(query_pos, key_pos, group_len, offsets[which_half], tok_total)

            def forward_update(current, which_half=which_half, allowed=allowed):
                run_max, run_sum, running = current
                scores = scores_of(which_half, key_blk, allowed)
                new_max = jnp.maximum(run_max, jnp.max(scores, axis=2))
                weights = jnp.exp(scores - new_max[:, :, None])
                factor = jnp.exp(run_max - new_max)
                run_sum = run_sum * factor + jnp.sum(weights, axis=2)
                value_mix = jnp.einsum(
                    "hit,td->ihd",
                    weights.astype(jnp.bfloat16),
                    value_blk,
                    preferred_element_type=jnp.float32,
                )
                running = running * factor.T[:, :, None] + value_mix
                return (new_max, run_sum, running)

            updated.append(
                lax.cond(
                    jnp.any(allowed), forward_update, lambda current: current, states[which_half]
                )
            )
        return tuple(updated)

    def initial_state():
        return (
            jnp.full((half_heads, tok_rows), -jnp.inf, jnp.float32),
            jnp.zeros((half_heads, tok_rows), jnp.float32),
            jnp.zeros((tok_rows, half_heads, head_dim), jnp.float32),
        )

    forward_init = (initial_state(), initial_state())
    levels = (group_span - 1).bit_length()
    window_keys = key_home[None]
    window_values = value_home[None]
    for level_idx in range(levels):
        far_keys, far_values = shifted((window_keys, window_values), "seq", 2**level_idx)
        window_keys = jnp.concatenate([window_keys, far_keys], axis=0)
        window_values = jnp.concatenate([window_values, far_values], axis=0)

    def window_forward(distance, states):
        return forward_tile(states, window_keys[distance], window_values[distance], distance)

    states = lax.fori_loop(0, group_span, window_forward, forward_init)
    attended_parts = []
    log_totals = []
    deltas = []
    for which_half in range(2):
        run_max, run_sum, running = states[which_half]
        part_out = (running / run_sum.T[:, :, None]).astype(jnp.bfloat16)
        attended_parts.append(part_out)
        log_totals.append(run_max + jnp.log(run_sum))
        deltas.append(
            jnp.einsum(
                "ihd,ihd->hi", grad_parts[which_half], part_out, preferred_element_type=jnp.float32
            )
        )

    def backward_tile(current, key_blk, value_blk, distance):
        query_grads, key_acc, value_acc = current
        key_pos = key_positions(distance)
        new_query = []
        for which_half in range(2):
            allowed = visible(query_pos, key_pos, group_len, offsets[which_half], tok_total)

            def backward_update(inputs, which_half=which_half, allowed=allowed):
                query_acc, key_sum, value_sum = inputs
                scores = scores_of(which_half, key_blk, allowed)
                prob_full = jnp.exp(scores - log_totals[which_half][:, :, None])
                weights = prob_full.astype(jnp.bfloat16)
                prob_grad = jnp.einsum(
                    "ihd,td->hit",
                    grad_parts[which_half],
                    value_blk,
                    preferred_element_type=jnp.float32,
                )
                score_grad = (prob_full * (prob_grad - deltas[which_half][:, :, None])).astype(
                    jnp.bfloat16
                )
                query_acc = query_acc + jnp.einsum(
                    "hit,td->ihd", score_grad, key_blk, preferred_element_type=jnp.float32
                )
                key_sum = key_sum + jnp.einsum(
                    "hit,ihd->td",
                    score_grad,
                    q_parts[which_half],
                    preferred_element_type=jnp.float32,
                )
                value_sum = value_sum + jnp.einsum(
                    "hit,ihd->td",
                    weights,
                    grad_parts[which_half],
                    preferred_element_type=jnp.float32,
                )
                return (query_acc, key_sum, value_sum)

            query_acc, key_acc, value_acc = lax.cond(
                jnp.any(allowed),
                backward_update,
                lambda inputs: inputs,
                (query_grads[which_half], key_acc, value_acc),
            )
            new_query.append(query_acc)
        return (tuple(new_query), key_acc, value_acc)

    zero_query = jnp.zeros((tok_rows, half_heads, head_dim), jnp.float32)
    window_len = 2**levels
    key_buffer = jnp.zeros((window_len, tok_rows, head_dim), jnp.float32)
    value_buffer = jnp.zeros((window_len, tok_rows, head_dim), jnp.float32)

    def window_backward(distance, packed):
        query_grads, key_buffer, value_buffer = packed
        query_grads, key_acc, value_acc = backward_tile(
            (query_grads, key_buffer[distance], value_buffer[distance]),
            window_keys[distance],
            window_values[distance],
            distance,
        )
        key_buffer = lax.dynamic_update_index_in_dim(key_buffer, key_acc, distance, 0)
        value_buffer = lax.dynamic_update_index_in_dim(value_buffer, value_acc, distance, 0)
        return (query_grads, key_buffer, value_buffer)

    query_grads, key_buffer, value_buffer = lax.fori_loop(
        0, group_span, window_backward, ((zero_query, zero_query), key_buffer, value_buffer)
    )
    for level_idx in reversed(range(levels)):
        reach_len = 2**level_idx
        far_keys, far_values = (
            shifted(
                key_buffer[reach_len : 2 * reach_len].astype(jnp.bfloat16), "seq", -reach_len
            ).astype(jnp.float32),
            shifted(
                value_buffer[reach_len : 2 * reach_len].astype(jnp.bfloat16), "seq", -reach_len
            ).astype(jnp.float32),
        )
        key_buffer = key_buffer[:reach_len] + far_keys
        value_buffer = value_buffer[:reach_len] + far_values
    key_acc = key_buffer[0]
    value_acc = value_buffer[0]
    attended = jnp.concatenate(attended_parts, axis=1)
    query_grad = (jnp.concatenate(query_grads, axis=1) * score_scale).astype(jnp.bfloat16)
    key_home_grad = (key_acc * score_scale).astype(jnp.bfloat16)[:, None, :]
    value_home_grad = value_acc.astype(jnp.bfloat16)[:, None, :]
    key_grad, value_grad = in_one_piece((key_home_grad, value_home_grad), "head", 0, 1, 2)
    return (attended, query_grad, key_grad, value_grad)


def solution(mesh):
    return jax.shard_map(
        per_device,
        mesh=mesh,
        in_specs=(
            P("seq", "head", None),
            P(("seq", "head"), None, None),
            P(("seq", "head"), None, None),
            P("seq", "head", None),
        ),
        out_specs=(
            P("seq", "head", None),
            P("seq", "head", None),
            P(("seq", "head"), None, None),
            P(("seq", "head"), None, None),
        ),
        check_vma=False,
    )
```

profile of v0, /device:TPU:1, one launch (start us, length us, event | category | flops | bytes accessed | tf_op | source)
XLA Modules:
  0.0 360.5 jit_solution(7658212550162454100)
XLA Ops:
  3.1 6.5 %all-to-all-start = ((bf16[64,4,256]{2,0,1:T(8,128)(2,1)}), bf16[64,4,256]{2,0,1:T(8,128)(2,1)S(1)}, u32[]{:S(2)}, u32[]{:S(2)}) async-start(bf16[64,4,256]{2,0,1:T(8,128)(2,1)} %pad_maximum_fusion.5), calls=%async_computation | async-start | bytes 262144 | tf_op jit(solution)/shard_map/all_to_all | solution.py:14
  11.0 3.7 %all-to-all-done = bf16[64,4,256]{2,0,1:T(8,128)(2,1)S(1)} async-done(((bf16[64,4,256]{2,0,1:T(8,128)(2,1)}), bf16[64,4,256]{2,0,1:T(8,128)(2,1)S(1)}, u32[]{:S(2)}, u32[]{:S(2)}) %all-to-all-start) | async-done | bytes 131104 | tf_op jit(solution)/shard_map/all_to_all | solution.py:14
  17.1 6.7 %collective-permute-done = bf16[1,256,128]{2,1,0:T(8,128)(2,1)S(1)} collective-permute-done((bf16[1,256,128]{2,1,0:T(8,128)(2,1)S(1)}, bf16[1,256,128]{2,1,0:T(8,128)(2,1)S(1)}, u32[]{:S(2)}, u32[]{:S(2)}) %collective-permute-start) | collective-permute-done | bytes 65568 | tf_op jit(solution)/shard_map/ppermute | solution.py:26
  25.0 7.1 %collective-permute-done.1 = bf16[2,256,128]{2,1,0:T(8,128)(2,1)S(1)} collective-permute-done((bf16[2,256,128]{2,1,0:T(8,128)(2,1)S(1)}, bf16[2,256,128]{2,1,0:T(8,128)(2,1)S(1)}, u32[]{:S(2)}, u32[]{:S(2)}) %collective-permute-start.1) | collective-permute-done | bytes 131104 | tf_op jit(solution)/shard_map/ppermute | solution.py:26
  32.3 1.8 collective-permute-done.5
  34.3 6.4 %collective-permute-done.2 = bf16[4,256,128]{2,1,0:T(8,128)(2,1)S(1)} collective-permute-done((bf16[4,256,128]{2,1,0:T(8,128)(2,1)S(1)}, bf16[4,256,128]{2,1,0:T(8,128)(2,1)S(1)}, u32[]{:S(2)}, u32[]{:S(2)}) %collective-permute-start.2) | collective-permute-done | bytes 262176 | tf_op jit(solution)/shard_map/ppermute | solution.py:26
  40.8 4.3 %collective-permute-done.6 = bf16[4,256,128]{2,1,0:T(8,128)(2,1)S(1)} collective-permute-done((bf16[4,256,128]{2,1,0:T(8,128)(2,1)S(1)}, bf16[4,256,128]{2,1,0:T(8,128)(2,1)S(1)}, u32[]{:S(2)}, u32[]{:S(2)}) %collective-permute-start.6) | collective-permute-done | bytes 262176 | tf_op jit(solution)/shard_map/ppermute | solution.py:26
  45.6 4.7 %collective-permute-done.3 = bf16[8,256,128]{2,1,0:T(8,128)(2,1)S(1)} collective-permute-done((bf16[8,256,128]{2,1,0:T(8,128)(2,1)S(1)}, bf16[8,256,128]{2,1,0:T(8,128)(2,1)S(1)}, u32[]{:S(2)}, u32[]{:S(2)}) %collective-permute-start.3) | collective-permute-done | bytes 524320 | tf_op jit(solution)/shard_map/ppermute | solution.py:26
  50.4 8.7 %collective-permute-done.7 = bf16[8,256,128]{2,1,0:T(8,128)(2,1)S(1)} collective-permute-done((bf16[8,256,128]{2,1,0:T(8,128)(2,1)S(1)}, bf16[8,256,128]{2,1,0:T(8,128)(2,1)S(1)}, u32[]{:S(2)}, u32[]{:S(2)}) %collective-permute-start.7) | collective-permute-done | bytes 524320 | tf_op jit(solution)/shard_map/ppermute | solution.py:26
  60.2 70.2 %while.54 = (s32[]{:T(128)}, f32[4,256]{1,0:T(4,128)S(1)}, f32[4,256]{1,0:T(4,128)S(1)}, f32[256,4,128]{2,0,1:T(8,128)S(1)}, f32[4,256]{1,0:T(4,128)S(1)}, /*ind...) while((s32[]{:T(128)}, f32[4,256]{1,0:T(4,128)S(1)}, ...), condition=%wide.region_11.12_spmd.clone.clone, body=%wide.region_0.11_spmd.clone.clone.sunk | while | flops 273188352 | bytes 9847346 | solution.py:115
  132.8 1.6 broadcast.1413
  134.3 1.5 broadcast.1413.clone
  135.9 116.0 %while.55 = (s32[]{:T(128)}, f32[256,4,128]{2,0,1:T(8,128)S(1)}, f32[256,4,128]{2,0,1:T(8,128)S(1)}, f32[16,256,128]{2,1,0:T(8,128)}, f32[16,256,128]{2,1,0:T(8,...) while((s32[]{:T(128)}, f32[256,4,128]{2,0,1:T(8,128)S(1)}, ...), condition=%wide.region_19.20_spmd.clone.clone, body=%wide.region_12.19_spmd.clone.clone.sunk | while | flops 675704320 | bytes 16679558 | solution.py:194
  139.2 1.7 conditional.18
  142.4 1.7 conditional.19
  150.2 1.7 conditional.19
  158.1 1.7 conditional.19
  166.0 1.7 conditional.19
  173.9 1.7 conditional.19
  181.7 1.7 conditional.19
  189.6 1.7 conditional.19
  197.5 1.7 conditional.19
  205.3 1.7 conditional.19
  255.0 6.5 %collective-permute-done.12 = bf16[8,256,128]{2,1,0:T(8,128)(2,1)S(1)} collective-permute-done((bf16[8,256,128]{2,1,0:T(8,128)(2,1)S(1)}, bf16[8,256,128]{2,1,0:T(8,128)(2,1)S(1)}, u32[]{:S(2)}, u32[]{:S(2)}) %collective-permute-start.12) | collective-permute-done | bytes 524320 | tf_op jit(solution)/shard_map/ppermute | solution.py:26
  261.6 32.4 %collective-permute-start.13 = (bf16[4,256,128]{2,1,0:T(8,128)(2,1)S(1)}, bf16[4,256,128]{2,1,0:T(8,128)(2,1)S(1)}, u32[]{:S(2)}, u32[]{:S(2)}) collective-permute-start(bf16[4,256,128]{2,1,0:T(8,128)(2,1)S(1)} %slice.156), channel_id=1, source_target_pairs={{0,240},{4,244},{8,248},{12,252},{16,0},{20,4},{24,8},{28,12},{32,... | collective-permute-start | bytes 786440 | tf_op jit(solution)/shard_map/ppermute | solution.py:26
  294.1 11.1 %collective-permute-start.9 = (bf16[4,256,128]{2,1,0:T(8,128)(2,1)S(1)}, bf16[4,256,128]{2,1,0:T(8,128)(2,1)S(1)}, u32[]{:S(2)}, u32[]{:S(2)}) collective-permute-start(bf16[4,256,128]{2,1,0:T(8,128)(2,1)S(1)} %slice.157), channel_id=1, source_target_pairs={{0,240},{4,244},{8,248},{12,252},{16,0},{20,4},{24,8},{28,12},{32,... | collective-permute-start | bytes 786440 | tf_op jit(solution)/shard_map/ppermute | solution.py:26
  307.1 15.0 %collective-permute-start.14 = (bf16[2,256,128]{2,1,0:T(8,128)(2,1)S(1)}, bf16[2,256,128]{2,1,0:T(8,128)(2,1)S(1)}, u32[]{:S(2)}, u32[]{:S(2)}) collective-permute-start(bf16[2,256,128]{2,1,0:T(8,128)(2,1)S(1)} %slice.158), channel_id=1, source_target_pairs={{0,248},{4,252},{8,0},{12,4},{16,8},{20,12},{24,16},{28,20},{32,24... | collective-permute-start | bytes 393224 | tf_op jit(solution)/shard_map/ppermute | solution.py:26
  322.2 5.2 %collective-permute-start.10 = (bf16[2,256,128]{2,1,0:T(8,128)(2,1)S(1)}, bf16[2,256,128]{2,1,0:T(8,128)(2,1)S(1)}, u32[]{:S(2)}, u32[]{:S(2)}) collective-permute-start(bf16[2,256,128]{2,1,0:T(8,128)(2,1)S(1)} %slice.159), channel_id=1, source_target_pairs={{0,248},{4,252},{8,0},{12,4},{16,8},{20,12},{24,16},{28,20},{32,24... | collective-permute-start | bytes 393224 | tf_op jit(solution)/shard_map/ppermute | solution.py:26
  327.5 8.0 %collective-permute-start.15 = (bf16[1,256,128]{2,1,0:T(8,128)(2,1)S(1)}, bf16[1,256,128]{2,1,0:T(8,128)(2,1)S(1)}, u32[]{:S(2)}, u32[]{:S(2)}) collective-permute-start(bf16[1,256,128]{2,1,0:T(8,128)(2,1)S(1)} %slice.160), channel_id=1, source_target_pairs={{0,252},{4,0},{8,4},{12,8},{16,12},{20,16},{24,20},{28,24},{32,28}... | collective-permute-start | bytes 196616 | tf_op jit(solution)/shard_map/ppermute | solution.py:26
  335.5 3.9 %collective-permute-start.11 = (bf16[1,256,128]{2,1,0:T(8,128)(2,1)S(1)}, bf16[1,256,128]{2,1,0:T(8,128)(2,1)S(1)}, u32[]{:S(2)}, u32[]{:S(2)}) collective-permute-start(bf16[1,256,128]{2,1,0:T(8,128)(2,1)S(1)} %slice.161), channel_id=1, source_target_pairs={{0,252},{4,0},{8,4},{12,8},{16,12},{20,16},{24,20},{28,24},{32,28}... | collective-permute-start | bytes 196616 | tf_op jit(solution)/shard_map/ppermute | solution.py:26
  342.8 11.1 %all-to-all-start.1 = ((bf16[4,2,8192]{2,1,0:T(2,128)(2,1)}), bf16[4,2,8192]{2,1,0:T(2,128)(2,1)S(1)}, u32[]{:S(2)}, u32[]{:S(2)}) async-start(bf16[4,2,8192]{2,1,0:T(2,128)(2,1)} %reshape.465), calls=%async_computation.1 | async-start | bytes 262144 | tf_op jit(solution)/shard_map/all_to_all | solution.py:14
  354.9 4.0 %all-to-all-done.1 = bf16[4,2,8192]{2,1,0:T(2,128)(2,1)S(1)} async-done(((bf16[4,2,8192]{2,1,0:T(2,128)(2,1)}), bf16[4,2,8192]{2,1,0:T(2,128)(2,1)S(1)}, u32[]{:S(2)}, u32[]{:S(2)}) %all-to-all-start.1) | async-done | bytes 131104 | tf_op jit(solution)/shard_map/all_to_all | solution.py:14
  (532 shorter events, 177.6 us)
Async XLA Ops:
  0.6 14.8 %copy-start.2 = (bf16[256,8,128]{2,1,0:T(8,128)(2,1)S(1)}, bf16[256,8,128]{2,1,0:T(8,128)(2,1)}, u32[]{:S(2)}) copy-start(bf16[256,8,128]{2,1,0:T(8,128)(2,1)} %param.19) | copy-start | bytes 1572868
  3.1 11.6 %all-to-all-start = ((bf16[64,4,256]{2,0,1:T(8,128)(2,1)}), bf16[64,4,256]{2,0,1:T(8,128)(2,1)S(1)}, u32[]{:S(2)}, u32[]{:S(2)}) async-start(bf16[64,4,256]{2,0,1:T(8,128)(2,1)} %pad_maximum_fusion.5), calls=%async_computation | async-start | bytes 262144 | tf_op jit(solution)/shard_map/all_to_all | solution.py:14
  14.7 9.1 %collective-permute-start = (bf16[1,256,128]{2,1,0:T(8,128)(2,1)S(1)}, bf16[1,256,128]{2,1,0:T(8,128)(2,1)S(1)}, u32[]{:S(2)}, u32[]{:S(2)}) collective-permute-start(bf16[1,256,128]{2,1,0:T(8,128)(2,1)S(1)} %get-tuple-element.1546), channel_id=1, source_target_pairs={{0,4},{4,8},{8,12},{12,16},{16,20},{20,24},{24,28},{28,32},{32,36}... | collective-permute-start | bytes 196616 | tf_op jit(solution)/shard_map/ppermute | solution.py:26
  15.8 9.1 %collective-permute-start.4 = (bf16[1,256,128]{2,1,0:T(8,128)(2,1)S(1)}, bf16[1,256,128]{2,1,0:T(8,128)(2,1)S(1)}, u32[]{:S(2)}, u32[]{:S(2)}) collective-permute-start(bf16[1,256,128]{2,1,0:T(8,128)(2,1)S(1)} %get-tuple-element.1545), channel_id=1, source_target_pairs={{0,4},{4,8},{8,12},{12,16},{16,20},{20,24},{24,28},{28,32},{32,36}... | collective-permute-start | bytes 196616 | tf_op jit(solution)/shard_map/ppermute | solution.py:26
  23.8 8.4 %collective-permute-start.1 = (bf16[2,256,128]{2,1,0:T(8,128)(2,1)S(1)}, bf16[2,256,128]{2,1,0:T(8,128)(2,1)S(1)}, u32[]{:S(2)}, u32[]{:S(2)}) collective-permute-start(bf16[2,256,128]{2,1,0:T(8,128)(2,1)S(1)} %pad_maximum_fusion.6), channel_id=1, source_target_pairs={{0,8},{4,12},{8,16},{12,20},{16,24},{20,28},{24,32},{28,36},{32,40... | collective-permute-start | bytes 393224 | tf_op jit(solution)/shard_map/ppermute | solution.py:26
  24.9 9.2 %collective-permute-start.5 = (bf16[2,256,128]{2,1,0:T(8,128)(2,1)S(1)}, bf16[2,256,128]{2,1,0:T(8,128)(2,1)S(1)}, u32[]{:S(2)}, u32[]{:S(2)}) collective-permute-start(bf16[2,256,128]{2,1,0:T(8,128)(2,1)S(1)} %pad_maximum_fusion.7), channel_id=1, source_target_pairs={{0,8},{4,12},{8,16},{12,20},{16,24},{20,28},{24,32},{28,36},{32,40... | collective-permute-start | bytes 393224 | tf_op jit(solution)/shard_map/ppermute | solution.py:26
  32.2 8.5 %collective-permute-start.2 = (bf16[4,256,128]{2,1,0:T(8,128)(2,1)S(1)}, bf16[4,256,128]{2,1,0:T(8,128)(2,1)S(1)}, u32[]{:S(2)}, u32[]{:S(2)}) collective-permute-start(bf16[4,256,128]{2,1,0:T(8,128)(2,1)S(1)} %pad_maximum_fusion.3), channel_id=1, source_target_pairs={{0,16},{4,20},{8,24},{12,28},{16,32},{20,36},{24,40},{28,44},{32,4... | collective-permute-start | bytes 786440 | tf_op jit(solution)/shard_map/ppermute | solution.py:26
  34.1 11.0 %collective-permute-start.6 = (bf16[4,256,128]{2,1,0:T(8,128)(2,1)S(1)}, bf16[4,256,128]{2,1,0:T(8,128)(2,1)S(1)}, u32[]{:S(2)}, u32[]{:S(2)}) collective-permute-start(bf16[4,256,128]{2,1,0:T(8,128)(2,1)S(1)} %pad_maximum_fusion.4), channel_id=1, source_target_pairs={{0,16},{4,20},{8,24},{12,28},{16,32},{20,36},{24,40},{28,44},{32,4... | collective-permute-start | bytes 786440 | tf_op jit(solution)/shard_map/ppermute | solution.py:26
  40.7 9.6 %collective-permute-start.3 = (bf16[8,256,128]{2,1,0:T(8,128)(2,1)S(1)}, bf16[8,256,128]{2,1,0:T(8,128)(2,1)S(1)}, u32[]{:S(2)}, u32[]{:S(2)}) collective-permute-start(bf16[8,256,128]{2,1,0:T(8,128)(2,1)S(1)} %pad_maximum_fusion), channel_id=1, source_target_pairs={{0,32},{4,36},{8,40},{12,44},{16,48},{20,52},{24,56},{28,60},{32,6... | collective-permute-start | bytes 1572872 | tf_op jit(solution)/shard_map/ppermute | solution.py:26
  45.2 13.9 %collective-permute-start.7 = (bf16[8,256,128]{2,1,0:T(8,128)(2,1)S(1)}, bf16[8,256,128]{2,1,0:T(8,128)(2,1)S(1)}, u32[]{:S(2)}, u32[]{:S(2)}) collective-permute-start(bf16[8,256,128]{2,1,0:T(8,128)(2,1)S(1)} %pad_maximum_fusion.1), channel_id=1, source_target_pairs={{0,32},{4,36},{8,40},{12,44},{16,48},{20,52},{24,56},{28,60},{32,6... | collective-permute-start | bytes 1572872 | tf_op jit(solution)/shard_map/ppermute | solution.py:26
  50.4 8.9 %copy-start.4 = (bf16[16,256,128]{2,1,0:T(8,128)(2,1)}, bf16[16,256,128]{2,1,0:T(8,128)(2,1)S(1)}, u32[]{:S(2)}) copy-start(bf16[16,256,128]{2,1,0:T(8,128)(2,1)S(1)} %constant_dynamic-update-slice_fusion.2) | copy-start | bytes 3145732
  59.2 1.0 copy-start.3
  251.9 9.6 %copy-start.1 = (f32[16,256,128]{2,1,0:T(8,128)S(1)}, f32[16,256,128]{2,1,0:T(8,128)}, u32[]{:S(2)}) copy-start(f32[16,256,128]{2,1,0:T(8,128)} %get-tuple-element.1247) | copy-start | bytes 6291460
  253.3 8.1 %collective-permute-start.12 = (bf16[8,256,128]{2,1,0:T(8,128)(2,1)S(1)}, bf16[8,256,128]{2,1,0:T(8,128)(2,1)S(1)}, u32[]{:S(2)}, u32[]{:S(2)}) collective-permute-start(bf16[8,256,128]{2,1,0:T(8,128)(2,1)S(1)} %slice.154), channel_id=1, source_target_pairs={{0,224},{4,228},{8,232},{12,236},{16,240},{20,244},{24,248},{28,25... | collective-permute-start | bytes 1572872 | tf_op jit(solution)/shard_map/ppermute | solution.py:26
  253.4 40.6 %copy-start = (f32[16,256,128]{2,1,0:T(8,128)S(1)}, f32[16,256,128]{2,1,0:T(8,128)}, u32[]{:S(2)}) copy-start(f32[16,256,128]{2,1,0:T(8,128)} %get-tuple-element.1246) | copy-start | bytes 6291460
  254.9 39.1 %collective-permute-start.8 = (bf16[8,256,128]{2,1,0:T(8,128)(2,1)S(1)}, bf16[8,256,128]{2,1,0:T(8,128)(2,1)S(1)}, u32[]{:S(2)}, u32[]{:S(2)}) collective-permute-start(bf16[8,256,128]{2,1,0:T(8,128)(2,1)S(1)} %slice.155), channel_id=1, source_target_pairs={{0,224},{4,228},{8,232},{12,236},{16,240},{20,244},{24,248},{28,25... | collective-permute-start | bytes 1572872 | tf_op jit(solution)/shard_map/ppermute | solution.py:26
  261.6 45.4 %collective-permute-start.13 = (bf16[4,256,128]{2,1,0:T(8,128)(2,1)S(1)}, bf16[4,256,128]{2,1,0:T(8,128)(2,1)S(1)}, u32[]{:S(2)}, u32[]{:S(2)}) collective-permute-start(bf16[4,256,128]{2,1,0:T(8,128)(2,1)S(1)} %slice.156), channel_id=1, source_target_pairs={{0,240},{4,244},{8,248},{12,252},{16,0},{20,4},{24,8},{28,12},{32,... | collective-permute-start | bytes 786440 | tf_op jit(solution)/shard_map/ppermute | solution.py:26
  294.1 28.0 %collective-permute-start.9 = (bf16[4,256,128]{2,1,0:T(8,128)(2,1)S(1)}, bf16[4,256,128]{2,1,0:T(8,128)(2,1)S(1)}, u32[]{:S(2)}, u32[]{:S(2)}) collective-permute-start(bf16[4,256,128]{2,1,0:T(8,128)(2,1)S(1)} %slice.157), channel_id=1, source_target_pairs={{0,240},{4,244},{8,248},{12,252},{16,0},{20,4},{24,8},{28,12},{32,... | collective-permute-start | bytes 786440 | tf_op jit(solution)/shard_map/ppermute | solution.py:26
  307.1 20.4 %collective-permute-start.14 = (bf16[2,256,128]{2,1,0:T(8,128)(2,1)S(1)}, bf16[2,256,128]{2,1,0:T(8,128)(2,1)S(1)}, u32[]{:S(2)}, u32[]{:S(2)}) collective-permute-start(bf16[2,256,128]{2,1,0:T(8,128)(2,1)S(1)} %slice.158), channel_id=1, source_target_pairs={{0,248},{4,252},{8,0},{12,4},{16,8},{20,12},{24,16},{28,20},{32,24... | collective-permute-start | bytes 393224 | tf_op jit(solution)/shard_map/ppermute | solution.py:26
  322.2 13.3 %collective-permute-start.10 = (bf16[2,256,128]{2,1,0:T(8,128)(2,1)S(1)}, bf16[2,256,128]{2,1,0:T(8,128)(2,1)S(1)}, u32[]{:S(2)}, u32[]{:S(2)}) collective-permute-start(bf16[2,256,128]{2,1,0:T(8,128)(2,1)S(1)} %slice.159), channel_id=1, source_target_pairs={{0,248},{4,252},{8,0},{12,4},{16,8},{20,12},{24,16},{28,20},{32,24... | collective-permute-start | bytes 393224 | tf_op jit(solution)/shard_map/ppermute | solution.py:26
  327.5 11.9 %collective-permute-start.15 = (bf16[1,256,128]{2,1,0:T(8,128)(2,1)S(1)}, bf16[1,256,128]{2,1,0:T(8,128)(2,1)S(1)}, u32[]{:S(2)}, u32[]{:S(2)}) collective-permute-start(bf16[1,256,128]{2,1,0:T(8,128)(2,1)S(1)} %slice.160), channel_id=1, source_target_pairs={{0,252},{4,0},{8,4},{12,8},{16,12},{20,16},{24,20},{28,24},{32,28}... | collective-permute-start | bytes 196616 | tf_op jit(solution)/shard_map/ppermute | solution.py:26
  335.5 5.3 %collective-permute-start.11 = (bf16[1,256,128]{2,1,0:T(8,128)(2,1)S(1)}, bf16[1,256,128]{2,1,0:T(8,128)(2,1)S(1)}, u32[]{:S(2)}, u32[]{:S(2)}) collective-permute-start(bf16[1,256,128]{2,1,0:T(8,128)(2,1)S(1)} %slice.161), channel_id=1, source_target_pairs={{0,252},{4,0},{8,4},{12,8},{16,12},{20,16},{24,20},{28,24},{32,28}... | collective-permute-start | bytes 196616 | tf_op jit(solution)/shard_map/ppermute | solution.py:26
  342.8 16.2 %all-to-all-start.1 = ((bf16[4,2,8192]{2,1,0:T(2,128)(2,1)}), bf16[4,2,8192]{2,1,0:T(2,128)(2,1)S(1)}, u32[]{:S(2)}, u32[]{:S(2)}) async-start(bf16[4,2,8192]{2,1,0:T(2,128)(2,1)} %reshape.465), calls=%async_computation.1 | async-start | bytes 262144 | tf_op jit(solution)/shard_map/all_to_all | solution.py:14
where the time goes:
time: 363 us; the launch traced here: 360 us
  starting transfers between devices  96.1 us (26%)
  local copies, waits for them, and re-layouts  80.3 us (22%)
  other arithmetic  59.4 us (16%)
  waiting for transfers between devices  56.4 us (16%)
  loops' own time  42.8 us (12%)
  matrix products  24.3 us (7%)
    ppermute x16, starting transfers between devices, shifted(): lax.ppermute(value, axis, [(i, (i + by) % size) for i in range(size)])  78.5 us
    ppermute x16, waiting for transfers between devices, shifted(): lax.ppermute(value, axis, [(i, (i + by) % size) for i in range(size)])  48.7 us
    reduce_or x32, other arithmetic, backward_tile(): jnp.any(allowed)  24.7 us
    reduce_or x32, other arithmetic, forward_tile(): jnp.any(allowed)  24.4 us
    another operation x1, loops' own time, per_device(): lax.fori_loop(0, group_span, window_backward, ((zero_query, zero_query),...  21.7 us
    another operation x1, loops' own time, per_device(): states = lax.fori_loop(0, group_span, window_forward, forward_init)  19.4 us
    all_to_all x2, starting transfers between devices, in_one_piece(): lax.all_to_all(both, axis, split_axis=split_dim, concat_axis=concat_dim,...  17.6 us
    squeeze x16, local copies, waits for them, and re-layouts, window_backward(): value_buffer[distance]  15.9 us
  transfers between devices with their start and end apart: 18, of which 12 were waited for; matrix products, arithmetic and copies ran while one was open for 2% of the time, Pallas kernels for 0%

commit v1 on v0

v1 whole, which is shorter than its diff:
```python
import functools
import math

import jax
import jax.numpy as jnp
from jax import lax
from jax.experimental import pallas as pl
from jax.experimental.pallas import tpu as pltpu
from jax.sharding import Mesh, PartitionSpec as P

BLOCK = 256
DIM = 128
HEADS = 8
HALF = 4
NX = 4
SCALE = 1.0 / math.sqrt(DIM)
TO_LOG2 = SCALE * math.log2(math.e)
F32 = jnp.float32
BF16 = jnp.bfloat16
COLUMN = ("ylo", "yhi", "core")


def dot(a, b):
    return jnp.dot(a, b, preferred_element_type=F32)


def causal():
    t = lax.broadcasted_iota(jnp.int32, (BLOCK, BLOCK), 0)
    i = lax.broadcasted_iota(jnp.int32, (BLOCK, BLOCK), 1)
    return t <= i


def slot_of(rank, x):
    return lax.rem(x - lax.rem(rank, NX) + NX, NX) * 2 + lax.div(rank, NX)


def forward_own(place, kv, q_t, acc, top, total):
    x = place[0]
    rank = place[1]

    def tile(slot, diagonal):
        key = kv[slot, :, :DIM]
        value_t = kv[slot, :, DIM:].T
        for h in range(HEADS):
            s = dot(key, q_t[h])
            if diagonal:
                s = jnp.where(causal(), s, -jnp.inf)
                new_top = jnp.max(s, axis=0, keepdims=True)
                w = jnp.exp2((s - new_top) * TO_LOG2)
                total[h : h + 1, :] = jnp.sum(w, axis=0, keepdims=True)
                acc[h] = dot(value_t, w.astype(BF16))
            else:
                old_top = top[h : h + 1, :]
                new_top = jnp.maximum(old_top, jnp.max(s, axis=0, keepdims=True))
                w = jnp.exp2((s - new_top) * TO_LOG2)
                fade = jnp.exp2((old_top - new_top) * TO_LOG2)
                total[h : h + 1, :] = total[h : h + 1, :] * fade + jnp.sum(w, axis=0, keepdims=True)
                acc[h] = acc[h] * fade + dot(value_t, w.astype(BF16))
            top[h : h + 1, :] = new_top

    tile(slot_of(rank, x), True)

    def step(b, carry):
        tile(slot_of(b, x), False)
        return carry

    lax.fori_loop(0, rank, step, 0)


def middle(place, kv, q_t, q, g_t, g, acc, top, total, out_t, log_total, delta, dq_t, dkv, acc2, top2, total2):
    wide = place[2]
    acc2[...] = acc[pl.ds(wide, HALF)]
    for h in range(HALF):
        top2[h : h + 1, :] = top[pl.ds(wide + h, 1), :]
        total2[h : h + 1, :] = total[pl.ds(wide + h, 1), :]

    def forward(b, carry):
        key = kv[b, :, :DIM]
        value_t = kv[b, :, DIM:].T
        for h in range(HALF):
            s = dot(key, q_t[wide + h])
            old_top = top2[h : h + 1, :]
            new_top = jnp.maximum(old_top, jnp.max(s, axis=0, keepdims=True))
            w = jnp.exp2((s - new_top) * TO_LOG2)
            fade = jnp.exp2((old_top - new_top) * TO_LOG2)
            total2[h : h + 1, :] = total2[h : h + 1, :] * fade + jnp.sum(w, axis=0, keepdims=True)
            acc2[h] = acc2[h] * fade + dot(value_t, w.astype(BF16))
            top2[h : h + 1, :] = new_top
        return carry

    lax.fori_loop(0, 2 * NX, forward, 0)

    def finish(h, a, t, l):
        o = (a / l).astype(BF16)
        out_t[h] = o
        log_total[pl.ds(h, 1), :] = t * TO_LOG2 + jnp.log2(l)
        delta[pl.ds(h, 1), :] = jnp.sum(o.astype(F32) * g_t[h].astype(F32), axis=0, keepdims=True)

    narrow = HALF - wide
    for h in range(HALF):
        finish(wide + h, acc2[h], top2[h : h + 1, :], total2[h : h + 1, :])
        finish(
            narrow + h,
            acc[narrow + h],
            top[pl.ds(narrow + h, 1), :],
            total[pl.ds(narrow + h, 1), :],
        )
    dq_t[...] = jnp.zeros_like(dq_t)

    def backward(b, carry):
        key = kv[b, :, :DIM]
        value = kv[b, :, DIM:]
        key_t = key.T
        dk = dv = None
        for h in range(HALF):
            j = wide + h
            s = dot(key, q_t[j])
            prob = jnp.exp2(s * TO_LOG2 - log_total[pl.ds(j, 1), :])
            prob_grad = dot(value, g_t[j])
            ds = (prob * (prob_grad - delta[pl.ds(j, 1), :])).astype(BF16)
            dv_h = dot(prob.astype(BF16), g[j])
            dk_h = dot(ds, q[j])
            dv = dv_h if dv is None else dv + dv_h
            dk = dk_h if dk is None else dk + dk_h
            dq_t[h] += dot(key_t, ds)
        dkv[b, :, :DIM] = (dk * SCALE).astype(BF16)
        dkv[b, :, DIM:] = dv.astype(BF16)
        return carry

    lax.fori_loop(0, 2 * NX, backward, 0)


def backward_own(place, kv, q_t, q, g_t, g, log_total, delta, dq_wide, dq_out, dkv, dq_t):
    x = place[0]
    rank = place[1]
    wide = place[2]
    dq_t[pl.ds(wide, HALF)] = dq_wide[...]
    dq_t[pl.ds(HALF - wide, HALF)] = jnp.zeros((HALF, DIM, BLOCK), F32)

    def tile(slot, diagonal):
        key = kv[slot, :, :DIM]
        value = kv[slot, :, DIM:]
        key_t = key.T
        dk = dv = None
        for h in range(HEADS):
            s = dot(key, q_t[h])
            prob = jnp.exp2(s * TO_LOG2 - log_total[h : h + 1, :])
            if diagonal:
                prob = jnp.where(causal(), prob, 0.0)
            prob_grad = dot(value, g_t[h])
            ds = (prob * (prob_grad - delta[h : h + 1, :])).astype(BF16)
            dv_h = dot(prob.astype(BF16), g[h])
            dk_h = dot(ds, q[h])
            dv = dv_h if dv is None else dv + dv_h
            dk = dk_h if dk is None else dk + dk_h
            dq_t[h] += dot(key_t, ds)
        dkv[slot, :, :DIM] = (dk * SCALE).astype(BF16)
        dkv[slot, :, DIM:] = dv.astype(BF16)

    def step(b, carry):
        tile(slot_of(b, x), False)
        return carry

    lax.fori_loop(0, rank, step, 0)
    tile(slot_of(rank, x), True)

    def blank(b, carry):
        dkv[slot_of(b, x)] = jnp.zeros((BLOCK, 2 * DIM), BF16)
        return carry

    lax.fori_loop(rank + 1, 2 * NX, blank, 0)
    for h in range(HEADS):
        dq_out[h] = (dq_t[h] * SCALE).astype(BF16)


def call(body, outs, ins, scratch=(), flops=1 << 30):
    vmem = pl.BlockSpec(memory_space=pltpu.VMEM)
    smem = pl.BlockSpec(memory_space=pltpu.SMEM)
    return pl.pallas_call(
        body,
        out_shape=outs,
        in_specs=[smem] + [vmem] * (len(ins) - 1),
        out_specs=[vmem] * len(outs),
        scratch_shapes=list(scratch),
        compiler_params=pltpu.CompilerParams(vmem_limit_bytes=40 << 20),
        cost_estimate=pl.CostEstimate(flops=flops, bytes_accessed=4 << 20, transcendentals=1 << 20),
    )(*ins)


def ring(size, by):
    return [(i, (i + by) % size) for i in range(size)]


def from_row(value):
    parts = [value]
    for by in range(1, NX):
        parts.append(lax.ppermute(value, "x", ring(NX, by)))
    return jnp.stack(parts).reshape(2 * NX, BLOCK, 2 * DIM)


def to_row(grads):
    grads = grads.reshape(NX, 2 * BLOCK, 2 * DIM)
    total = grads[0].astype(F32)
    for by in range(1, NX):
        total = total + lax.ppermute(grads[by], "x", ring(NX, -by)).astype(F32)
    return total


def per_device(queries, key_vectors, value_vectors, out_grad):
    x = lax.axis_index("x")
    z = lax.axis_index("z")
    rank = lax.axis_index("ylo") * NX + x
    wide = jnp.where(z % 2 == 0, HALF, 0)
    place = jnp.stack([x, rank, wide]).astype(jnp.int32)

    both = jnp.concatenate([key_vectors, value_vectors], axis=2)
    both = jnp.concatenate([both, both], axis=1)
    home = lax.all_to_all(both, COLUMN, 1, 0, tiled=True)[:, 0, :]
    own = from_row(home)
    before = from_row(lax.ppermute(home, "z", ring(8, 1)))

    q = jnp.transpose(queries, (1, 0, 2))
    q_t = jnp.transpose(queries, (1, 2, 0))
    g = jnp.transpose(out_grad, (1, 0, 2))
    g_t = jnp.transpose(out_grad, (1, 2, 0))

    sds = jax.ShapeDtypeStruct
    acc_shape = sds((HEADS, DIM, BLOCK), F32)
    row_shape = sds((HEADS, BLOCK), F32)
    acc, top, total = call(
        forward_own,
        [acc_shape, row_shape, row_shape],
        [place, own, q_t],
        flops=4 << 30,
    )
    out_t, log_total, delta, dq_wide, dkv_before = call(
        middle,
        [
            sds((HEADS, DIM, BLOCK), BF16),
            row_shape,
            row_shape,
            sds((HALF, DIM, BLOCK), F32),
            sds((2 * NX, BLOCK, 2 * DIM), BF16),
        ],
        [place, before, q_t, q, g_t, g, acc, top, total],
        [
            pltpu.VMEM((HALF, DIM, BLOCK), F32),
            pltpu.VMEM((HALF, BLOCK), F32),
            pltpu.VMEM((HALF, BLOCK), F32),
        ],
        flops=8 << 30,
    )
    row_before = lax.ppermute(to_row(dkv_before).astype(BF16), "z", ring(8, -1))
    dq_t, dkv_own = call(
        backward_own,
        [sds((HEADS, DIM, BLOCK), BF16), sds((2 * NX, BLOCK, 2 * DIM), BF16)],
        [place, own, q_t, q, g_t, g, log_total, delta, dq_wide],
        [pltpu.VMEM((HEADS, DIM, BLOCK), F32)],
        flops=8 << 30,
    )
    row = (to_row(dkv_own) + row_before.astype(F32)).astype(BF16)
    back = lax.all_to_all(row.reshape(8, 64, 2 * DIM), COLUMN, 0, 0, tiled=True)
    back = back.reshape(2, HALF, 64, 2 * DIM).astype(F32)
    back = jnp.transpose(back[0] + back[1], (1, 0, 2)).astype(BF16)
    attended = jnp.transpose(out_t, (2, 0, 1))
    query_grad = jnp.transpose(dq_t, (2, 0, 1))
    return attended, query_grad, back[:, :, :DIM], back[:, :, DIM:]


def solution(mesh):
    inner = Mesh(mesh.devices.reshape(8, 2, NX, 2, 2), ("z", "ylo", "x", "yhi", "core"))
    tokens = ("z", "ylo", "x")
    heads = ("yhi", "core")
    by_head = P(tokens, heads, None)
    by_token = P(tokens + heads, None, None)
    return jax.shard_map(
        per_device,
        mesh=inner,
        in_specs=(by_head, by_token, by_token, by_head),
        out_specs=(by_head, by_head, by_token, by_token),
        check_vma=False,
    )
```

time: 363 us -> 121 us (0.33)
  local copies, waits for them, and re-layouts: 80.3 us -> 5.43 us
  other arithmetic: 59.4 us -> 2.52 us
  starting transfers between devices: 96.1 us -> 40.8 us
  loops' own time: 42.8 us -> 0 us
  Pallas kernels: 0 us -> 25.7 us
  matrix products: 24.3 us -> 0 us
  waiting for transfers between devices: 56.4 us -> 33.1 us
  blocking collectives: 0 us -> 12.2 us
    ppermute x16 -> x14, starting transfers between devices: 78.5 us -> 23.7 us  [the longest x6 11.2 us: to_row(): total = total + lax.ppermute(grads[by], 'x', ring(NX, -by)).astype(F32)]
    reduce_or x64 -> x0, other arithmetic: 49.1 us -> none  [the longest x32 24.7 us: backward_tile(): jnp.any(allowed)]
    squeeze x48 -> x0, local copies, waits for them, and re-layouts: 44.3 us -> none  [the longest x16 15.9 us: window_backward(): value_buffer[distance]]
    another operation x66 -> x0, loops' own time: 42.8 us -> none  [the longest x1 21.7 us: per_device(): lax.fori_loop(0, group_span, window_backward, ((zero_query, zero_query),...]
    pallas_call x0 -> x3, Pallas kernels: none -> 25.7 us  [call(): pl.pallas_call(body, out_shape=outs, in_specs=[smem] + [vmem] * (len(ins)...]
    dot_general x70 -> x0, matrix products: 24.3 us -> none  [the longest x20 6.91 us: scores_of(): jnp.einsum('ihd,td->hit', q_parts[which_half], key_blk, preferred_element...]
    dynamic_update_slice x32 -> x0, local copies, waits for them, and re-layouts: 21.3 us -> none  [the longest x16 10.7 us: window_backward(): lax.dynamic_update_index_in_dim(key_buffer, key_acc, distance, 0)]
    ppermute x16 -> x14, waiting for transfers between devices: 48.7 us -> 28.9 us  [the longest x6 22.9 us: from_row(): parts.append(lax.ppermute(value, 'x', ring(NX, by)))]
  transfers between devices with their start and end apart: 18 -> 15, of which waited for: 12 -> 11; matrix products, arithmetic and copies ran while one was open for 2% -> 4% of each run, Pallas kernels for 0% -> 5%
where the time goes in v1:
time: 121 us
  starting transfers between devices  40.8 us (34%)
  waiting for transfers between devices  33.1 us (27%)
  Pallas kernels  25.7 us (21%)
  blocking collectives  12.2 us (10%)
  local copies, waits for them, and re-layouts  5.43 us (4%)
  other arithmetic  2.52 us (2%)
    pallas_call x3, Pallas kernels, call(): pl.pallas_call(body, out_shape=outs, in_specs=[smem] + [vmem] * (len(ins)...  25.7 us
    ppermute x6, waiting for transfers between devices, from_row(): parts.append(lax.ppermute(value, 'x', ring(NX, by)))  22.9 us
    all_to_all x1, starting transfers between devices, per_device(): back = lax.all_to_all(row.reshape(8, 64, 2 * DIM), COLUMN, 0, 0, tiled=True)  17.1 us
    all_to_all x1, blocking collectives, per_device(): home = lax.all_to_all(both, COLUMN, 1, 0, tiled=True)[:, 0, :]  12.2 us
    ppermute x6, starting transfers between devices, to_row(): total = total + lax.ppermute(grads[by], 'x', ring(NX, -by)).astype(F32)  11.2 us
    ppermute x6, waiting for transfers between devices, to_row(): total = total + lax.ppermute(grads[by], 'x', ring(NX, -by)).astype(F32)  6.05 us
    ppermute x1, starting transfers between devices, per_device(): row_before = lax.ppermute(to_row(dkv_before).astype(BF16), 'z', ring(8, -1))  5.64 us
    ppermute x6, starting transfers between devices, from_row(): parts.append(lax.ppermute(value, 'x', ring(NX, by)))  5.14 us
  transfers between devices with their start and end apart: 15, of which 11 were waited for; matrix products, arithmetic and copies ran while one was open for 4% of the time, Pallas kernels for 5%

profile of v1, /device:TPU:1, one launch (start us, length us, event | category | flops | bytes accessed | tf_op | source)
XLA Modules:
  0.0 120.7 jit_solution(5585242440995026448)
XLA Ops:
  0.6 0.9 copy.14
  1.6 12.2 %all_to_all.20 = bf16[64,8,256]{2,0,1:T(8,128)(2,1)S(1)} all-to-all(bf16[64,8,256]{2,0,1:T(8,128)(2,1)S(1)} %maximum_maximum_fusion), channel_id=1, replica_groups=mesh['z'=8,'ylo'=2,'x'=4,'yhi'=2,'core'=2] {'ylo','yhi','core'}, dimensions={1} | all-to-all | bytes 524288 | tf_op jit(solution)/shard_map/all_to_all | solution.py:218
  13.8 2.5 %collective-permute-start.6 = (bf16[512,256]{1,0:T(8,128)(2,1)S(1)}, bf16[512,256]{1,0:T(8,128)(2,1)S(1)}, u32[]{:S(2)}, u32[]{:S(2)}) collective-permute-start(bf16[512,256]{1,0:T(8,128)(2,1)S(1)} %bitcast.52), channel_id=1, source_target_pairs={{0,12},{4,0},{8,4},{12,8},{1,13},{5,1},{9,5},{13,9},{2,14},{6,2},{... | collective-permute-start | bytes 786440 | tf_op jit(solution)/shard_map/ppermute | solution.py:197
  16.3 0.5 collective-permute-start.5
  16.8 0.6 collective-permute-start.4
  17.4 1.6 %collective-permute-start = (bf16[512,256]{1,0:T(8,128)(2,1)S(1)}, bf16[512,256]{1,0:T(8,128)(2,1)S(1)}, u32[]{:S(2)}, u32[]{:S(2)}) collective-permute-start(bf16[512,256]{1,0:T(8,128)(2,1)S(1)} %bitcast.55), channel_id=1, source_target_pairs={{0,32},{32,64},{64,96},{96,128},{128,160},{160,192},{192,224},{224... | collective-permute-start | bytes 786440 | tf_op jit(solution)/shard_map/ppermute | solution.py:220
  20.0 1.8 %collective-permute-done.6 = bf16[512,256]{1,0:T(8,128)(2,1)S(1)} collective-permute-done((bf16[512,256]{1,0:T(8,128)(2,1)S(1)}, bf16[512,256]{1,0:T(8,128)(2,1)S(1)}, u32[]{:S(2)}, u32[]{:S(2)}) %collective-permute-start.6) | collective-permute-done | bytes 262176 | tf_op jit(solution)/shard_map/ppermute | solution.py:197
  21.9 2.8 %collective-permute-done.5 = bf16[512,256]{1,0:T(8,128)(2,1)} collective-permute-done((bf16[512,256]{1,0:T(8,128)(2,1)S(1)}, bf16[512,256]{1,0:T(8,128)(2,1)}, u32[]{:S(2)}, u32[]{:S(2)}) %collective-permute-start.5) | collective-permute-done | bytes 262176 | tf_op jit(solution)/shard_map/ppermute | solution.py:197
  24.6 7.1 %collective-permute-done.4 = bf16[512,256]{1,0:T(8,128)(2,1)} collective-permute-done((bf16[512,256]{1,0:T(8,128)(2,1)S(1)}, bf16[512,256]{1,0:T(8,128)(2,1)}, u32[]{:S(2)}, u32[]{:S(2)}) %collective-permute-start.4) | collective-permute-done | bytes 262176 | tf_op jit(solution)/shard_map/ppermute | solution.py:197
  31.8 1.2 pad_maximum_fusion.1
  33.0 0.6 collective-permute-start.2
  33.6 0.8 collective-permute-start.1
  34.5 2.8 %shard_map.75 = (f32[8,128,256]{2,1,0:T(8,128)S(1)}, f32[8,256]{1,0:T(8,128)S(1)}, f32[8,256]{1,0:T(8,128)S(1)}) custom-call(s32[3]{0:T(128)S(1)} %pad_add_fusion.place, bf16[8,256,256]{2,1,0:T(8,128)(2,1)S(1)} %bitcast.42, bf16[8,128,256]{2,1,0:T(8,128)(2,1)S(1)} %bitcast.45), custom_call_target="tpu_custom_call" | custom-call | flops 4294967296 | bytes 4194304 | tf_op jit(solution)/shard_map/pallas_call | solution.py:179
  37.3 3.1 %collective-permute-done.3 = bf16[512,256]{1,0:T(8,128)(2,1)S(1)} collective-permute-done((bf16[512,256]{1,0:T(8,128)(2,1)S(1)}, bf16[512,256]{1,0:T(8,128)(2,1)S(1)}, u32[]{:S(2)}, u32[]{:S(2)}) %collective-permute-start.3) | collective-permute-done | bytes 262176 | tf_op jit(solution)/shard_map/ppermute | solution.py:197
  40.4 1.1 collective-permute-done.2
  41.5 6.9 %collective-permute-done.1 = bf16[512,256]{1,0:T(8,128)(2,1)S(1)} collective-permute-done((bf16[512,256]{1,0:T(8,128)(2,1)S(1)}, bf16[512,256]{1,0:T(8,128)(2,1)S(1)}, u32[]{:S(2)}, u32[]{:S(2)}) %collective-permute-start.1) | collective-permute-done | bytes 262176 | tf_op jit(solution)/shard_map/ppermute | solution.py:197
  48.6 20.0 %shard_map.76 = (bf16[8,128,256]{2,1,0:T(8,128)(2,1)S(1)}, f32[8,256]{1,0:T(8,128)S(1)}, f32[8,256]{1,0:T(8,128)S(1)}, f32[4,128,256]{2,1,0:T(8,128)S(1)}, bf16[8,256,256]{2,1,0:T(8,128)(2,1)S(1)}) custom-call(s32[3]{0:T(128)S(1)} %pad_add_fusion.place, bf16[8,256,256]{2,1,0:T(8,128)(2,1)S(1)} %bitcast.44, bf16[8,128,256]{2,1,0:T(8,128)(2,1)S(1)} %bitcast.46, ...), custom_call_target="tpu_custom_call" | custom-call | flops 8589934592 | bytes 4194304 | tf_op jit(solution)/shard_map/pallas_call | solution.py:179
  68.8 1.1 collective-permute-start.11
  69.9 1.6 %collective-permute-start.10 = (bf16[512,256]{1,0:T(8,128)(2,1)S(1)}, bf16[512,256]{1,0:T(8,128)(2,1)S(1)}, u32[]{:S(2)}, u32[]{:S(2)}) collective-permute-start(bf16[512,256]{1,0:T(8,128)(2,1)S(1)} %bitcast.59), channel_id=1, source_target_pairs={{0,12},{4,0},{8,4},{12,8},{1,13},{5,1},{9,5},{13,9},{2,14},{6,2},{... | collective-permute-start | bytes 786440 | tf_op jit(solution)/shard_map/ppermute | solution.py:205
  71.5 2.9 %shard_map.77 = (bf16[8,128,256]{2,1,0:T(8,128)(2,1)S(1)}, bf16[8,256,256]{2,1,0:T(8,128)(2,1)S(1)}) custom-call(s32[3]{0:T(128)S(1)} %pad_add_fusion.place, bf16[8,256,256]{2,1,0:T(8,128)(2,1)S(1)} %bitcast.43, bf16[8,128,256]{2,1,0:T(8,128)(2,1)S(1)} %bitcast.47, bf16[8,256,128]{2,1,0:T(8,128)(2,1)S(1)} %get-tuple-element.43.q, ...), custom_call_target="tpu_custom_call" | custom-call | flops 8589934592 | bytes 4194304 | tf_op jit(solution)/shard_map/pallas_call | solution.py:179
  74.4 2.7 %collective-permute-start.9 = (bf16[512,256]{1,0:T(8,128)(2,1)S(1)}, bf16[512,256]{1,0:T(8,128)(2,1)S(1)}, u32[]{:S(2)}, u32[]{:S(2)}) collective-permute-start(bf16[512,256]{1,0:T(8,128)(2,1)S(1)} %bitcast.64), channel_id=1, source_target_pairs={{0,4},{4,8},{8,12},{12,0},{1,5},{5,9},{9,13},{13,1},{2,6},{6,10},{... | collective-permute-start | bytes 786440 | tf_op jit(solution)/shard_map/ppermute | solution.py:205
  77.2 5.6 %collective-permute-start.8 = (bf16[512,256]{1,0:T(8,128)(2,1)S(1)}, bf16[512,256]{1,0:T(8,128)(2,1)S(1)}, u32[]{:S(2)}, u32[]{:S(2)}) collective-permute-start(bf16[512,256]{1,0:T(8,128)(2,1)S(1)} %bitcast.63), channel_id=1, source_target_pairs={{0,8},{4,12},{8,0},{12,4},{1,9},{5,13},{9,1},{13,5},{2,10},{6,14},... | collective-permute-start | bytes 786440 | tf_op jit(solution)/shard_map/ppermute | solution.py:205
  83.5 5.6 %collective-permute-start.13 = (bf16[512,256]{1,0:T(8,128)(2,1)S(1)}, bf16[512,256]{1,0:T(8,128)(2,1)S(1)}, u32[]{:S(2)}, u32[]{:S(2)}) collective-permute-start(bf16[512,256]{1,0:T(8,128)(2,1)S(1)} %fusion.2), channel_id=1, source_target_pairs={{0,224},{32,0},{64,32},{96,64},{128,96},{160,128},{192,160},{224,1... | collective-permute-start | bytes 786440 | tf_op jit(solution)/shard_map/ppermute | solution.py:253
  89.2 4.6 %collective-permute-done.8 = bf16[512,256]{1,0:T(8,128)(2,1)S(1)} collective-permute-done((bf16[512,256]{1,0:T(8,128)(2,1)S(1)}, bf16[512,256]{1,0:T(8,128)(2,1)S(1)}, u32[]{:S(2)}, u32[]{:S(2)}) %collective-permute-start.8) | collective-permute-done | bytes 262176 | tf_op jit(solution)/shard_map/ppermute | solution.py:205
  93.8 1.0 collective-permute-done.7
  94.8 0.9 fusion.6
  95.7 17.1 %all-to-all-start.1 = ((bf16[8,64,256]{2,1,0:T(8,128)(2,1)}), bf16[8,64,256]{2,1,0:T(8,128)(2,1)S(1)}, u32[]{:S(2)}, u32[]{:S(2)}) async-start(bf16[8,64,256]{2,1,0:T(8,128)(2,1)} %bitcast.32), calls=%async_computation.1 | async-start | bytes 524288 | tf_op jit(solution)/shard_map/all_to_all | solution.py:262
  112.8 1.1 copy.20
  113.9 1.1 copy.21
  115.0 4.2 %all-to-all-done.1 = bf16[8,64,256]{2,1,0:T(8,128)(2,1)S(1)} async-done(((bf16[8,64,256]{2,1,0:T(8,128)(2,1)}), bf16[8,64,256]{2,1,0:T(8,128)(2,1)S(1)}, u32[]{:S(2)}, u32[]{:S(2)}) %all-to-all-start.1) | async-done | bytes 262176 | tf_op jit(solution)/shard_map/all_to_all | solution.py:262
  119.3 0.7 copy.23
  120.0 0.7 copy.22
  (28 shorter events, 2.2 us)
Async XLA Ops:
  0.6 0.9 copy-start.2
  1.5 17.5 %copy-start = (bf16[256,8,128]{2,1,0:T(8,128)(2,1)S(1)}, bf16[256,8,128]{2,1,0:T(8,128)(2,1)}, u32[]{:S(2)}) copy-start(bf16[256,8,128]{2,1,0:T(8,128)(2,1)} %param.4) | copy-start | bytes 1572868
  1.5 17.5 %copy-start.1 = (bf16[256,8,128]{2,1,0:T(8,128)(2,1)S(1)}, bf16[256,8,128]{2,1,0:T(8,128)(2,1)}, u32[]{:S(2)}) copy-start(bf16[256,8,128]{2,1,0:T(8,128)(2,1)} %param.7) | copy-start | bytes 1572868
  13.8 8.0 %collective-permute-start.6 = (bf16[512,256]{1,0:T(8,128)(2,1)S(1)}, bf16[512,256]{1,0:T(8,128)(2,1)S(1)}, u32[]{:S(2)}, u32[]{:S(2)}) collective-permute-start(bf16[512,256]{1,0:T(8,128)(2,1)S(1)} %bitcast.52), channel_id=1, source_target_pairs={{0,12},{4,0},{8,4},{12,8},{1,13},{5,1},{9,5},{13,9},{2,14},{6,2},{... | collective-permute-start | bytes 786440 | tf_op jit(solution)/shard_map/ppermute | solution.py:197
  16.3 8.3 %collective-permute-start.5 = (bf16[512,256]{1,0:T(8,128)(2,1)S(1)}, bf16[512,256]{1,0:T(8,128)(2,1)}, u32[]{:S(2)}, u32[]{:S(2)}) collective-permute-start(bf16[512,256]{1,0:T(8,128)(2,1)S(1)} %bitcast.53), channel_id=1, source_target_pairs={{0,8},{4,12},{8,0},{12,4},{1,9},{5,13},{9,1},{13,5},{2,10},{6,14},... | collective-permute-start | bytes 786440 | tf_op jit(solution)/shard_map/ppermute | solution.py:197
  16.8 14.9 %collective-permute-start.4 = (bf16[512,256]{1,0:T(8,128)(2,1)S(1)}, bf16[512,256]{1,0:T(8,128)(2,1)}, u32[]{:S(2)}, u32[]{:S(2)}) collective-permute-start(bf16[512,256]{1,0:T(8,128)(2,1)S(1)} %bitcast.54), channel_id=1, source_target_pairs={{0,4},{4,8},{8,12},{12,0},{1,5},{5,9},{9,13},{13,1},{2,6},{6,10},{... | collective-permute-start | bytes 786440 | tf_op jit(solution)/shard_map/ppermute | solution.py:197
  17.4 15.5 %collective-permute-start = (bf16[512,256]{1,0:T(8,128)(2,1)S(1)}, bf16[512,256]{1,0:T(8,128)(2,1)S(1)}, u32[]{:S(2)}, u32[]{:S(2)}) collective-permute-start(bf16[512,256]{1,0:T(8,128)(2,1)S(1)} %bitcast.55), channel_id=1, source_target_pairs={{0,32},{32,64},{64,96},{96,128},{128,160},{160,192},{192,224},{224... | collective-permute-start | bytes 786440 | tf_op jit(solution)/shard_map/ppermute | solution.py:220
  32.9 7.4 %collective-permute-start.3 = (bf16[512,256]{1,0:T(8,128)(2,1)S(1)}, bf16[512,256]{1,0:T(8,128)(2,1)S(1)}, u32[]{:S(2)}, u32[]{:S(2)}) collective-permute-start(bf16[512,256]{1,0:T(8,128)(2,1)S(1)} %collective-permute-done), channel_id=1, source_target_pairs={{0,12},{4,0},{8,4},{12,8},{1,13},{5,1},{9,5},{13,9},{2,14},{6,2},{... | collective-permute-start | bytes 786440 | tf_op jit(solution)/shard_map/ppermute | solution.py:197
  33.0 8.5 %collective-permute-start.2 = (bf16[512,256]{1,0:T(8,128)(2,1)S(1)}, bf16[512,256]{1,0:T(8,128)(2,1)S(1)}, u32[]{:S(2)}, u32[]{:S(2)}) collective-permute-start(bf16[512,256]{1,0:T(8,128)(2,1)S(1)} %collective-permute-done), channel_id=1, source_target_pairs={{0,8},{4,12},{8,0},{12,4},{1,9},{5,13},{9,1},{13,5},{2,10},{6,14},... | collective-permute-start | bytes 786440 | tf_op jit(solution)/shard_map/ppermute | solution.py:197
  33.6 14.8 %collective-permute-start.1 = (bf16[512,256]{1,0:T(8,128)(2,1)S(1)}, bf16[512,256]{1,0:T(8,128)(2,1)S(1)}, u32[]{:S(2)}, u32[]{:S(2)}) collective-permute-start(bf16[512,256]{1,0:T(8,128)(2,1)S(1)} %collective-permute-done), channel_id=1, source_target_pairs={{0,4},{4,8},{8,12},{12,0},{1,5},{5,9},{9,13},{13,1},{2,6},{6,10},{... | collective-permute-start | bytes 786440 | tf_op jit(solution)/shard_map/ppermute | solution.py:197
  68.7 14.3 %collective-permute-start.12 = (bf16[512,256]{1,0:T(8,128)(2,1)S(1)}, bf16[512,256]{1,0:T(8,128)(2,1)S(1)}, u32[]{:S(2)}, u32[]{:S(2)}) collective-permute-start(bf16[512,256]{1,0:T(8,128)(2,1)S(1)} %bitcast.62), channel_id=1, source_target_pairs={{0,4},{4,8},{8,12},{12,0},{1,5},{5,9},{9,13},{13,1},{2,6},{6,10},{... | collective-permute-start | bytes 786440 | tf_op jit(solution)/shard_map/ppermute | solution.py:205
  68.8 14.3 %collective-permute-start.11 = (bf16[512,256]{1,0:T(8,128)(2,1)S(1)}, bf16[512,256]{1,0:T(8,128)(2,1)S(1)}, u32[]{:S(2)}, u32[]{:S(2)}) collective-permute-start(bf16[512,256]{1,0:T(8,128)(2,1)S(1)} %bitcast.60), channel_id=1, source_target_pairs={{0,8},{4,12},{8,0},{12,4},{1,9},{5,13},{9,1},{13,5},{2,10},{6,14},... | collective-permute-start | bytes 786440 | tf_op jit(solution)/shard_map/ppermute | solution.py:205
  69.9 13.5 %collective-permute-start.10 = (bf16[512,256]{1,0:T(8,128)(2,1)S(1)}, bf16[512,256]{1,0:T(8,128)(2,1)S(1)}, u32[]{:S(2)}, u32[]{:S(2)}) collective-permute-start(bf16[512,256]{1,0:T(8,128)(2,1)S(1)} %bitcast.59), channel_id=1, source_target_pairs={{0,12},{4,0},{8,4},{12,8},{1,13},{5,1},{9,5},{13,9},{2,14},{6,2},{... | collective-permute-start | bytes 786440 | tf_op jit(solution)/shard_map/ppermute | solution.py:205
  74.4 14.7 %collective-permute-start.9 = (bf16[512,256]{1,0:T(8,128)(2,1)S(1)}, bf16[512,256]{1,0:T(8,128)(2,1)S(1)}, u32[]{:S(2)}, u32[]{:S(2)}) collective-permute-start(bf16[512,256]{1,0:T(8,128)(2,1)S(1)} %bitcast.64), channel_id=1, source_target_pairs={{0,4},{4,8},{8,12},{12,0},{1,5},{5,9},{9,13},{13,1},{2,6},{6,10},{... | collective-permute-start | bytes 786440 | tf_op jit(solution)/shard_map/ppermute | solution.py:205
  77.2 16.6 %collective-permute-start.8 = (bf16[512,256]{1,0:T(8,128)(2,1)S(1)}, bf16[512,256]{1,0:T(8,128)(2,1)S(1)}, u32[]{:S(2)}, u32[]{:S(2)}) collective-permute-start(bf16[512,256]{1,0:T(8,128)(2,1)S(1)} %bitcast.63), channel_id=1, source_target_pairs={{0,8},{4,12},{8,0},{12,4},{1,9},{5,13},{9,1},{13,5},{2,10},{6,14},... | collective-permute-start | bytes 786440 | tf_op jit(solution)/shard_map/ppermute | solution.py:205
  83.0 11.8 %collective-permute-start.7 = (bf16[512,256]{1,0:T(8,128)(2,1)S(1)}, bf16[512,256]{1,0:T(8,128)(2,1)S(1)}, u32[]{:S(2)}, u32[]{:S(2)}) collective-permute-start(bf16[512,256]{1,0:T(8,128)(2,1)S(1)} %bitcast.61), channel_id=1, source_target_pairs={{0,12},{4,0},{8,4},{12,8},{1,13},{5,1},{9,5},{13,9},{2,14},{6,2},{... | collective-permute-start | bytes 786440 | tf_op jit(solution)/shard_map/ppermute | solution.py:205
  83.5 11.3 %collective-permute-start.13 = (bf16[512,256]{1,0:T(8,128)(2,1)S(1)}, bf16[512,256]{1,0:T(8,128)(2,1)S(1)}, u32[]{:S(2)}, u32[]{:S(2)}) collective-permute-start(bf16[512,256]{1,0:T(8,128)(2,1)S(1)} %fusion.2), channel_id=1, source_target_pairs={{0,224},{32,0},{64,32},{96,64},{128,96},{160,128},{192,160},{224,1... | collective-permute-start | bytes 786440 | tf_op jit(solution)/shard_map/ppermute | solution.py:253
  95.7 23.5 %all-to-all-start.1 = ((bf16[8,64,256]{2,1,0:T(8,128)(2,1)}), bf16[8,64,256]{2,1,0:T(8,128)(2,1)S(1)}, u32[]{:S(2)}, u32[]{:S(2)}) async-start(bf16[8,64,256]{2,1,0:T(8,128)(2,1)} %bitcast.32), calls=%async_computation.1 | async-start | bytes 524288 | tf_op jit(solution)/shard_map/all_to_all | solution.py:262

commit v2 on v1

v2 whole, which is shorter than its diff:
```python
import math

import jax
import jax.numpy as jnp
from jax import lax
from jax.experimental import pallas as pl
from jax.experimental.pallas import tpu as pltpu
from jax.sharding import Mesh, PartitionSpec as P

BLOCK = 256
DIM = 128
HEADS = 8
HALF = 4
NX = 4
RANKS = 8
LIMIT = 63 << 20
SCALE = 1.0 / math.sqrt(DIM)
TO_LOG2 = SCALE * math.log2(math.e)
F32 = jnp.float32
BF16 = jnp.bfloat16
PLANE = ("ylo", "x", "yhi", "core")


def dot(a, b):
    return jnp.dot(a, b, preferred_element_type=F32)


def causal():
    t = lax.broadcasted_iota(jnp.int32, (BLOCK, BLOCK), 0)
    i = lax.broadcasted_iota(jnp.int32, (BLOCK, BLOCK), 1)
    return t <= i


def forward_tile(kv, heads, q_t, acc, top, total, scores, first, diagonal):
    key = kv[:, :DIM]
    value_t = kv[:, DIM:].T
    for h in range(heads):
        scores[h] = dot(key, q_t[h])
    for h in range(heads):
        s = scores[h]
        if diagonal:
            s = jnp.where(causal(), s, -jnp.inf)
        new_top = jnp.max(s, axis=0, keepdims=True)
        if first:
            w = jnp.exp2((s - new_top) * TO_LOG2)
            total[h : h + 1, :] = jnp.sum(w, axis=0, keepdims=True)
            acc[h] = dot(value_t, w.astype(BF16))
        else:
            old_top = top[h : h + 1, :]
            new_top = jnp.maximum(old_top, new_top)
            w = jnp.exp2((s - new_top) * TO_LOG2)
            fade = jnp.exp2((old_top - new_top) * TO_LOG2)
            total[h : h + 1, :] = total[h : h + 1, :] * fade + jnp.sum(w, axis=0, keepdims=True)
            acc[h] = acc[h] * fade + dot(value_t, w.astype(BF16))
        top[h : h + 1, :] = new_top


def backward_tile(kv, heads, q_t, q, g_t, g, log_total, delta, dq_t, scores, grads, probs, ds, diagonal):
    key = kv[:, :DIM]
    value = kv[:, DIM:]
    key_t = key.T
    for h in range(heads):
        scores[h] = dot(key, q_t[h])
        grads[h] = dot(value, g_t[h])
    for h in range(heads):
        prob = jnp.exp2(scores[h] * TO_LOG2 - log_total[h : h + 1, :])
        if diagonal:
            prob = jnp.where(causal(), prob, 0.0)
        probs[h] = prob.astype(BF16)
        ds[h] = (prob * (grads[h] - delta[h : h + 1, :])).astype(BF16)
    dv = dot(probs[0], g[0])
    dk = dot(ds[0], q[0])
    for h in range(1, heads):
        dv = dv + dot(probs[h], g[h])
        dk = dk + dot(ds[h], q[h])
    for h in range(heads):
        dq_t[h] += dot(key_t, ds[h])
    return jnp.concatenate([dk * SCALE, dv], axis=1)


def far_forward(place, kv_far, q_t_far, part_far, log_part, kv, q_t, acc, part, top, total, scores, sems):
    loads = [pltpu.make_async_copy(q_t_far, q_t, sems.at[0]), pltpu.make_async_copy(kv_far, kv, sems.at[1])]
    for load in loads:
        load.start()
    for load in loads:
        load.wait()
    forward_tile(kv[0], HALF, q_t, acc, top, total, scores, True, False)

    def forward(b, carry):
        forward_tile(kv[b], HALF, q_t, acc, top, total, scores, False, False)
        return carry

    lax.fori_loop(1, kv.shape[0], forward, 0)
    for h in range(HALF):
        part[h] = (acc[h] / total[h : h + 1, :]).astype(BF16)
    log_part[...] = top[...] * TO_LOG2 + jnp.log2(total[...])
    store = pltpu.make_async_copy(part, part_far, sems.at[2])
    store.start()
    store.wait()


def finish(o, g_t):
    rounded = o.astype(BF16)
    return rounded, jnp.sum(rounded.astype(F32) * g_t.astype(F32), axis=0, keepdims=True)


def own_forward(
    place, kv_far, q_t_far, g_t_far,
    out_far, own_wide_far, log_narrow, delta_narrow, log_wide,
    kv, q_t, g_t, acc, out, own_wide, top, total, scores, sems,
):
    rank = place[0]
    wide = place[1]
    narrow = HALF - wide
    loads = [
        pltpu.make_async_copy(q_t_far, q_t, sems.at[0]),
        pltpu.make_async_copy(kv_far, kv, sems.at[1]),
        pltpu.make_async_copy(g_t_far.at[pl.ds(narrow, HALF)], g_t, sems.at[2]),
    ]
    for load in loads:
        load.start()
    for load in loads[:2]:
        load.wait()
    forward_tile(kv[rank], HEADS, q_t, acc, top, total, scores, True, True)

    def forward(b, carry):
        forward_tile(kv[b], HEADS, q_t, acc, top, total, scores, False, False)
        return carry

    lax.fori_loop(0, rank, forward, 0)
    for h in range(HALF):
        own_wide[h] = acc[wide + h] / total[pl.ds(wide + h, 1), :]
        log_wide[h : h + 1, :] = top[pl.ds(wide + h, 1), :] * TO_LOG2 + jnp.log2(total[pl.ds(wide + h, 1), :])
    store_wide = pltpu.make_async_copy(own_wide, own_wide_far, sems.at[3])
    store_wide.start()
    loads[2].wait()
    for h in range(HALF):
        sum_h = total[pl.ds(narrow + h, 1), :]
        out[h], delta_narrow[h : h + 1, :] = finish(acc[narrow + h] / sum_h, g_t[h])
        log_narrow[h : h + 1, :] = top[pl.ds(narrow + h, 1), :] * TO_LOG2 + jnp.log2(sum_h)
    store_out = pltpu.make_async_copy(out, out_far.at[pl.ds(narrow, HALF)], sems.at[4])
    store_out.start()
    store_wide.wait()
    store_out.wait()


def merge(
    place, own_wide_far, part_far, g_t_far, log_narrow, delta_narrow, log_wide, log_part, out_in,
    out_far, log_total, delta, stats,
    own_wide, part, g_t, out, sems,
):
    wide = place[1]
    narrow = HALF - wide
    wides = pl.ds(wide, HALF)
    loads = [
        pltpu.make_async_copy(own_wide_far, own_wide, sems.at[0]),
        pltpu.make_async_copy(part_far, part, sems.at[1]),
        pltpu.make_async_copy(g_t_far.at[wides], g_t, sems.at[2]),
    ]
    for load in loads:
        load.start()
    for load in loads:
        load.wait()
    for h in range(HALF):
        a = log_wide[h : h + 1, :]
        b = log_part[h : h + 1, :]
        top = jnp.maximum(a, b)
        log_h = top + jnp.log2(jnp.exp2(a - top) + jnp.exp2(b - top))
        out[h], delta_h = finish(
            own_wide[h] * jnp.exp2(a - log_h) + part[h].astype(F32) * jnp.exp2(b - log_h), g_t[h]
        )
        stats[h : h + 1, :] = log_h
        stats[HALF + h : HALF + h + 1, :] = delta_h
        log_total[pl.ds(wide + h, 1), :] = log_h
        delta[pl.ds(wide + h, 1), :] = delta_h
        log_total[pl.ds(narrow + h, 1), :] = log_narrow[h : h + 1, :]
        delta[pl.ds(narrow + h, 1), :] = delta_narrow[h : h + 1, :]
    store = pltpu.make_async_copy(out, out_far.at[wides], sems.at[3])
    store.start()
    store.wait()


def own_backward(
    place, kv_far, q_t_far, q_far, g_t_far, g_far, log_total, delta,
    dq_far, dkv_far,
    kv, q_t, q, g_t, g, dq_t, dkv, scores, grads, probs, ds, sems, tile_sems,
):
    rank = place[0]
    loads = [
        pltpu.make_async_copy(far, near, sems.at[i])
        for i, (far, near) in enumerate([(q_t_far, q_t), (kv_far, kv), (g_t_far, g_t), (g_far, g), (q_far, q)])
    ]
    for load in loads:
        load.start()

    def store(b):
        return pltpu.make_async_copy(dkv.at[b], dkv_far.at[b], tile_sems.at[b])

    def blank(b, carry):
        dkv[b] = jnp.zeros((BLOCK, 2 * DIM), F32)
        store(b).start()
        return carry

    lax.fori_loop(rank + 1, RANKS, blank, 0)
    dq_t[...] = jnp.zeros_like(dq_t)
    for load in loads:
        load.wait()

    def tile(b, diagonal):
        dkv[b] = backward_tile(
            kv[b], HEADS, q_t, q, g_t, g, log_total, delta, dq_t, scores, grads, probs, ds, diagonal
        )
        store(b).start()

    tile(rank, True)

    def backward(b, carry):
        tile(b, False)
        return carry

    lax.fori_loop(0, rank, backward, 0)
    dq_store = pltpu.make_async_copy(dq_t, dq_far, sems.at[5])
    dq_store.start()
    for b in range(RANKS):
        store(b).wait()
    dq_store.wait()


def far_backward(
    place, kv_far, q_t_far, q_far, g_t_far, g_far, stats, dkv_own_far,
    dq_far, dkv_far,
    kv, q_t, q, g_t, g, dkv_own, dq_t, dq, dkv, log_total, delta, scores, grads, probs, ds, sems, tile_sems,
):
    tiles = kv.shape[0]
    loads = [
        pltpu.make_async_copy(far, near, sems.at[i])
        for i, (far, near) in enumerate(
            [(q_t_far, q_t), (kv_far, kv), (g_t_far, g_t), (g_far, g), (q_far, q), (dkv_own_far, dkv_own)]
        )
    ]
    for load in loads:
        load.start()
    log_total[...] = stats[:HALF, :]
    delta[...] = stats[HALF:, :]
    dq_t[...] = jnp.zeros_like(dq_t)
    for load in loads:
        load.wait()

    def store(b):
        return pltpu.make_async_copy(dkv.at[b], dkv_far.at[b], tile_sems.at[b])

    def backward(b, carry):
        dkv[b] = (
            backward_tile(kv[b], HALF, q_t, q, g_t, g, log_total, delta, dq_t, scores, grads, probs, ds, False)
            + dkv_own[b]
        ).astype(BF16)
        store(b).start()
        return carry

    lax.fori_loop(0, tiles, backward, 0)
    dq[...] = (dq_t[...] * SCALE).astype(BF16)
    dq_store = pltpu.make_async_copy(dq, dq_far, sems.at[6])
    dq_store.start()
    for b in range(tiles):
        store(b).wait()
    dq_store.wait()


FAR = pl.BlockSpec(memory_space=pltpu.HBM)
NEAR = pl.BlockSpec(memory_space=pltpu.VMEM)


def call(body, outs, ins, scratch, sems, flops, aliases=None):
    return pl.pallas_call(
        body,
        out_shape=[jax.ShapeDtypeStruct(s, t) for s, t, _ in outs],
        in_specs=[pl.BlockSpec(memory_space=pltpu.SMEM)] + [spec for _, spec in ins[1:]],
        out_specs=[spec for _, _, spec in outs],
        scratch_shapes=[pltpu.VMEM(s, t) for s, t in scratch] + [pltpu.SemaphoreType.DMA((n,)) for n in sems],
        input_output_aliases=aliases or {},
        compiler_params=pltpu.CompilerParams(vmem_limit_bytes=LIMIT),
        cost_estimate=pl.CostEstimate(flops=flops, bytes_accessed=4 << 20, transcendentals=1 << 20),
    )(*[a for a, _ in ins])


def ring(size, by):
    return [(i, (i + by) % size) for i in range(size)]


def spread(block):
    many = jnp.broadcast_to(block[None], (RANKS,) + block.shape).reshape((4 * RANKS,) + block.shape[1:])
    got = lax.all_to_all(many, PLANE, 0, 0, tiled=True)
    return got.reshape(RANKS, BLOCK, 2 * DIM)


def collect(grads):
    got = lax.all_to_all(grads.reshape(4 * RANKS, 64, 2 * DIM), PLANE, 0, 0, tiled=True)
    return jnp.sum(got.reshape(RANKS, 4, 64, 2 * DIM).astype(F32), axis=0)


def per_device(queries, key_vectors, value_vectors, out_grad):
    rank = lax.axis_index("ylo") * NX + lax.axis_index("x")
    wide = jnp.where(lax.axis_index("z") % 2 == 0, HALF, 0)
    place = jnp.stack([rank, wide]).astype(jnp.int32)

    block = jnp.transpose(jnp.concatenate([key_vectors, value_vectors], axis=2), (1, 0, 2))
    planes = lax.axis_size("z")
    planes = lax.axis_size("z")
    own = spread(block)

    def widest(a, heads):
        return jnp.where(wide == HALF, a[:, heads + HALF : heads + 2 * HALF], a[:, heads : heads + HALF])

    sent = jnp.concatenate([widest(queries, 0), widest(out_grad, 0)], axis=1)
    far = lax.ppermute(sent, "z", ring(planes, -1))
    q = jnp.transpose(queries, (1, 0, 2))
    q_t = jnp.transpose(queries, (1, 2, 0))
    g = jnp.transpose(out_grad, (1, 0, 2))
    g_t = jnp.transpose(out_grad, (1, 2, 0))
    q_far = jnp.transpose(far[:, :HALF], (1, 0, 2))
    q_t_far = jnp.transpose(far[:, :HALF], (1, 2, 0))
    g_far = jnp.transpose(far[:, HALF:], (1, 0, 2))
    g_t_far = jnp.transpose(far[:, HALF:], (1, 2, 0))

    full_t = (HEADS, DIM, BLOCK)
    full = (HEADS, BLOCK, DIM)
    half_t = (HALF, DIM, BLOCK)
    half = (HALF, BLOCK, DIM)
    rows = (HEADS, BLOCK)
    few = (HALF, BLOCK)
    square = (HEADS, BLOCK, BLOCK)
    kv_shape = (RANKS, BLOCK, 2 * DIM)
    tile = 2 * BLOCK
    tiled = (RANKS * BLOCK // tile, tile, 2 * DIM)
    tall = (HALF, tile, BLOCK)
    part, log_part = call(
        far_forward,
        [(half_t, BF16, FAR), (few, F32, NEAR)],
        [(place, None), (own.reshape(tiled), FAR), (q_t_far, FAR)],
        [(tiled, BF16), (half_t, BF16), (half_t, F32), (half_t, BF16), (few, F32), (few, F32), (tall, F32)],
        [3],
        4 << 30,
    )
    part = lax.ppermute(part, "z", ring(planes, 1))
    log_part = lax.ppermute(log_part, "z", ring(planes, 1))
    out_t, own_wide, log_narrow, delta_narrow, log_wide = call(
        own_forward,
        [(full_t, BF16, FAR), (half_t, F32, FAR), (few, F32, NEAR), (few, F32, NEAR), (few, F32, NEAR)],
        [(place, None), (own, FAR), (q_t, FAR), (g_t, FAR)],
        [
            (kv_shape, BF16), (full_t, BF16), (half_t, BF16), (full_t, F32), (half_t, BF16), (half_t, F32),
            (rows, F32), (rows, F32), (square, F32),
        ],
        [5],
        8 << 30,
    )
    out_t, log_total, delta, stats = call(
        merge,
        [(full_t, BF16, FAR), (rows, F32, NEAR), (rows, F32, NEAR), (rows, F32, NEAR)],
        [
            (place, None), (own_wide, FAR), (part, FAR), (g_t, FAR), (log_narrow, NEAR), (delta_narrow, NEAR),
            (log_wide, NEAR), (log_part, NEAR), (out_t, FAR),
        ],
        [(half_t, F32), (half_t, BF16), (half_t, BF16), (half_t, BF16)],
        [4],
        1 << 20,
        {8: 0},
    )
    stats_far = lax.ppermute(stats, "z", ring(planes, -1))
    dq_t, dkv = call(
        own_backward,
        [(full_t, F32, FAR), (kv_shape, F32, FAR)],
        [
            (place, None), (own, FAR), (q_t, FAR), (q, FAR), (g_t, FAR), (g, FAR),
            (log_total, NEAR), (delta, NEAR),
        ],
        [
            (kv_shape, BF16), (full_t, BF16), (full, BF16), (full_t, BF16), (full, BF16),
            (full_t, F32), (kv_shape, F32), (square, F32), (square, F32), (square, BF16), (square, BF16),
        ],
        [6, RANKS],
        16 << 30,
    )
    dq_far, dkv = call(
        far_backward,
        [(half_t, BF16, FAR), (tiled, BF16, FAR)],
        [
            (place, None), (own.reshape(tiled), FAR), (q_t_far, FAR), (q_far, FAR), (g_t_far, FAR), (g_far, FAR),
            (stats_far, NEAR), (dkv.reshape(tiled), FAR),
        ],
        [
            (tiled, BF16), (half_t, BF16), (half, BF16), (half_t, BF16), (half, BF16), (tiled, F32),
            (half_t, F32), (half_t, BF16), (tiled, BF16), (few, F32), (few, F32),
            (tall, F32), (tall, F32), (tall, BF16), (tall, BF16),
        ],
        [7, RANKS * BLOCK // tile],
        8 << 30,
    )
    dq_back = lax.ppermute(dq_far, "z", ring(planes, 1)).astype(F32)
    back = jnp.transpose(collect(dkv).astype(BF16), (1, 0, 2))
    attended = jnp.transpose(out_t, (2, 0, 1))
    high = wide == HALF
    low_part = dq_t[:HALF] * SCALE + jnp.where(high, 0.0, dq_back)
    high_part = dq_t[HALF:] * SCALE + jnp.where(high, dq_back, 0.0)
    query_grad = jnp.transpose(jnp.concatenate([low_part, high_part], axis=0).astype(BF16), (2, 0, 1))
    return attended, query_grad, back[:, :, :DIM], back[:, :, DIM:]


def solution(mesh):
    inner = Mesh(mesh.devices.reshape(8, 2, NX, 2, 2), ("z", "ylo", "x", "yhi", "core"))
    tokens = ("z", "ylo", "x")
    heads = ("yhi", "core")
    by_head = P(tokens, heads, None)
    by_token = P(tokens + heads, None, None)
    return jax.shard_map(
        per_device,
        mesh=inner,
        in_specs=(by_head, by_token, by_token, by_head),
        out_specs=(by_head, by_head, by_token, by_token),
        check_vma=False,
    )
```

time: 121 us -> 109 us (0.901)
  blocking collectives: 12.2 us -> 0 us
  waiting for transfers between devices: 33.1 us -> 27.1 us
  local copies, waits for them, and re-layouts: 5.43 us -> 11.1 us
  Pallas kernels: 25.7 us -> 30 us
  starting transfers between devices: 40.8 us -> 37 us
    ppermute x14 -> x5, starting transfers between devices: 23.7 us -> 7.82 us  [the longest x1 5.65 us: per_device(): far = lax.ppermute(sent, 'z', ring(planes, -1))]
    all_to_all x1 -> x0, blocking collectives: 12.2 us -> none  [per_device(): home = lax.all_to_all(both, COLUMN, 1, 0, tiled=True)[:, 0, :]]
    all_to_all x1 -> x2, starting transfers between devices: 17.1 us -> 29.2 us  [the longest x1 20.5 us: collect(): lax.all_to_all(grads.reshape(4 * RANKS, 64, 2 * DIM), PLANE, 0, 0, tiled=...]
    ppermute x14 -> x5, waiting for transfers between devices: 28.9 us -> 20.2 us  [the longest x1 8.12 us: per_device(): far = lax.ppermute(sent, 'z', ring(planes, -1))]
    pallas_call x3 -> x5, Pallas kernels: 25.7 us -> 30 us  [call(): pl.pallas_call(body, out_shape=[jax.ShapeDtypeStruct(s, t) for s, t, _ in...]
    all_to_all x1 -> x2, waiting for transfers between devices: 4.17 us -> 6.91 us  [the longest x1 6.91 us: collect(): lax.all_to_all(grads.reshape(4 * RANKS, 64, 2 * DIM), PLANE, 0, 0, tiled=...]
    transpose x1 -> x4, local copies, waits for them, and re-layouts: 0.19 us -> 2.74 us  [the longest x1 1.01 us: per_device(): g_far = jnp.transpose(far[:, HALF:], (1, 0, 2))]
    unnamed x14 -> x28, local copies, waits for them, and re-layouts: 5.08 us -> 7.22 us
  transfers between devices with their start and end apart: 15 -> 7, of which waited for: 11 -> 4; matrix products, arithmetic and copies ran while one was open for 4% -> 8% of each run, Pallas kernels for 5% -> 9%
where the time goes in v2:
time: 109 us; the launch traced here: 108 us
  starting transfers between devices  37 us (34%)
  Pallas kernels  30 us (28%)
  waiting for transfers between devices  27.1 us (25%)
  local copies, waits for them, and re-layouts  11.1 us (10%)
  other arithmetic  2.03 us (2%)
    pallas_call x5, Pallas kernels, call(): pl.pallas_call(body, out_shape=[jax.ShapeDtypeStruct(s, t) for s, t, _ in...  30 us
    all_to_all x1, starting transfers between devices, collect(): lax.all_to_all(grads.reshape(4 * RANKS, 64, 2 * DIM), PLANE, 0, 0, tiled=...  20.5 us
    all_to_all x1, starting transfers between devices, spread(): got = lax.all_to_all(many, PLANE, 0, 0, tiled=True)  8.63 us
    ppermute x1, waiting for transfers between devices, per_device(): far = lax.ppermute(sent, 'z', ring(planes, -1))  8.12 us
    ppermute x1, waiting for transfers between devices, per_device(): dq_back = lax.ppermute(dq_far, 'z', ring(planes, 1)).astype(F32)  7.74 us
    unnamed x28, local copies, waits for them, and re-layouts  7.22 us
    all_to_all x1, waiting for transfers between devices, collect(): lax.all_to_all(grads.reshape(4 * RANKS, 64, 2 * DIM), PLANE, 0, 0, tiled=...  6.91 us
    ppermute x1, starting transfers between devices, per_device(): far = lax.ppermute(sent, 'z', ring(planes, -1))  5.65 us
  transfers between devices with their start and end apart: 7, of which 4 were waited for; matrix products, arithmetic and copies ran while one was open for 8% of the time, Pallas kernels for 9%

profile of v2, /device:TPU:1, one launch (start us, length us, event | category | flops | bytes accessed | tf_op | source)
XLA Modules:
  0.0 108.1 jit_solution(1724748495832688531)
XLA Ops:
  0.6 1.0 maximum_bitcast_fusion.1
  1.7 1.1 %broadcast_in_dim.12 = bf16[8,4,64,256]{3,2,1,0:T(8,128)(2,1)} broadcast(bf16[4,64,256]{2,1,0:T(8,128)(2,1)S(1)} %copy.23), dimensions={1,2,3} | broadcast | bytes 1179648 | tf_op jit(solution)/shard_map/broadcast_in_dim | solution.py:291
  2.8 8.6 %all-to-all-start = ((bf16[32,64,256]{2,1,0:T(8,128)(2,1)}), bf16[32,64,256]{2,1,0:T(8,128)(2,1)}, u32[]{:S(2)}, u32[]{:S(2)}) async-start(bf16[32,64,256]{2,1,0:T(8,128)(2,1)} %bitcast.3), calls=%async_computation | async-start | bytes 2097152 | tf_op jit(solution)/shard_map/all_to_all | solution.py:292
  11.8 5.7 %collective-permute-start = (bf16[256,8,128]{2,0,1:T(8,128)(2,1)S(1)}, bf16[256,8,128]{2,0,1:T(8,128)(2,1)S(1)}, u32[]{:S(2)}, u32[]{:S(2)}) collective-permute-start(bf16[256,8,128]{2,0,1:T(8,128)(2,1)S(1)} %pad_maximum_fusion), channel_id=1, source_target_pairs={{0,224},{32,0},{64,32},{96,64},{128,96},{160,128},{192,160},{224,1... | collective-permute-start | bytes 1572872 | tf_op jit(solution)/shard_map/ppermute | solution.py:315
  17.4 1.1 %copy.24 = bf16[256,8,128]{0,2,1:T(8,128)(2,1)} copy(bf16[256,8,128]{2,1,0:T(8,128)(2,1)S(1)} %copy-done) | data formatting | bytes 1048576 | tf_op args[0]
  18.5 1.1 %copy.25 = bf16[256,8,128]{0,2,1:T(8,128)(2,1)} copy(bf16[256,8,128]{2,1,0:T(8,128)(2,1)S(1)} %copy-done.1) | data formatting | bytes 1048576 | tf_op args[3]
  19.7 0.6 pad_add_fusion.place
  20.3 8.1 %collective-permute-done = bf16[256,8,128]{2,0,1:T(8,128)(2,1)S(1)} collective-permute-done((bf16[256,8,128]{2,0,1:T(8,128)(2,1)S(1)}, bf16[256,8,128]{2,0,1:T(8,128)(2,1)S(1)}, u32[]{:S(2)}, u32[]{:S(2)}) %collective-permute-start) | collective-permute-done | bytes 524320 | tf_op jit(solution)/shard_map/ppermute | solution.py:315
  28.4 1.0 slice_bitcast_fusion
  29.4 0.9 copy.30.q_t_far
  30.3 0.9 copy.34.g_t_far
  31.1 6.8 %shard_map.76 = (bf16[4,128,256]{2,1,0:T(8,128)(2,1)}, f32[4,256]{1,0:T(4,128)}) custom-call(s32[2]{0:T(128)} %pad_add_fusion.place, bf16[4,512,256]{2,1,0:T(8,128)(2,1)} %bitcast.7.kv_far, bf16[4,128,256]{2,1,0:T(8,128)(2,1)} %copy.30.q_t_far), custom_call_target="tpu_custom_call" | custom-call | flops 4294967296 | bytes 4194304 | tf_op jit(solution)/shard_map/pallas_call | solution.py:274
  38.0 0.1 collective-permute-start.2
  38.1 0.7 collective-permute-start.1
  38.8 4.4 %shard_map.75 = (bf16[8,128,256]{2,1,0:T(8,128)(2,1)}, f32[4,128,256]{2,1,0:T(8,128)}, f32[4,256]{1,0:T(4,128)}, f32[4,256]{1,0:T(4,128)}, f32[4,256]{1,0:T(4,128)}) custom-call(s32[2]{0:T(128)} %pad_add_fusion.place, bf16[8,256,256]{2,1,0:T(8,128)(2,1)} %bitcast.4.kv_far, bf16[8,128,256]{2,1,0:T(8,128)(2,1)} %bitcast.35, bf16[8,128,256]{2,1,0:T(8,128)(2,1)} %bitcast.37), custom_call_target="tpu_custom_call" | custom-call | flops 8589934592 | bytes 4194304 | tf_op jit(solution)/shard_map/pallas_call | solution.py:274
  43.2 4.3 %collective-permute-done.1.part_far = bf16[4,128,256]{2,1,0:T(8,128)(2,1)S(1)} collective-permute-done((bf16[4,128,256]{2,1,0:T(8,128)(2,1)}, bf16[4,128,256]{2,1,0:T(8,128)(2,1)S(1)}, u32[]{:S(2)}, u32[]{:S(2)}) %collective-permute-start.1) | collective-permute-done | bytes 262176 | tf_op jit(solution)/shard_map/ppermute | solution.py:344
  47.6 0.7 copy-done.7
  48.3 3.5 %shard_map.77 = (bf16[8,128,256]{2,1,0:T(8,128)(2,1)}, f32[8,256]{1,0:T(8,128)}, f32[8,256]{1,0:T(8,128)}, f32[8,256]{1,0:T(8,128)}) custom-call(s32[2]{0:T(128)} %pad_add_fusion.place, f32[4,128,256]{2,1,0:T(8,128)} %get-tuple-element.19.own_wide_far, bf16[4,128,256]{2,1,0:T(8,128)(2,1)} %copy-done.7, ...), custom_call_target="tpu_custom_call", output_to_operand_aliasing={{0}: (8, {})} | custom-call | flops 1048576 | bytes 4194304 | tf_op jit(solution)/shard_map/pallas_call | solution.py:274
  51.8 1.3 %collective-permute-start.3 = (f32[8,256]{1,0:T(8,128)}, f32[8,256]{1,0:T(8,128)S(1)}, u32[]{:S(2)}, u32[]{:S(2)}) collective-permute-start(f32[8,256]{1,0:T(8,128)} %get-tuple-element.30), channel_id=1, source_target_pairs={{0,224},{32,0},{64,32},{96,64},{128,96},{160,128},{192,160},{224,1... | collective-permute-start | bytes 24584 | tf_op jit(solution)/shard_map/ppermute | solution.py:369
  53.0 5.9 %shard_map.78 = (f32[8,128,256]{2,1,0:T(8,128)}, f32[8,256,256]{2,1,0:T(8,128)}) custom-call(s32[2]{0:T(128)} %pad_add_fusion.place, bf16[8,256,256]{2,1,0:T(8,128)(2,1)} %bitcast.4.kv_far, bf16[8,128,256]{2,1,0:T(8,128)(2,1)} %bitcast.36, bf16[8,256,128]{2,1,0:T(8,128)(2,1)} %bitcast.31, bf16[8,128,256]{2,1,0:T(8,128)(2,1)} %bitcast.39, ...), custom_call_target="tpu_custom_call" | custom-call | flops 17179869184 | bytes 4194304 | tf_op jit(solution)/shard_map/pallas_call | solution.py:274
  58.9 0.6 copy-done.8
  59.5 9.3 %shard_map.79 = (bf16[4,128,256]{2,1,0:T(8,128)(2,1)}, bf16[4,512,256]{2,1,0:T(8,128)(2,1)}) custom-call(s32[2]{0:T(128)} %pad_add_fusion.place, bf16[4,512,256]{2,1,0:T(8,128)(2,1)} %bitcast.7.kv_far, bf16[4,128,256]{2,1,0:T(8,128)(2,1)} %copy.30.q_t_far, bf16[4,256,128]{2,1,0:T(8,128)(2,1)} %get-tuple-element.49.q_far, bf16[4,128,256]{2,1,0:T(8,128)(2,1)} %copy.34.g_t_far, ...), custom_call_target="tpu_custom_call" | custom-call | flops 8589934592 | bytes 4194304 | tf_op jit(solution)/shard_map/pallas_call | solution.py:274
  68.9 20.5 %all-to-all-start.1 = ((bf16[32,64,256]{2,1,0:T(8,128)(2,1)}), bf16[32,64,256]{2,1,0:T(8,128)(2,1)S(1)}, u32[]{:S(2)}, u32[]{:S(2)}) async-start(bf16[32,64,256]{2,1,0:T(8,128)(2,1)} %bitcast.33), calls=%async_computation.1 | async-start | bytes 2097152 | tf_op jit(solution)/shard_map/all_to_all | solution.py:297
  89.5 0.1 collective-permute-start.4
  89.6 1.1 copy.35
  90.6 7.7 %collective-permute-done.4 = bf16[4,128,256]{2,1,0:T(8,128)(2,1)S(1)} collective-permute-done((bf16[4,128,256]{2,1,0:T(8,128)(2,1)S(1)}, bf16[4,128,256]{2,1,0:T(8,128)(2,1)S(1)}, u32[]{:S(2)}, u32[]{:S(2)}) %collective-permute-start.4) | collective-permute-done | bytes 262176 | tf_op jit(solution)/shard_map/ppermute | solution.py:399
  98.4 0.1 fusion.1
  98.6 1.1 copy.36
  99.7 6.9 %all-to-all-done.1 = bf16[32,64,256]{2,1,0:T(8,128)(2,1)S(1)} async-done(((bf16[32,64,256]{2,1,0:T(8,128)(2,1)}), bf16[32,64,256]{2,1,0:T(8,128)(2,1)S(1)}, u32[]{:S(2)}, u32[]{:S(2)}) %all-to-all-start.1) | async-done | bytes 1048608 | tf_op jit(solution)/shard_map/all_to_all | solution.py:297
  106.6 0.1 reduce_sum.12
  106.8 0.7 copy.38
  107.4 0.7 copy.37
  (28 shorter events, 0.4 us)
Async XLA Ops:
  0.6 10.8 %copy-start = (bf16[256,8,128]{2,1,0:T(8,128)(2,1)S(1)}, bf16[256,8,128]{2,1,0:T(8,128)(2,1)}, u32[]{:S(2)}) copy-start(bf16[256,8,128]{2,1,0:T(8,128)(2,1)} %param.4) | copy-start | bytes 1572868
  1.7 9.9 %copy-start.1 = (bf16[256,8,128]{2,1,0:T(8,128)(2,1)S(1)}, bf16[256,8,128]{2,1,0:T(8,128)(2,1)}, u32[]{:S(2)}) copy-start(bf16[256,8,128]{2,1,0:T(8,128)(2,1)} %param.7) | copy-start | bytes 1572868
  2.8 28.3 %all-to-all-start = ((bf16[32,64,256]{2,1,0:T(8,128)(2,1)}), bf16[32,64,256]{2,1,0:T(8,128)(2,1)}, u32[]{:S(2)}, u32[]{:S(2)}) async-start(bf16[32,64,256]{2,1,0:T(8,128)(2,1)} %bitcast.3), calls=%async_computation | async-start | bytes 2097152 | tf_op jit(solution)/shard_map/all_to_all | solution.py:292
  11.5 7.0 %copy-start.2 = (bf16[256,8,128]{2,0,1:T(8,128)(2,1)}, bf16[256,8,128]{2,0,1:T(8,128)(2,1)S(1)}, u32[]{:S(2)}) copy-start(bf16[256,8,128]{2,0,1:T(8,128)(2,1)S(1)} %copy.44) | copy-start | bytes 1572868
  11.6 8.0 %copy-start.3 = (bf16[256,8,128]{2,0,1:T(8,128)(2,1)}, bf16[256,8,128]{2,0,1:T(8,128)(2,1)S(1)}, u32[]{:S(2)}) copy-start(bf16[256,8,128]{2,0,1:T(8,128)(2,1)S(1)} %copy.43) | copy-start | bytes 1572868
  11.8 16.6 %collective-permute-start = (bf16[256,8,128]{2,0,1:T(8,128)(2,1)S(1)}, bf16[256,8,128]{2,0,1:T(8,128)(2,1)S(1)}, u32[]{:S(2)}, u32[]{:S(2)}) collective-permute-start(bf16[256,8,128]{2,0,1:T(8,128)(2,1)S(1)} %pad_maximum_fusion), channel_id=1, source_target_pairs={{0,224},{32,0},{64,32},{96,64},{128,96},{160,128},{192,160},{224,1... | collective-permute-start | bytes 1572872 | tf_op jit(solution)/shard_map/ppermute | solution.py:315
  38.0 5.2 %collective-permute-start.2 = (f32[4,256]{1,0:T(4,128)}, f32[4,256]{1,0:T(4,128)S(1)}, u32[]{:S(2)}, u32[]{:S(2)}) collective-permute-start(f32[4,256]{1,0:T(4,128)} %get-tuple-element.24), channel_id=1, source_target_pairs={{0,32},{32,64},{64,96},{96,128},{128,160},{160,192},{192,224},{224... | collective-permute-start | bytes 12296 | tf_op jit(solution)/shard_map/ppermute | solution.py:345
  38.1 9.5 %collective-permute-start.1 = (bf16[4,128,256]{2,1,0:T(8,128)(2,1)}, bf16[4,128,256]{2,1,0:T(8,128)(2,1)S(1)}, u32[]{:S(2)}, u32[]{:S(2)}) collective-permute-start(bf16[4,128,256]{2,1,0:T(8,128)(2,1)} %get-tuple-element.20), channel_id=1, source_target_pairs={{0,32},{32,64},{64,96},{96,128},{128,160},{160,192},{192,224},{224... | collective-permute-start | bytes 786440 | tf_op jit(solution)/shard_map/ppermute | solution.py:344
  43.2 4.4 %copy-start.9 = (f32[4,256]{1,0:T(4,128)}, f32[4,256]{1,0:T(4,128)S(1)}, u32[]{:S(2)}) copy-start(f32[4,256]{1,0:T(4,128)S(1)} %collective-permute-done.2.log_part) | copy-start | bytes 12292
  47.6 0.7 copy-start.7
  51.8 7.1 %collective-permute-start.3 = (f32[8,256]{1,0:T(8,128)}, f32[8,256]{1,0:T(8,128)S(1)}, u32[]{:S(2)}, u32[]{:S(2)}) collective-permute-start(f32[8,256]{1,0:T(8,128)} %get-tuple-element.30), channel_id=1, source_target_pairs={{0,224},{32,0},{64,32},{96,64},{128,96},{160,128},{192,160},{224,1... | collective-permute-start | bytes 24584 | tf_op jit(solution)/shard_map/ppermute | solution.py:369
  58.9 0.6 copy-start.8
  68.9 20.6 %copy-start.6 = (bf16[4,128,256]{2,1,0:T(8,128)(2,1)S(1)}, bf16[4,128,256]{2,1,0:T(8,128)(2,1)}, u32[]{:S(2)}) copy-start(bf16[4,128,256]{2,1,0:T(8,128)(2,1)} %get-tuple-element.32) | copy-start | bytes 786436
  68.9 20.7 %copy-start.5 = (bf16[8,128,256]{2,1,0:T(8,128)(2,1)S(1)}, bf16[8,128,256]{2,1,0:T(8,128)(2,1)}, u32[]{:S(2)}) copy-start(bf16[8,128,256]{2,1,0:T(8,128)(2,1)} %get-tuple-element.26) | copy-start | bytes 1572868
  68.9 29.5 %copy-start.4 = (f32[8,128,256]{2,1,0:T(8,128)S(1)}, f32[8,128,256]{2,1,0:T(8,128)}, u32[]{:S(2)}) copy-start(f32[8,128,256]{2,1,0:T(8,128)} %get-tuple-element.29) | copy-start | bytes 3145732
  68.9 37.7 %all-to-all-start.1 = ((bf16[32,64,256]{2,1,0:T(8,128)(2,1)}), bf16[32,64,256]{2,1,0:T(8,128)(2,1)S(1)}, u32[]{:S(2)}, u32[]{:S(2)}) async-start(bf16[32,64,256]{2,1,0:T(8,128)(2,1)} %bitcast.33), calls=%async_computation.1 | async-start | bytes 2097152 | tf_op jit(solution)/shard_map/all_to_all | solution.py:297
  89.5 8.9 %collective-permute-start.4 = (bf16[4,128,256]{2,1,0:T(8,128)(2,1)S(1)}, bf16[4,128,256]{2,1,0:T(8,128)(2,1)S(1)}, u32[]{:S(2)}, u32[]{:S(2)}) collective-permute-start(bf16[4,128,256]{2,1,0:T(8,128)(2,1)S(1)} %copy-done.6), channel_id=1, source_target_pairs={{0,32},{32,64},{64,96},{96,128},{128,160},{160,192},{192,224},{224... | collective-permute-start | bytes 786440 | tf_op jit(solution)/shard_map/ppermute | solution.py:399

commit v3 on v2

v3 whole, which is shorter than its diff:
```python
import math

import jax
import jax.numpy as jnp
from jax import lax
from jax.experimental import pallas as pl
from jax.experimental.pallas import tpu as pltpu
from jax.sharding import Mesh, PartitionSpec as P

BLOCK = 256
DIM = 128
HEADS = 8
HALF = 4
NX = 4
RANKS = 8
EXTRA = 16
LIMIT = 63 << 20
SCALE = 1.0 / math.sqrt(DIM)
TO_LOG2 = SCALE * math.log2(math.e)
F32 = jnp.float32
BF16 = jnp.bfloat16
PLANE = ("ylo", "x", "yhi", "core")


def dot(a, b):
    return jnp.dot(a, b, preferred_element_type=F32)


def causal():
    t = lax.broadcasted_iota(jnp.int32, (BLOCK, BLOCK), 0)
    i = lax.broadcasted_iota(jnp.int32, (BLOCK, BLOCK), 1)
    return t <= i


def forward_tile(kv, lo, hi, q_t, acc, top, total, scores, first, masked):
    key = kv[:, :DIM]
    value_t = kv[:, DIM:].T
    for h in range(lo, hi):
        scores[h] = dot(key, q_t[h])
    for h in range(lo, hi):
        s = scores[h]
        if h < masked:
            s = jnp.where(causal(), s, -jnp.inf)
        new_top = jnp.max(s, axis=0, keepdims=True)
        if first:
            w = jnp.exp2((s - new_top) * TO_LOG2)
            total[h : h + 1, :] = jnp.sum(w, axis=0, keepdims=True)
            acc[h] = dot(value_t, w.astype(BF16))
        else:
            old_top = top[h : h + 1, :]
            new_top = jnp.maximum(old_top, new_top)
            w = jnp.exp2((s - new_top) * TO_LOG2)
            fade = jnp.exp2((old_top - new_top) * TO_LOG2)
            total[h : h + 1, :] = total[h : h + 1, :] * fade + jnp.sum(w, axis=0, keepdims=True)
            acc[h] = acc[h] * fade + dot(value_t, w.astype(BF16))
        top[h : h + 1, :] = new_top


def backward_tile(kv, lo, hi, q_t, q, g_t, g, log_total, delta, dq_t, scores, grads, probs, ds, masked):
    key = kv[:, :DIM]
    value = kv[:, DIM:]
    key_t = key.T
    for h in range(lo, hi):
        scores[h] = dot(key, q_t[h])
        grads[h] = dot(value, g_t[h])
    for h in range(lo, hi):
        prob = jnp.exp2(scores[h] * TO_LOG2 - log_total[h : h + 1, :])
        if h < masked:
            prob = jnp.where(causal(), prob, 0.0)
        probs[h] = prob.astype(BF16)
        ds[h] = (prob * (grads[h] - delta[h : h + 1, :])).astype(BF16)
    dv = dot(probs[lo], g[lo])
    dk = dot(ds[lo], q[lo])
    for h in range(lo + 1, hi):
        dv = dv + dot(probs[h], g[h])
        dk = dk + dot(ds[h], q[h])
    for h in range(lo, hi):
        dq_t[h] += dot(key_t, ds[h])
    return jnp.concatenate([dk * SCALE, dv], axis=1)


def finish(o, g_t):
    rounded = o.astype(BF16)
    return rounded, jnp.sum(rounded.astype(F32) * g_t.astype(F32), axis=0, keepdims=True)


def pack(o, log):
    row = lax.broadcasted_iota(jnp.int32, (EXTRA, BLOCK), 0)
    first = log.astype(BF16).astype(F32)
    second = (log - first).astype(BF16).astype(F32)
    third = log - first - second
    tail = jnp.where(row == 0, first, jnp.where(row == 1, second, jnp.where(row == 2, third, 0.0)))
    return jnp.concatenate([o.astype(BF16), tail.astype(BF16)], axis=0)


def log_of(packed):
    return jnp.sum(packed[DIM:].astype(F32), axis=0, keepdims=True)


def merged(a, b):
    log_a = log_of(a)
    log_b = log_of(b)
    top = jnp.maximum(log_a, log_b)
    log = top + jnp.log2(jnp.exp2(log_a - top) + jnp.exp2(log_b - top))
    return a[:DIM].astype(F32) * jnp.exp2(log_a - log) + b[:DIM].astype(F32) * jnp.exp2(log_b - log), log


def start_all(pairs, sems):
    copies = [pltpu.make_async_copy(a, b, sems.at[i]) for i, (a, b) in enumerate(pairs)]
    for copy in copies:
        copy.start()
    return copies


def wait_all(copies):
    for copy in copies:
        copy.wait()


def forward(
    place, kv_in, q_t_in, q_t_next_in, g_t_in,
    out_out, mine_out, next_out, log_narrow, delta_narrow,
    kv, q_t, g_t, acc, out, mine, nexts, top, total, scores, sems, out_sems,
):
    rank = place[0]
    wide = place[1]
    narrow = HALF - wide
    loads = start_all(
        [
            (q_t_in, q_t.at[pl.ds(0, HEADS)]),
            (q_t_next_in, q_t.at[pl.ds(HEADS, HALF)]),
            (kv_in, kv),
            (g_t_in.at[pl.ds(narrow, HALF)], g_t),
        ],
        sems,
    )
    wait_all(loads[:3])
    every = HEADS + HALF
    forward_tile(kv[rank], 0, every, q_t, acc, top, total, scores, True, HEADS)

    def below(b, carry):
        forward_tile(kv[b], 0, every, q_t, acc, top, total, scores, False, 0)
        return carry

    def above(b, carry):
        forward_tile(kv[b], HEADS, every, q_t, acc, top, total, scores, False, 0)
        return carry

    lax.fori_loop(0, rank, below, 0)
    lax.fori_loop(rank + 1, RANKS, above, 0)

    def result(n):
        total_n = total[pl.ds(n, 1), :]
        return acc[n] / total_n, top[pl.ds(n, 1), :] * TO_LOG2 + jnp.log2(total_n)

    for h in range(HALF):
        nexts[h] = pack(*result(HEADS + h))
        mine[h] = pack(*result(wide + h))
    stores = start_all([(nexts, next_out), (mine, mine_out)], out_sems)
    loads[3].wait()
    for h in range(HALF):
        o, log_h = result(narrow + h)
        out[h], delta_narrow[h : h + 1, :] = finish(o, g_t[h])
        log_narrow[h : h + 1, :] = log_h
    last = pltpu.make_async_copy(out, out_out.at[pl.ds(narrow, HALF)], out_sems.at[2])
    last.start()
    wait_all(stores)
    last.wait()


def backward_narrow(
    place, kv_in, q_t_in, q_in, g_t_in, g_in, log_narrow, delta_narrow,
    dq_out, dkv_out,
    kv, q_t, q, g_t, g, dq_t, dq, dkv, scores, grads, probs, ds, sems, tile_sems,
):
    rank = place[0]
    part = pl.ds(HALF - place[1], HALF)
    loads = start_all(
        [(q_t_in.at[part], q_t), (kv_in, kv), (g_t_in.at[part], g_t), (g_in.at[part], g), (q_in.at[part], q)],
        sems,
    )
    dq_t[...] = jnp.zeros_like(dq_t)
    wait_all(loads)

    def store(b):
        return pltpu.make_async_copy(dkv.at[b], dkv_out.at[b], tile_sems.at[b])

    def tile(b, masked):
        dkv[b] = backward_tile(
            kv[b], 0, HALF, q_t, q, g_t, g, log_narrow, delta_narrow, dq_t, scores, grads, probs, ds, masked
        )
        store(b).start()

    tile(rank, HALF)

    def below(b, carry):
        tile(b, 0)
        return carry

    lax.fori_loop(0, rank, below, 0)
    dq[...] = (dq_t[...] * SCALE).astype(BF16)
    last = pltpu.make_async_copy(dq, dq_out, sems.at[5])
    last.start()

    def settle(b, carry):
        store(b).wait()
        return carry

    lax.fori_loop(0, rank + 1, settle, 0)
    last.wait()


def backward_wide(
    place, kv_in, q_t_in, q_in, g_t_in, g_in, q_t_next_in, q_next_in, g_t_next_in, g_next_in,
    mine_in, before_in, next_in, after_in, dkv_narrow_in, out_in,
    out_out, dq_out, dq_next_out, dkv_out,
    kv, q_t, q, g_t, g, mine, before, nexts, after, dkv_narrow, out, dq_t, dq, dkv, log_total, delta,
    scores, grads, probs, ds, sems, out_sems, tile_sems,
):
    rank = place[0]
    part = pl.ds(place[1], HALF)
    first = pl.ds(0, HALF)
    second = pl.ds(HALF, HALF)
    loads = start_all(
        [
            (mine_in, mine), (before_in, before), (g_t_in.at[part], g_t.at[first]),
            (next_in, nexts), (after_in, after), (g_t_next_in, g_t.at[second]),
            (q_t_in.at[part], q_t.at[first]), (q_t_next_in, q_t.at[second]), (kv_in, kv),
            (g_in.at[part], g.at[first]), (g_next_in, g.at[second]),
            (q_in.at[part], q.at[first]), (q_next_in, q.at[second]), (dkv_narrow_in, dkv_narrow),
        ],
        sems,
    )
    dq_t[...] = jnp.zeros_like(dq_t)
    wait_all(loads[:6])
    for h in range(HALF):
        o, log_h = merged(mine[h], before[h])
        out[h], delta[h : h + 1, :] = finish(o, g_t[h])
        log_total[h : h + 1, :] = log_h
        n = HALF + h
        o, log_h = merged(after[h], nexts[h])
        _, delta[n : n + 1, :] = finish(o, g_t[n])
        log_total[n : n + 1, :] = log_h
    out_store = pltpu.make_async_copy(out, out_out.at[part], out_sems.at[0])
    out_store.start()
    wait_all(loads[6:])

    def store(b):
        return pltpu.make_async_copy(dkv.at[b], dkv_out.at[b], tile_sems.at[b])

    def tile(b, lo, masked):
        grad = backward_tile(
            kv[b], lo, HEADS, q_t, q, g_t, g, log_total, delta, dq_t, scores, grads, probs, ds, masked
        )
        if lo == 0:
            grad = grad + dkv_narrow[b]
        dkv[b] = grad.astype(BF16)
        store(b).start()

    tile(rank, 0, HALF)

    def below(b, carry):
        tile(b, 0, 0)
        return carry

    def above(b, carry):
        tile(b, HALF, 0)
        return carry

    lax.fori_loop(0, rank, below, 0)
    lax.fori_loop(rank + 1, RANKS, above, 0)
    dq[...] = (dq_t[...] * SCALE).astype(BF16)
    dq_store = pltpu.make_async_copy(dq.at[first], dq_out, out_sems.at[1])
    dq_next_store = pltpu.make_async_copy(dq.at[second], dq_next_out, out_sems.at[2])
    dq_store.start()
    dq_next_store.start()
    for b in range(RANKS):
        store(b).wait()
    out_store.wait()
    dq_store.wait()
    dq_next_store.wait()


FAR = pl.BlockSpec(memory_space=pltpu.HBM)
NEAR = pl.BlockSpec(memory_space=pltpu.VMEM)


def call(body, outs, ins, scratch, sems, flops, aliases=None):
    return pl.pallas_call(
        body,
        out_shape=[jax.ShapeDtypeStruct(s, t) for s, t, _ in outs],
        in_specs=[pl.BlockSpec(memory_space=pltpu.SMEM)] + [spec for _, spec in ins[1:]],
        out_specs=[spec for _, _, spec in outs],
        scratch_shapes=[pltpu.VMEM(s, t) for s, t in scratch] + [pltpu.SemaphoreType.DMA((n,)) for n in sems],
        input_output_aliases=aliases or {},
        compiler_params=pltpu.CompilerParams(vmem_limit_bytes=LIMIT),
        cost_estimate=pl.CostEstimate(flops=flops, bytes_accessed=4 << 20, transcendentals=1 << 20),
    )(*[a for a, _ in ins])


def ring(size, by):
    return [(i, (i + by) % size) for i in range(size)]


def spread(block):
    many = jnp.broadcast_to(block[None], (RANKS,) + block.shape).reshape((4 * RANKS,) + block.shape[1:])
    got = lax.all_to_all(many, PLANE, 0, 0, tiled=True)
    return got.reshape(RANKS, BLOCK, 2 * DIM)


def collect(grads):
    got = lax.all_to_all(grads.reshape(4 * RANKS, 64, 2 * DIM), PLANE, 0, 0, tiled=True)
    return jnp.sum(got.reshape(RANKS, 4, 64, 2 * DIM).astype(F32), axis=0)


def per_device(queries, key_vectors, value_vectors, out_grad):
    rank = lax.axis_index("ylo") * NX + lax.axis_index("x")
    wide = jnp.where(lax.axis_index("z") % 2 == 0, HALF, 0)
    place = jnp.stack([rank, wide]).astype(jnp.int32)

    block = jnp.transpose(jnp.concatenate([key_vectors, value_vectors], axis=2), (1, 0, 2))
    planes = lax.axis_size("z")
    planes = lax.axis_size("z")
    own = spread(block)

    high = wide == HALF

    def widest(a):
        return jnp.where(high, a[:, HALF:], a[:, :HALF])

    q_next = lax.ppermute(widest(queries), "z", ring(planes, -1))
    g_next = lax.ppermute(widest(out_grad), "z", ring(planes, -1))
    q = jnp.transpose(queries, (1, 0, 2))
    q_t = jnp.transpose(queries, (1, 2, 0))
    g = jnp.transpose(out_grad, (1, 0, 2))
    g_t = jnp.transpose(out_grad, (1, 2, 0))
    q_t_next = jnp.transpose(q_next, (1, 2, 0))
    q_next = jnp.transpose(q_next, (1, 0, 2))
    g_t_next = jnp.transpose(g_next, (1, 2, 0))
    g_next = jnp.transpose(g_next, (1, 0, 2))

    every = HEADS + HALF
    full_t = (HEADS, DIM, BLOCK)
    full = (HEADS, BLOCK, DIM)
    half_t = (HALF, DIM, BLOCK)
    half = (HALF, BLOCK, DIM)
    packed = (HALF, DIM + EXTRA, BLOCK)
    rows = (HEADS, BLOCK)
    few = (HALF, BLOCK)
    square = (HEADS, BLOCK, BLOCK)
    small = (HALF, BLOCK, BLOCK)
    kv_shape = (RANKS, BLOCK, 2 * DIM)
    out_t, mine, nexts, log_narrow, delta_narrow = call(
        forward,
        [(full_t, BF16, FAR), (packed, BF16, FAR), (packed, BF16, FAR), (few, F32, NEAR), (few, F32, NEAR)],
        [(place, None), (own, FAR), (q_t, FAR), (q_t_next, FAR), (g_t, FAR)],
        [
            (kv_shape, BF16), ((every, DIM, BLOCK), BF16), (half_t, BF16), ((every, DIM, BLOCK), F32),
            (half_t, BF16), (packed, BF16), (packed, BF16), ((2 * HEADS, BLOCK), F32), ((2 * HEADS, BLOCK), F32),
            ((every, BLOCK, BLOCK), F32),
        ],
        [4, 3],
        12 << 30,
    )
    before = lax.ppermute(nexts, "z", ring(planes, 1))
    after = lax.ppermute(mine, "z", ring(planes, -1))
    dq_narrow, dkv_narrow = call(
        backward_narrow,
        [(half_t, BF16, FAR), (kv_shape, F32, FAR)],
        [
            (place, None), (own, FAR), (q_t, FAR), (q, FAR), (g_t, FAR), (g, FAR),
            (log_narrow, NEAR), (delta_narrow, NEAR),
        ],
        [
            (kv_shape, BF16), (half_t, BF16), (half, BF16), (half_t, BF16), (half, BF16), (half_t, F32),
            (half_t, BF16), (kv_shape, F32), (small, F32), (small, F32), (small, BF16), (small, BF16),
        ],
        [6, RANKS],
        8 << 30,
    )
    out_t, dq_wide, dq_next, dkv = call(
        backward_wide,
        [(full_t, BF16, FAR), (half_t, BF16, FAR), (half_t, BF16, FAR), (kv_shape, BF16, FAR)],
        [
            (place, None), (own, FAR), (q_t, FAR), (q, FAR), (g_t, FAR), (g, FAR), (q_t_next, FAR), (q_next, FAR),
            (g_t_next, FAR), (g_next, FAR), (mine, FAR), (before, FAR), (nexts, FAR), (after, FAR),
            (dkv_narrow, FAR), (out_t, FAR),
        ],
        [
            (kv_shape, BF16), (full_t, BF16), (full, BF16), (full_t, BF16), (full, BF16),
            (packed, BF16), (packed, BF16), (packed, BF16), (packed, BF16), (kv_shape, F32), (half_t, BF16),
            (full_t, F32), (full_t, BF16), (kv_shape, BF16), (rows, F32), (rows, F32),
            (square, F32), (square, F32), (square, BF16), (square, BF16),
        ],
        [14, 3, RANKS],
        16 << 30,
        {15: 0},
    )
    dq_back = lax.ppermute(dq_next, "z", ring(planes, 1))
    back = jnp.transpose(collect(dkv).astype(BF16), (1, 0, 2))
    attended = jnp.transpose(out_t, (2, 0, 1))
    dq_wide = (dq_wide.astype(F32) + dq_back.astype(F32)).astype(BF16)
    dq_t = jnp.concatenate([jnp.where(high, dq_narrow, dq_wide), jnp.where(high, dq_wide, dq_narrow)], axis=0)
    query_grad = jnp.transpose(dq_t, (2, 0, 1))
    return attended, query_grad, back[:, :, :DIM], back[:, :, DIM:]


def solution(mesh):
    inner = Mesh(mesh.devices.reshape(8, 2, NX, 2, 2), ("z", "ylo", "x", "yhi", "core"))
    tokens = ("z", "ylo", "x")
    heads = ("yhi", "core")
    by_head = P(tokens, heads, None)
    by_token = P(tokens + heads, None, None)
    return jax.shard_map(
        per_device,
        mesh=inner,
        in_specs=(by_head, by_token, by_token, by_head),
        out_specs=(by_head, by_head, by_token, by_token),
        check_vma=False,
    )
```

time: 109 us -> 98.9 us (0.907)
  Pallas kernels: 30 us -> 24.5 us
  starting transfers between devices: 37 us -> 35.1 us
  local copies, waits for them, and re-layouts: 11.1 us -> 9.53 us
    all_to_all x1, starting transfers between devices: 20.5 us -> 14.6 us  [collect(): lax.all_to_all(grads.reshape(4 * RANKS, 64, 2 * DIM), PLANE, 0, 0, tiled=...]
    pallas_call x5 -> x3, Pallas kernels: 30 us -> 24.5 us  [call(): pl.pallas_call(body, out_shape=[jax.ShapeDtypeStruct(s, t) for s, t, _ in...]
    ppermute x5, starting transfers between devices: 7.82 us -> 11.7 us  [the longest x1 5.65 us: per_device(): q_next = lax.ppermute(widest(queries), 'z', ring(planes, -1))]
    transpose x3 -> x2, local copies, waits for them, and re-layouts: 2.72 us -> 1.7 us  [the longest x1 0.86 us: per_device(): g_t_next = jnp.transpose(g_next, (1, 2, 0))]
    unnamed x28 -> x32, local copies, waits for them, and re-layouts: 7.22 us -> 6.68 us
  transfers between devices with their start and end apart: 7 -> 7, of which waited for: 4 -> 6; matrix products, arithmetic and copies ran while one was open for 8% -> 7% of each run, Pallas kernels for 9% -> 4%
where the time goes in v3:
time: 98.9 us; the launch traced here: 98.5 us
  starting transfers between devices  35.1 us (35%)
  waiting for transfers between devices  26.5 us (27%)
  Pallas kernels  24.5 us (25%)
  local copies, waits for them, and re-layouts  9.53 us (10%)
  other arithmetic  1.96 us (2%)
    pallas_call x3, Pallas kernels, call(): pl.pallas_call(body, out_shape=[jax.ShapeDtypeStruct(s, t) for s, t, _ in...  24.5 us
    all_to_all x1, starting transfers between devices, collect(): lax.all_to_all(grads.reshape(4 * RANKS, 64, 2 * DIM), PLANE, 0, 0, tiled=...  14.6 us
    all_to_all x1, starting transfers between devices, spread(): got = lax.all_to_all(many, PLANE, 0, 0, tiled=True)  8.76 us
    ppermute x1, waiting for transfers between devices, per_device(): dq_back = lax.ppermute(dq_next, 'z', ring(planes, 1))  8.29 us
    unnamed x32, local copies, waits for them, and re-layouts  6.68 us
    all_to_all x1, waiting for transfers between devices, collect(): lax.all_to_all(grads.reshape(4 * RANKS, 64, 2 * DIM), PLANE, 0, 0, tiled=...  6.38 us
    ppermute x1, starting transfers between devices, per_device(): q_next = lax.ppermute(widest(queries), 'z', ring(planes, -1))  5.65 us
    ppermute x1, starting transfers between devices, per_device(): after = lax.ppermute(mine, 'z', ring(planes, -1))  5.17 us
  transfers between devices with their start and end apart: 7, of which 6 were waited for; matrix products, arithmetic and copies ran while one was open for 7% of the time, Pallas kernels for 4%

profile of v3, /device:TPU:1, one launch (start us, length us, event | category | flops | bytes accessed | tf_op | source)
XLA Modules:
  0.0 98.5 jit_solution(16360500431172958238)
XLA Ops:
  0.6 1.0 %maximum_bitcast_fusion.1 = bf16[4,64,256]{2,0,1:T(4,128)(2,1)S(1)} fusion(bf16[64,4,128]{2,1,0:T(4,128)(2,1)} %param.6, bf16[64,4,128]{2,1,0:T(4,128)(2,1)} %param.5), kind=kLoop, calls=%fused_computation.6 | loop fusion | flops 262144 | bytes 262144 | tf_op jit(solution)/shard_map/transpose | solution.py:321
  1.7 1.1 %broadcast_in_dim.2 = bf16[8,4,64,256]{3,2,1,0:T(8,128)(2,1)} broadcast(bf16[4,64,256]{2,1,0:T(8,128)(2,1)S(1)} %copy.23), dimensions={1,2,3} | broadcast | bytes 1179648 | tf_op jit(solution)/shard_map/broadcast_in_dim | solution.py:306
  2.8 8.8 %all-to-all-start = ((bf16[32,64,256]{2,1,0:T(8,128)(2,1)}), bf16[32,64,256]{2,1,0:T(8,128)(2,1)}, u32[]{:S(2)}, u32[]{:S(2)}) async-start(bf16[32,64,256]{2,1,0:T(8,128)(2,1)} %bitcast.3), calls=%async_computation | async-start | bytes 2097152 | tf_op jit(solution)/shard_map/all_to_all | solution.py:307
  11.6 0.1 copy.44
  11.7 0.0 copy-start.2
  11.7 5.7 %collective-permute-start = (bf16[256,4,128]{2,0,1:T(8,128)(2,1)S(1)}, bf16[256,4,128]{2,0,1:T(8,128)(2,1)S(1)}, u32[]{:S(2)}, u32[]{:S(2)}) collective-permute-start(bf16[256,4,128]{2,0,1:T(8,128)(2,1)S(1)} %slice_select_fusion.1), channel_id=1, source_target_pairs={{0,224},{32,0},{64,32},{96,64},{128,96},{160,128},{192,160},{224,1... | collective-permute-start | bytes 786440 | tf_op jit(solution)/shard_map/ppermute | solution.py:331
  17.4 0.1 copy.43
  17.5 0.8 collective-permute-start.1
  18.3 1.1 %copy.24 = bf16[256,8,128]{0,2,1:T(8,128)(2,1)} copy(bf16[256,8,128]{2,1,0:T(8,128)(2,1)S(1)} %copy-done) | data formatting | bytes 1048576 | tf_op args[0]
  19.4 1.1 %copy.26 = bf16[256,8,128]{0,2,1:T(8,128)(2,1)} copy(bf16[256,8,128]{2,1,0:T(8,128)(2,1)S(1)} %copy-done.1) | data formatting | bytes 1048576 | tf_op args[3]
  20.6 0.6 pad_add_fusion.place
  21.1 1.6 %collective-permute-done = bf16[256,4,128]{2,0,1:T(8,128)(2,1)S(1)} collective-permute-done((bf16[256,4,128]{2,0,1:T(8,128)(2,1)S(1)}, bf16[256,4,128]{2,0,1:T(8,128)(2,1)S(1)}, u32[]{:S(2)}, u32[]{:S(2)}) %collective-permute-start) | collective-permute-done | bytes 262176 | tf_op jit(solution)/shard_map/ppermute | solution.py:331
  22.7 0.8 copy.33.q_t_next_in
  23.5 4.8 %collective-permute-done.1 = bf16[256,4,128]{2,0,1:T(8,128)(2,1)S(1)} collective-permute-done((bf16[256,4,128]{2,0,1:T(8,128)(2,1)S(1)}, bf16[256,4,128]{2,0,1:T(8,128)(2,1)S(1)}, u32[]{:S(2)}, u32[]{:S(2)}) %collective-permute-start.1) | collective-permute-done | bytes 262176 | tf_op jit(solution)/shard_map/ppermute | solution.py:332
  28.3 0.9 copy.34.g_t_next_in
  29.2 9.0 %shard_map.75 = (bf16[8,128,256]{2,1,0:T(8,128)(2,1)}, bf16[4,144,256]{2,1,0:T(8,128)(2,1)}, bf16[4,144,256]{2,1,0:T(8,128)(2,1)}, f32[4,256]{1,0:T(4,128)}, f32[4,256]{1,0:T(4,128)}) custom-call(s32[2]{0:T(128)} %pad_add_fusion.place, bf16[8,256,256]{2,1,0:T(8,128)(2,1)} %bitcast.4.kv_in, bf16[8,128,256]{2,1,0:T(8,128)(2,1)} %bitcast.29, ...), custom_call_target="tpu_custom_call" | custom-call | flops 12884901888 | bytes 4194304 | tf_op jit(solution)/shard_map/pallas_call | solution.py:289
  38.2 5.2 %collective-permute-start.3 = (bf16[4,144,256]{2,1,0:T(8,128)(2,1)}, bf16[4,144,256]{2,1,0:T(8,128)(2,1)S(1)}, u32[]{:S(2)}, u32[]{:S(2)}) collective-permute-start(bf16[4,144,256]{2,1,0:T(8,128)(2,1)} %get-tuple-element.15.mine_in), channel_id=1, source_target_pairs={{0,224},{32,0},{64,32},{96,64},{128,96},{160,128},{192,160},{224,1... | collective-permute-start | bytes 884744 | tf_op jit(solution)/shard_map/ppermute | solution.py:366
  43.4 3.8 %shard_map.76 = (bf16[4,128,256]{2,1,0:T(8,128)(2,1)}, f32[8,256,256]{2,1,0:T(8,128)}) custom-call(s32[2]{0:T(128)} %pad_add_fusion.place, bf16[8,256,256]{2,1,0:T(8,128)(2,1)} %bitcast.4.kv_in, bf16[8,128,256]{2,1,0:T(8,128)(2,1)} %bitcast.30, bf16[8,256,128]{2,1,0:T(8,128)(2,1)} %bitcast.23, bf16[8,128,256]{2,1,0:T(8,128)(2,1)} %bitcast.33, ...), custom_call_target="tpu_custom_call" | custom-call | flops 8589934592 | bytes 4194304 | tf_op jit(solution)/shard_map/pallas_call | solution.py:289
  47.2 2.4 %collective-permute-done.3.after_in = bf16[4,144,256]{2,1,0:T(8,128)(2,1)S(1)} collective-permute-done((bf16[4,144,256]{2,1,0:T(8,128)(2,1)}, bf16[4,144,256]{2,1,0:T(8,128)(2,1)S(1)}, u32[]{:S(2)}, u32[]{:S(2)}) %collective-permute-start.3) | collective-permute-done | bytes 294944 | tf_op jit(solution)/shard_map/ppermute | solution.py:366
  49.6 3.0 %collective-permute-done.2.before_in = bf16[4,144,256]{2,1,0:T(8,128)(2,1)S(1)} collective-permute-done((bf16[4,144,256]{2,1,0:T(8,128)(2,1)}, bf16[4,144,256]{2,1,0:T(8,128)(2,1)S(1)}, u32[]{:S(2)}, u32[]{:S(2)}) %collective-permute-start.2) | collective-permute-done | bytes 294944 | tf_op jit(solution)/shard_map/ppermute | solution.py:365
  52.7 0.7 copy-done.10
  53.4 11.7 %shard_map.77 = (bf16[8,128,256]{2,1,0:T(8,128)(2,1)}, bf16[4,128,256]{2,1,0:T(8,128)(2,1)}, bf16[4,128,256]{2,1,0:T(8,128)(2,1)}, bf16[8,256,256]{2,1,0:T(8,128)(2,1)}) custom-call(s32[2]{0:T(128)} %pad_add_fusion.place, bf16[8,256,256]{2,1,0:T(8,128)(2,1)} %bitcast.4.kv_in, bf16[8,128,256]{2,1,0:T(8,128)(2,1)} %bitcast.31, ...), custom_call_target="tpu_custom_call", output_to_operand_aliasing={{0}: (15, {})} | custom-call | flops 17179869184 | bytes 4194304 | tf_op jit(solution)/shard_map/pallas_call | solution.py:289
  65.2 14.6 %all-to-all-start.1 = ((bf16[32,64,256]{2,1,0:T(8,128)(2,1)}), bf16[32,64,256]{2,1,0:T(8,128)(2,1)S(1)}, u32[]{:S(2)}, u32[]{:S(2)}) async-start(bf16[32,64,256]{2,1,0:T(8,128)(2,1)} %bitcast.27), calls=%async_computation.1 | async-start | bytes 2097152 | tf_op jit(solution)/shard_map/all_to_all | solution.py:312
  79.8 0.1 collective-permute-start.4
  79.9 1.1 %copy.35 = bf16[256,8,128]{2,1,0:T(8,128)(2,1)} copy(bf16[256,8,128]{0,2,1:T(8,128)(2,1)S(1)} %bitcast.35) | data formatting | bytes 1048576
  81.0 8.3 %collective-permute-done.4 = bf16[4,128,256]{2,1,0:T(8,128)(2,1)S(1)} collective-permute-done((bf16[4,128,256]{2,1,0:T(8,128)(2,1)S(1)}, bf16[4,128,256]{2,1,0:T(8,128)(2,1)S(1)}, u32[]{:S(2)}, u32[]{:S(2)}) %collective-permute-start.4) | collective-permute-done | bytes 262176 | tf_op jit(solution)/shard_map/ppermute | solution.py:399
  89.3 0.1 broadcast_select_fusion.1
  89.5 1.1 %copy.36 = bf16[256,8,128]{2,1,0:T(8,128)(2,1)} copy(bf16[256,8,128]{0,2,1:T(8,128)(2,1)S(1)} %maximum_bitcast_fusion) | data formatting | bytes 1048576
  90.5 6.4 %all-to-all-done.1 = bf16[32,64,256]{2,1,0:T(8,128)(2,1)S(1)} async-done(((bf16[32,64,256]{2,1,0:T(8,128)(2,1)}), bf16[32,64,256]{2,1,0:T(8,128)(2,1)S(1)}, u32[]{:S(2)}, u32[]{:S(2)}) %all-to-all-start.1) | async-done | bytes 1048608 | tf_op jit(solution)/shard_map/all_to_all | solution.py:312
  96.9 0.1 reduce_sum.12
  97.1 0.7 copy.38
  97.8 0.7 copy.37
  (29 shorter events, 0.2 us)
Async XLA Ops:
  0.6 10.9 %copy-start = (bf16[256,8,128]{2,1,0:T(8,128)(2,1)S(1)}, bf16[256,8,128]{2,1,0:T(8,128)(2,1)}, u32[]{:S(2)}) copy-start(bf16[256,8,128]{2,1,0:T(8,128)(2,1)} %param.4) | copy-start | bytes 1572868
  2.8 14.6 %copy-start.1 = (bf16[256,8,128]{2,1,0:T(8,128)(2,1)S(1)}, bf16[256,8,128]{2,1,0:T(8,128)(2,1)}, u32[]{:S(2)}) copy-start(bf16[256,8,128]{2,1,0:T(8,128)(2,1)} %param.7) | copy-start | bytes 1572868
  2.8 26.4 %all-to-all-start = ((bf16[32,64,256]{2,1,0:T(8,128)(2,1)}), bf16[32,64,256]{2,1,0:T(8,128)(2,1)}, u32[]{:S(2)}, u32[]{:S(2)}) async-start(bf16[32,64,256]{2,1,0:T(8,128)(2,1)} %bitcast.3), calls=%async_computation | async-start | bytes 2097152 | tf_op jit(solution)/shard_map/all_to_all | solution.py:307
  11.7 8.9 %copy-start.2 = (bf16[256,8,128]{2,0,1:T(8,128)(2,1)}, bf16[256,8,128]{2,0,1:T(8,128)(2,1)S(1)}, u32[]{:S(2)}) copy-start(bf16[256,8,128]{2,0,1:T(8,128)(2,1)S(1)} %copy.44) | copy-start | bytes 1572868
  11.7 11.0 %collective-permute-start = (bf16[256,4,128]{2,0,1:T(8,128)(2,1)S(1)}, bf16[256,4,128]{2,0,1:T(8,128)(2,1)S(1)}, u32[]{:S(2)}, u32[]{:S(2)}) collective-permute-start(bf16[256,4,128]{2,0,1:T(8,128)(2,1)S(1)} %slice_select_fusion.1), channel_id=1, source_target_pairs={{0,224},{32,0},{64,32},{96,64},{128,96},{160,128},{192,160},{224,1... | collective-permute-start | bytes 786440 | tf_op jit(solution)/shard_map/ppermute | solution.py:331
  17.4 3.1 %copy-start.3 = (bf16[256,8,128]{2,0,1:T(8,128)(2,1)}, bf16[256,8,128]{2,0,1:T(8,128)(2,1)S(1)}, u32[]{:S(2)}) copy-start(bf16[256,8,128]{2,0,1:T(8,128)(2,1)S(1)} %copy.43) | copy-start | bytes 1572868
  17.5 10.8 %collective-permute-start.1 = (bf16[256,4,128]{2,0,1:T(8,128)(2,1)S(1)}, bf16[256,4,128]{2,0,1:T(8,128)(2,1)S(1)}, u32[]{:S(2)}, u32[]{:S(2)}) collective-permute-start(bf16[256,4,128]{2,0,1:T(8,128)(2,1)S(1)} %slice_select_fusion), channel_id=1, source_target_pairs={{0,224},{32,0},{64,32},{96,64},{128,96},{160,128},{192,160},{224,1... | collective-permute-start | bytes 786440 | tf_op jit(solution)/shard_map/ppermute | solution.py:332
  22.7 15.5 %copy-start.7 = (bf16[256,4,128]{2,0,1:T(8,128)(2,1)}, bf16[256,4,128]{2,0,1:T(8,128)(2,1)S(1)}, u32[]{:S(2)}) copy-start(bf16[256,4,128]{2,0,1:T(8,128)(2,1)S(1)} %collective-permute-done) | copy-start | bytes 786436
  28.3 9.9 %copy-start.8 = (bf16[256,4,128]{2,0,1:T(8,128)(2,1)}, bf16[256,4,128]{2,0,1:T(8,128)(2,1)S(1)}, u32[]{:S(2)}) copy-start(bf16[256,4,128]{2,0,1:T(8,128)(2,1)S(1)} %collective-permute-done.1) | copy-start | bytes 786436
  38.2 11.4 %collective-permute-start.3 = (bf16[4,144,256]{2,1,0:T(8,128)(2,1)}, bf16[4,144,256]{2,1,0:T(8,128)(2,1)S(1)}, u32[]{:S(2)}, u32[]{:S(2)}) collective-permute-start(bf16[4,144,256]{2,1,0:T(8,128)(2,1)} %get-tuple-element.15.mine_in), channel_id=1, source_target_pairs={{0,224},{32,0},{64,32},{96,64},{128,96},{160,128},{192,160},{224,1... | collective-permute-start | bytes 884744 | tf_op jit(solution)/shard_map/ppermute | solution.py:366
  43.4 9.3 %collective-permute-start.2 = (bf16[4,144,256]{2,1,0:T(8,128)(2,1)}, bf16[4,144,256]{2,1,0:T(8,128)(2,1)S(1)}, u32[]{:S(2)}, u32[]{:S(2)}) collective-permute-start(bf16[4,144,256]{2,1,0:T(8,128)(2,1)} %get-tuple-element.16.next_in), channel_id=1, source_target_pairs={{0,32},{32,64},{64,96},{96,128},{128,160},{160,192},{192,224},{224... | collective-permute-start | bytes 884744 | tf_op jit(solution)/shard_map/ppermute | solution.py:365
  49.6 3.0 %copy-start.9 = (bf16[4,144,256]{2,1,0:T(8,128)(2,1)}, bf16[4,144,256]{2,1,0:T(8,128)(2,1)S(1)}, u32[]{:S(2)}) copy-start(bf16[4,144,256]{2,1,0:T(8,128)(2,1)S(1)} %collective-permute-done.3.after_in) | copy-start | bytes 884740
  52.7 0.7 copy-start.10
  65.1 14.7 %copy-start.11 = (bf16[4,128,256]{2,1,0:T(8,128)(2,1)S(1)}, bf16[4,128,256]{2,1,0:T(8,128)(2,1)}, u32[]{:S(2)}) copy-start(bf16[4,128,256]{2,1,0:T(8,128)(2,1)} %get-tuple-element.24) | copy-start | bytes 786436
  65.1 14.8 %copy-start.4 = (bf16[8,128,256]{2,1,0:T(8,128)(2,1)S(1)}, bf16[8,128,256]{2,1,0:T(8,128)(2,1)}, u32[]{:S(2)}) copy-start(bf16[8,128,256]{2,1,0:T(8,128)(2,1)} %get-tuple-element.21) | copy-start | bytes 1572868
  65.1 24.1 %copy-start.5 = (bf16[4,128,256]{2,1,0:T(8,128)(2,1)S(1)}, bf16[4,128,256]{2,1,0:T(8,128)(2,1)}, u32[]{:S(2)}) copy-start(bf16[4,128,256]{2,1,0:T(8,128)(2,1)} %get-tuple-element.22) | copy-start | bytes 786436
  65.1 24.1 %copy-start.6 = (bf16[4,128,256]{2,1,0:T(8,128)(2,1)S(1)}, bf16[4,128,256]{2,1,0:T(8,128)(2,1)}, u32[]{:S(2)}) copy-start(bf16[4,128,256]{2,1,0:T(8,128)(2,1)} %get-tuple-element.23) | copy-start | bytes 786436
  65.2 31.8 %all-to-all-start.1 = ((bf16[32,64,256]{2,1,0:T(8,128)(2,1)}), bf16[32,64,256]{2,1,0:T(8,128)(2,1)S(1)}, u32[]{:S(2)}, u32[]{:S(2)}) async-start(bf16[32,64,256]{2,1,0:T(8,128)(2,1)} %bitcast.27), calls=%async_computation.1 | async-start | bytes 2097152 | tf_op jit(solution)/shard_map/all_to_all | solution.py:312
  79.8 9.5 %collective-permute-start.4 = (bf16[4,128,256]{2,1,0:T(8,128)(2,1)S(1)}, bf16[4,128,256]{2,1,0:T(8,128)(2,1)S(1)}, u32[]{:S(2)}, u32[]{:S(2)}) collective-permute-start(bf16[4,128,256]{2,1,0:T(8,128)(2,1)S(1)} %copy-done.11), channel_id=1, source_target_pairs={{0,32},{32,64},{64,96},{96,128},{128,160},{160,192},{192,224},{224... | collective-permute-start | bytes 786440 | tf_op jit(solution)/shard_map/ppermute | solution.py:399

commit v4 on v3

--- a/solution.py
+++ b/solution.py
@@ -13,6 +13,8 @@
 HALF = 4
 NX = 4
 RANKS = 8
+TILE = 2 * BLOCK
+TILES = RANKS * BLOCK // TILE
 EXTRA = 16
 LIMIT = 63 << 20
 SCALE = 1.0 / math.sqrt(DIM)
@@ -26,13 +28,13 @@
     return jnp.dot(a, b, preferred_element_type=F32)
 
 
-def causal():
-    t = lax.broadcasted_iota(jnp.int32, (BLOCK, BLOCK), 0)
-    i = lax.broadcasted_iota(jnp.int32, (BLOCK, BLOCK), 1)
-    return t <= i
-
-
-def forward_tile(kv, lo, hi, q_t, acc, top, total, scores, first, masked):
+def causal(place):
+    t = lax.broadcasted_iota(jnp.int32, (TILE, BLOCK), 0)
+    i = lax.broadcasted_iota(jnp.int32, (TILE, BLOCK), 1)
+    return t <= i + lax.rem(place[0], TILE // BLOCK) * BLOCK
+
+
+def forward_tile(place, kv, lo, hi, q_t, acc, top, total, scores, first, masked):
     key = kv[:, :DIM]
     value_t = kv[:, DIM:].T
     for h in range(lo, hi):
@@ -40,7 +42,7 @@
     for h in range(lo, hi):
         s = scores[h]
         if h < masked:
-            s = jnp.where(causal(), s, -jnp.inf)
+            s = jnp.where(causal(place), s, -jnp.inf)
         new_top = jnp.max(s, axis=0, keepdims=True)
         if first:
             w = jnp.exp2((s - new_top) * TO_LOG2)
@@ -56,7 +58,9 @@
         top[h : h + 1, :] = new_top
 
 
-def backward_tile(kv, lo, hi, q_t, q, g_t, g, log_total, delta, dq_t, scores, grads, probs, ds, masked):
+def backward_tile(
+    place, kv, lo, hi, q_t, q, g_t, g, log_total, delta, dq_t, scores, grads, probs, ds, masked, ready=None
+):
     key = kv[:, :DIM]
     value = kv[:, DIM:]
     key_t = key.T
@@ -66,9 +70,11 @@
     for h in range(lo, hi):
         prob = jnp.exp2(scores[h] * TO_LOG2 - log_total[h : h + 1, :])
         if h < masked:
-            prob = jnp.where(causal(), prob, 0.0)
+            prob = jnp.where(causal(place), prob, 0.0)
         probs[h] = prob.astype(BF16)
         ds[h] = (prob * (grads[h] - delta[h : h + 1, :])).astype(BF16)
+    if ready is not None:
+        ready()
     dv = dot(probs[lo], g[lo])
     dk = dot(ds[lo], q[lo])
     for h in range(lo + 1, hi):
@@ -136,18 +142,19 @@
     )
     wait_all(loads[:3])
     every = HEADS + HALF
-    forward_tile(kv[rank], 0, every, q_t, acc, top, total, scores, True, HEADS)
+    mine_at = lax.div(rank, TILE // BLOCK)
+    forward_tile(place, kv[mine_at], 0, every, q_t, acc, top, total, scores, True, HEADS)
 
     def below(b, carry):
-        forward_tile(kv[b], 0, every, q_t, acc, top, total, scores, False, 0)
+        forward_tile(place, kv[b], 0, every, q_t, acc, top, total, scores, False, 0)
         return carry
 
     def above(b, carry):
-        forward_tile(kv[b], HEADS, every, q_t, acc, top, total, scores, False, 0)
-        return carry
-
-    lax.fori_loop(0, rank, below, 0)
-    lax.fori_loop(rank + 1, RANKS, above, 0)
+        forward_tile(place, kv[b], HEADS, every, q_t, acc, top, total, scores, False, 0)
+        return carry
+
+    lax.fori_loop(0, mine_at, below, 0)
+    lax.fori_loop(mine_at + 1, TILES, above, 0)
 
     def result(n):
         total_n = total[pl.ds(n, 1), :]
@@ -173,31 +180,32 @@
     dq_out, dkv_out,
     kv, q_t, q, g_t, g, dq_t, dq, dkv, scores, grads, probs, ds, sems, tile_sems,
 ):
-    rank = place[0]
+    mine_at = lax.div(place[0], TILE // BLOCK)
     part = pl.ds(HALF - place[1], HALF)
     loads = start_all(
         [(q_t_in.at[part], q_t), (kv_in, kv), (g_t_in.at[part], g_t), (g_in.at[part], g), (q_in.at[part], q)],
         sems,
     )
     dq_t[...] = jnp.zeros_like(dq_t)
-    wait_all(loads)
+    wait_all(loads[:3])
 
     def store(b):
         return pltpu.make_async_copy(dkv.at[b], dkv_out.at[b], tile_sems.at[b])
 
-    def tile(b, masked):
+    def tile(b, masked, ready=None):
         dkv[b] = backward_tile(
-            kv[b], 0, HALF, q_t, q, g_t, g, log_narrow, delta_narrow, dq_t, scores, grads, probs, ds, masked
+            place, kv[b], 0, HALF, q_t, q, g_t, g, log_narrow, delta_narrow, dq_t, scores, grads, probs, ds,
+            masked, ready,
         )
         store(b).start()
 
-    tile(rank, HALF)
+    tile(mine_at, HALF, lambda: wait_all(loads[3:]))
 
     def below(b, carry):
         tile(b, 0)
         return carry
 
-    lax.fori_loop(0, rank, below, 0)
+    lax.fori_loop(0, mine_at, below, 0)
     dq[...] = (dq_t[...] * SCALE).astype(BF16)
     last = pltpu.make_async_copy(dq, dq_out, sems.at[5])
     last.start()
@@ -206,18 +214,18 @@
         store(b).wait()
         return carry
 
-    lax.fori_loop(0, rank + 1, settle, 0)
+    lax.fori_loop(0, mine_at + 1, settle, 0)
     last.wait()
 
 
 def backward_wide(
-    place, kv_in, q_t_in, q_in, g_t_in, g_in, q_t_next_in, q_next_in, g_t_next_in, g_next_in,
+    place, kv_in, q_t_in, q_in, g_t_in, g_in, q_t_next_in, g_t_next_in,
     mine_in, before_in, next_in, after_in, dkv_narrow_in, out_in,
     out_out, dq_out, dq_next_out, dkv_out,
     kv, q_t, q, g_t, g, mine, before, nexts, after, dkv_narrow, out, dq_t, dq, dkv, log_total, delta,
     scores, grads, probs, ds, sems, out_sems, tile_sems,
 ):
-    rank = place[0]
+    mine_at = lax.div(place[0], TILE // BLOCK)
     part = pl.ds(place[1], HALF)
     first = pl.ds(0, HALF)
     second = pl.ds(HALF, HALF)
@@ -225,9 +233,8 @@
         [
             (mine_in, mine), (before_in, before), (g_t_in.at[part], g_t.at[first]),
             (next_in, nexts), (after_in, after), (g_t_next_in, g_t.at[second]),
-            (q_t_in.at[part], q_t.at[first]), (q_t_next_in, q_t.at[second]), (kv_in, kv),
-            (g_in.at[part], g.at[first]), (g_next_in, g.at[second]),
-            (q_in.at[part], q.at[first]), (q_next_in, q.at[second]), (dkv_narrow_in, dkv_narrow),
+            (q_t_next_in, q_t.at[second]), (q_t_in.at[part], q_t.at[first]), (kv_in, kv),
+            (g_in.at[part], g.at[first]), (q_in.at[part], q.at[first]), (dkv_narrow_in, dkv_narrow),
         ],
         sems,
     )
@@ -243,21 +250,26 @@
         log_total[n : n + 1, :] = log_h
     out_store = pltpu.make_async_copy(out, out_out.at[part], out_sems.at[0])
     out_store.start()
-    wait_all(loads[6:])
+    wait_all(loads[6:7])
+    for n in range(HALF, HEADS):
+        q[n] = q_t[n].T
+        g[n] = g_t[n].T
+    wait_all(loads[7:9])
 
     def store(b):
         return pltpu.make_async_copy(dkv.at[b], dkv_out.at[b], tile_sems.at[b])
 
-    def tile(b, lo, masked):
+    def tile(b, lo, masked, ready=None):
         grad = backward_tile(
-            kv[b], lo, HEADS, q_t, q, g_t, g, log_total, delta, dq_t, scores, grads, probs, ds, masked
+            place, kv[b], lo, HEADS, q_t, q, g_t, g, log_total, delta, dq_t, scores, grads, probs, ds,
+            masked, ready,
         )
         if lo == 0:
             grad = grad + dkv_narrow[b]
         dkv[b] = grad.astype(BF16)
         store(b).start()
 
-    tile(rank, 0, HALF)
+    tile(mine_at, 0, HALF, lambda: wait_all(loads[9:]))
 
     def below(b, carry):
         tile(b, 0, 0)
@@ -267,14 +279,14 @@
         tile(b, HALF, 0)
         return carry
 
-    lax.fori_loop(0, rank, below, 0)
-    lax.fori_loop(rank + 1, RANKS, above, 0)
+    lax.fori_loop(0, mine_at, below, 0)
+    lax.fori_loop(mine_at + 1, TILES, above, 0)
     dq[...] = (dq_t[...] * SCALE).astype(BF16)
     dq_store = pltpu.make_async_copy(dq.at[first], dq_out, out_sems.at[1])
     dq_next_store = pltpu.make_async_copy(dq.at[second], dq_next_out, out_sems.at[2])
     dq_store.start()
     dq_next_store.start()
-    for b in range(RANKS):
+    for b in range(TILES):
         store(b).wait()
     out_store.wait()
     dq_store.wait()
@@ -305,7 +317,7 @@
 def spread(block):
     many = jnp.broadcast_to(block[None], (RANKS,) + block.shape).reshape((4 * RANKS,) + block.shape[1:])
     got = lax.all_to_all(many, PLANE, 0, 0, tiled=True)
-    return got.reshape(RANKS, BLOCK, 2 * DIM)
+    return got.reshape(TILES, TILE, 2 * DIM)
 
 
 def collect(grads):
@@ -325,19 +337,16 @@
 
     high = wide == HALF
 
-    def widest(a):
-        return jnp.where(high, a[:, HALF:], a[:, :HALF])
-
-    q_next = lax.ppermute(widest(queries), "z", ring(planes, -1))
-    g_next = lax.ppermute(widest(out_grad), "z", ring(planes, -1))
     q = jnp.transpose(queries, (1, 0, 2))
     q_t = jnp.transpose(queries, (1, 2, 0))
     g = jnp.transpose(out_grad, (1, 0, 2))
     g_t = jnp.transpose(out_grad, (1, 2, 0))
-    q_t_next = jnp.transpose(q_next, (1, 2, 0))
-    q_next = jnp.transpose(q_next, (1, 0, 2))
-    g_t_next = jnp.transpose(g_next, (1, 2, 0))
-    g_next = jnp.transpose(g_next, (1, 0, 2))
+
+    def widest(a):
+        return jnp.where(high, a[HALF:], a[:HALF])
+
+    q_t_next = lax.ppermute(widest(q_t), "z", ring(planes, -1))
+    g_t_next = lax.ppermute(widest(g_t), "z", ring(planes, -1))
 
     every = HEADS + HALF
     full_t = (HEADS, DIM, BLOCK)
@@ -347,9 +356,9 @@
     packed = (HALF, DIM + EXTRA, BLOCK)
     rows = (HEADS, BLOCK)
     few = (HALF, BLOCK)
-    square = (HEADS, BLOCK, BLOCK)
-    small = (HALF, BLOCK, BLOCK)
-    kv_shape = (RANKS, BLOCK, 2 * DIM)
+    square = (HEADS, TILE, BLOCK)
+    small = (HALF, TILE, BLOCK)
+    kv_shape = (TILES, TILE, 2 * DIM)
     out_t, mine, nexts, log_narrow, delta_narrow = call(
         forward,
         [(full_t, BF16, FAR), (packed, BF16, FAR), (packed, BF16, FAR), (few, F32, NEAR), (few, F32, NEAR)],
@@ -357,7 +366,7 @@
         [
             (kv_shape, BF16), ((every, DIM, BLOCK), BF16), (half_t, BF16), ((every, DIM, BLOCK), F32),
             (half_t, BF16), (packed, BF16), (packed, BF16), ((2 * HEADS, BLOCK), F32), ((2 * HEADS, BLOCK), F32),
-            ((every, BLOCK, BLOCK), F32),
+            ((every, TILE, BLOCK), F32),
         ],
         [4, 3],
         12 << 30,
@@ -375,15 +384,15 @@
             (kv_shape, BF16), (half_t, BF16), (half, BF16), (half_t, BF16), (half, BF16), (half_t, F32),
             (half_t, BF16), (kv_shape, F32), (small, F32), (small, F32), (small, BF16), (small, BF16),
         ],
-        [6, RANKS],
+        [6, TILES],
         8 << 30,
     )
     out_t, dq_wide, dq_next, dkv = call(
         backward_wide,
         [(full_t, BF16, FAR), (half_t, BF16, FAR), (half_t, BF16, FAR), (kv_shape, BF16, FAR)],
         [
-            (place, None), (own, FAR), (q_t, FAR), (q, FAR), (g_t, FAR), (g, FAR), (q_t_next, FAR), (q_next, FAR),
-            (g_t_next, FAR), (g_next, FAR), (mine, FAR), (before, FAR), (nexts, FAR), (after, FAR),
+            (place, None), (own, FAR), (q_t, FAR), (q, FAR), (g_t, FAR), (g, FAR), (q_t_next, FAR),
+            (g_t_next, FAR), (mine, FAR), (before, FAR), (nexts, FAR), (after, FAR),
             (dkv_narrow, FAR), (out_t, FAR),
         ],
         [
@@ -392,9 +401,9 @@
             (full_t, F32), (full_t, BF16), (kv_shape, BF16), (rows, F32), (rows, F32),
             (square, F32), (square, F32), (square, BF16), (square, BF16),
         ],
-        [14, 3, RANKS],
+        [12, 3, TILES],
         16 << 30,
-        {15: 0},
+        {13: 0},
     )
     dq_back = lax.ppermute(dq_next, "z", ring(planes, 1))
     back = jnp.transpose(collect(dkv).astype(BF16), (1, 0, 2))

time: 98.9 us -> 94.7 us (0.958)
  starting transfers between devices: 35.1 us -> 32.6 us
  local copies, waits for them, and re-layouts: 9.53 us -> 7.25 us
  waiting for transfers between devices: 26.5 us -> 27.6 us
    all_to_all x1, waiting for transfers between devices: 0.01 us -> 5.75 us  [spread(): got = lax.all_to_all(many, PLANE, 0, 0, tiled=True)]
    ppermute x2, waiting for transfers between devices: 6.35 us -> 2.4 us  [the longest x1 2.39 us: per_device(): q_t_next = lax.ppermute(widest(q_t), 'z', ring(planes, -1))]
    all_to_all x1, starting transfers between devices: 14.6 us -> 11.7 us  [collect(): lax.all_to_all(grads.reshape(4 * RANKS, 64, 2 * DIM), PLANE, 0, 0, tiled=...]
    unnamed x32 -> x28, local copies, waits for them, and re-layouts: 6.68 us -> 4.93 us
  transfers between devices with their start and end apart: 7 -> 7, of which waited for: 6 -> 6; matrix products, arithmetic and copies ran while one was open for 7% -> 5% of each run, Pallas kernels for 4% -> 14%
where the time goes in v4:
time: 94.7 us; the launch traced here: 94.2 us
  starting transfers between devices  32.6 us (34%)
  waiting for transfers between devices  27.6 us (29%)
  Pallas kernels  23.9 us (25%)
  local copies, waits for them, and re-layouts  7.25 us (8%)
  other arithmetic  1.97 us (2%)
    pallas_call x3, Pallas kernels, call(): pl.pallas_call(body, out_shape=[jax.ShapeDtypeStruct(s, t) for s, t, _ in...  23.9 us
    all_to_all x1, starting transfers between devices, collect(): lax.all_to_all(grads.reshape(4 * RANKS, 64, 2 * DIM), PLANE, 0, 0, tiled=...  11.7 us
    all_to_all x1, starting transfers between devices, spread(): got = lax.all_to_all(many, PLANE, 0, 0, tiled=True)  8.76 us
    ppermute x1, waiting for transfers between devices, per_device(): dq_back = lax.ppermute(dq_next, 'z', ring(planes, 1))  7.74 us
    all_to_all x1, waiting for transfers between devices, collect(): lax.all_to_all(grads.reshape(4 * RANKS, 64, 2 * DIM), PLANE, 0, 0, tiled=...  6.93 us
    all_to_all x1, waiting for transfers between devices, spread(): got = lax.all_to_all(many, PLANE, 0, 0, tiled=True)  5.75 us
    ppermute x1, starting transfers between devices, per_device(): q_t_next = lax.ppermute(widest(q_t), 'z', ring(planes, -1))  5.65 us
    ppermute x1, starting transfers between devices, per_device(): after = lax.ppermute(mine, 'z', ring(planes, -1))  5.64 us
  transfers between devices with their start and end apart: 7, of which 6 were waited for; matrix products, arithmetic and copies ran while one was open for 5% of the time, Pallas kernels for 14%

profile of v4, /device:TPU:1, one launch (start us, length us, event | category | flops | bytes accessed | tf_op | source)
XLA Modules:
  0.0 94.2 jit_solution(16530921631302174949)
XLA Ops:
  0.6 0.0 copy-start.2
  0.6 1.0 %maximum_bitcast_fusion.1 = bf16[4,64,256]{2,0,1:T(4,128)(2,1)S(1)} fusion(bf16[64,4,128]{2,1,0:T(4,128)(2,1)} %param.6, bf16[64,4,128]{2,1,0:T(4,128)(2,1)} %param.5), kind=kLoop, calls=%fused_computation.8 | loop fusion | flops 262144 | bytes 262144 | tf_op jit(solution)/shard_map/transpose | solution.py:333
  1.7 1.1 %broadcast_in_dim.2 = bf16[8,4,64,256]{3,2,1,0:T(8,128)(2,1)} broadcast(bf16[4,64,256]{2,1,0:T(8,128)(2,1)S(1)} %copy.16), dimensions={1,2,3} | broadcast | bytes 1179648 | tf_op jit(solution)/shard_map/broadcast_in_dim | solution.py:318
  2.8 8.8 %all-to-all-start = ((bf16[32,64,256]{2,1,0:T(8,128)(2,1)}), bf16[32,64,256]{2,1,0:T(8,128)(2,1)}, u32[]{:S(2)}, u32[]{:S(2)}) async-start(bf16[32,64,256]{2,1,0:T(8,128)(2,1)} %bitcast.3), calls=%async_computation | async-start | bytes 2097152 | tf_op jit(solution)/shard_map/all_to_all | solution.py:319
  11.6 0.3 copy.17
  11.9 0.0 copy-start
  12.0 5.7 %collective-permute-start = (bf16[4,128,256]{2,1,0:T(8,128)(2,1)S(1)}, bf16[4,128,256]{2,1,0:T(8,128)(2,1)S(1)}, u32[]{:S(2)}, u32[]{:S(2)}) collective-permute-start(bf16[4,128,256]{2,1,0:T(8,128)(2,1)S(1)} %slice_select_fusion.1), channel_id=1, source_target_pairs={{0,224},{32,0},{64,32},{96,64},{128,96},{160,128},{192,160},{224,1... | collective-permute-start | bytes 786440 | tf_op jit(solution)/shard_map/ppermute | solution.py:348
  17.6 0.3 copy.19
  18.0 0.8 collective-permute-start.1
  18.8 0.6 pad_add_fusion.place
  19.4 1.2 %copy_bitcast_fusion = (bf16[8,256,128]{2,1,0:T(8,128)(2,1)}, bf16[8,256,128]{2,1,0:T(8,128)(2,1)}) fusion(bf16[256,8,128]{2,1,0:T(8,128)(2,1)S(1)} %copy-done.3, bf16[256,8,128]{2,1,0:T(8,128)(2,1)S(1)} %copy-done.2), kind=kLoop, calls=%fused_computation.1 | loop fusion | bytes 2097152 | tf_op jit(solution)/shard_map/transpose | solution.py:342
  20.6 2.4 %collective-permute-done.q_t_next_in = bf16[4,128,256]{2,1,0:T(8,128)(2,1)S(1)} collective-permute-done((bf16[4,128,256]{2,1,0:T(8,128)(2,1)S(1)}, bf16[4,128,256]{2,1,0:T(8,128)(2,1)S(1)}, u32[]{:S(2)}, u32[]{:S(2)}) %collective-permute-start) | collective-permute-done | bytes 262176 | tf_op jit(solution)/shard_map/ppermute | solution.py:348
  23.0 5.8 %all-to-all-done = bf16[32,64,256]{2,1,0:T(8,128)(2,1)} async-done(((bf16[32,64,256]{2,1,0:T(8,128)(2,1)}), bf16[32,64,256]{2,1,0:T(8,128)(2,1)}, u32[]{:S(2)}, u32[]{:S(2)}) %all-to-all-start) | async-done | bytes 1048608 | tf_op jit(solution)/shard_map/all_to_all | solution.py:319
  28.7 8.6 %shard_map.75 = (bf16[8,128,256]{2,1,0:T(8,128)(2,1)}, bf16[4,144,256]{2,1,0:T(8,128)(2,1)}, bf16[4,144,256]{2,1,0:T(8,128)(2,1)}, f32[4,256]{1,0:T(4,128)}, f32[4,256]{1,0:T(4,128)}) custom-call(s32[2]{0:T(128)} %pad_add_fusion.place, bf16[4,512,256]{2,1,0:T(8,128)(2,1)} %bitcast.4.kv_in, bf16[8,128,256]{2,1,0:T(8,128)(2,1)} %bitcast.20, ...), custom_call_target="tpu_custom_call" | custom-call | flops 12884901888 | bytes 4194304 | tf_op jit(solution)/shard_map/pallas_call | solution.py:301
  37.3 5.6 %collective-permute-start.3 = (bf16[4,144,256]{2,1,0:T(8,128)(2,1)}, bf16[4,144,256]{2,1,0:T(8,128)(2,1)S(1)}, u32[]{:S(2)}, u32[]{:S(2)}) collective-permute-start(bf16[4,144,256]{2,1,0:T(8,128)(2,1)} %get-tuple-element.15.mine_in), channel_id=1, source_target_pairs={{0,224},{32,0},{64,32},{96,64},{128,96},{160,128},{192,160},{224,1... | collective-permute-start | bytes 884744 | tf_op jit(solution)/shard_map/ppermute | solution.py:375
  42.9 0.0 collective-permute-start.2
  42.9 4.5 %shard_map.76 = (bf16[4,128,256]{2,1,0:T(8,128)(2,1)}, f32[4,512,256]{2,1,0:T(8,128)}) custom-call(s32[2]{0:T(128)} %pad_add_fusion.place, bf16[4,512,256]{2,1,0:T(8,128)(2,1)} %bitcast.4.kv_in, bf16[8,128,256]{2,1,0:T(8,128)(2,1)} %bitcast.21, bf16[8,256,128]{2,1,0:T(8,128)(2,1)} %get-tuple-element.39.q_in, bf16[8,128,256]{2,1,0:T(8,128)(2,1)} %bitcast.25, ...), custom_call_target="tpu_custom_call" | custom-call | flops 8589934592 | bytes 4194304 | tf_op jit(solution)/shard_map/pallas_call | solution.py:301
  47.5 0.0 collective-permute-done.1.g_t_next_in
  47.5 1.7 %collective-permute-done.3.after_in = bf16[4,144,256]{2,1,0:T(8,128)(2,1)S(1)} collective-permute-done((bf16[4,144,256]{2,1,0:T(8,128)(2,1)}, bf16[4,144,256]{2,1,0:T(8,128)(2,1)S(1)}, u32[]{:S(2)}, u32[]{:S(2)}) %collective-permute-start.3) | collective-permute-done | bytes 294944 | tf_op jit(solution)/shard_map/ppermute | solution.py:375
  49.2 3.0 %collective-permute-done.2.before_in = bf16[4,144,256]{2,1,0:T(8,128)(2,1)S(1)} collective-permute-done((bf16[4,144,256]{2,1,0:T(8,128)(2,1)}, bf16[4,144,256]{2,1,0:T(8,128)(2,1)S(1)}, u32[]{:S(2)}, u32[]{:S(2)}) %collective-permute-start.2) | collective-permute-done | bytes 294944 | tf_op jit(solution)/shard_map/ppermute | solution.py:374
  52.2 0.7 copy-done.8
  53.0 10.9 %shard_map.77 = (bf16[8,128,256]{2,1,0:T(8,128)(2,1)}, bf16[4,128,256]{2,1,0:T(8,128)(2,1)}, bf16[4,128,256]{2,1,0:T(8,128)(2,1)}, bf16[4,512,256]{2,1,0:T(8,128)(2,1)}) custom-call(s32[2]{0:T(128)} %pad_add_fusion.place, bf16[4,512,256]{2,1,0:T(8,128)(2,1)} %bitcast.4.kv_in, bf16[8,128,256]{2,1,0:T(8,128)(2,1)} %bitcast.22, ...), custom_call_target="tpu_custom_call", output_to_operand_aliasing={{0}: (13, {})} | custom-call | flops 17179869184 | bytes 4194304 | tf_op jit(solution)/shard_map/pallas_call | solution.py:301
  63.9 11.7 %all-to-all-start.1 = ((bf16[32,64,256]{2,1,0:T(8,128)(2,1)}), bf16[32,64,256]{2,1,0:T(8,128)(2,1)S(1)}, u32[]{:S(2)}, u32[]{:S(2)}) async-start(bf16[32,64,256]{2,1,0:T(8,128)(2,1)} %bitcast.27), calls=%async_computation.1 | async-start | bytes 2097152 | tf_op jit(solution)/shard_map/all_to_all | solution.py:324
  75.6 0.1 collective-permute-start.4
  75.7 1.1 %copy.21 = bf16[256,8,128]{2,1,0:T(8,128)(2,1)} copy(bf16[256,8,128]{0,2,1:T(8,128)(2,1)S(1)} %bitcast.29) | data formatting | bytes 1048576
  76.8 7.7 %collective-permute-done.4 = bf16[4,128,256]{2,1,0:T(8,128)(2,1)S(1)} collective-permute-done((bf16[4,128,256]{2,1,0:T(8,128)(2,1)S(1)}, bf16[4,128,256]{2,1,0:T(8,128)(2,1)S(1)}, u32[]{:S(2)}, u32[]{:S(2)}) %collective-permute-start.4) | collective-permute-done | bytes 262176 | tf_op jit(solution)/shard_map/ppermute | solution.py:408
  84.5 0.1 broadcast_select_fusion.1
  84.7 1.1 %copy.22 = bf16[256,8,128]{2,1,0:T(8,128)(2,1)} copy(bf16[256,8,128]{0,2,1:T(8,128)(2,1)S(1)} %maximum_bitcast_fusion) | data formatting | bytes 1048576
  85.8 6.9 %all-to-all-done.1 = bf16[32,64,256]{2,1,0:T(8,128)(2,1)S(1)} async-done(((bf16[32,64,256]{2,1,0:T(8,128)(2,1)}), bf16[32,64,256]{2,1,0:T(8,128)(2,1)S(1)}, u32[]{:S(2)}, u32[]{:S(2)}) %all-to-all-start.1) | async-done | bytes 1048608 | tf_op jit(solution)/shard_map/all_to_all | solution.py:324
  92.7 0.1 reduce_sum.12
  92.9 0.7 copy.24
  93.6 0.7 copy.23
  (24 shorter events, 0.2 us)
Async XLA Ops:
  0.6 10.9 %copy-start.2 = (bf16[256,8,128]{2,1,0:T(8,128)(2,1)S(1)}, bf16[256,8,128]{2,1,0:T(8,128)(2,1)}, u32[]{:S(2)}) copy-start(bf16[256,8,128]{2,1,0:T(8,128)(2,1)} %param.4) | copy-start | bytes 1572868
  2.8 14.8 %copy-start.3 = (bf16[256,8,128]{2,1,0:T(8,128)(2,1)S(1)}, bf16[256,8,128]{2,1,0:T(8,128)(2,1)}, u32[]{:S(2)}) copy-start(bf16[256,8,128]{2,1,0:T(8,128)(2,1)} %param.7) | copy-start | bytes 1572868
  2.8 25.9 %all-to-all-start = ((bf16[32,64,256]{2,1,0:T(8,128)(2,1)}), bf16[32,64,256]{2,1,0:T(8,128)(2,1)}, u32[]{:S(2)}, u32[]{:S(2)}) async-start(bf16[32,64,256]{2,1,0:T(8,128)(2,1)} %bitcast.3), calls=%async_computation | async-start | bytes 2097152 | tf_op jit(solution)/shard_map/all_to_all | solution.py:319
  11.9 8.7 %copy-start = (bf16[256,8,128]{0,2,1:T(8,128)(2,1)}, bf16[256,8,128]{0,2,1:T(8,128)(2,1)S(1)}, u32[]{:S(2)}) copy-start(bf16[256,8,128]{0,2,1:T(8,128)(2,1)S(1)} %copy.17) | copy-start | bytes 1572868
  12.0 11.0 %collective-permute-start = (bf16[4,128,256]{2,1,0:T(8,128)(2,1)S(1)}, bf16[4,128,256]{2,1,0:T(8,128)(2,1)S(1)}, u32[]{:S(2)}, u32[]{:S(2)}) collective-permute-start(bf16[4,128,256]{2,1,0:T(8,128)(2,1)S(1)} %slice_select_fusion.1), channel_id=1, source_target_pairs={{0,224},{32,0},{64,32},{96,64},{128,96},{160,128},{192,160},{224,1... | collective-permute-start | bytes 786440 | tf_op jit(solution)/shard_map/ppermute | solution.py:348
  17.9 5.0 %copy-start.1 = (bf16[256,8,128]{0,2,1:T(8,128)(2,1)}, bf16[256,8,128]{0,2,1:T(8,128)(2,1)S(1)}, u32[]{:S(2)}) copy-start(bf16[256,8,128]{0,2,1:T(8,128)(2,1)S(1)} %copy.19) | copy-start | bytes 1572868
  18.0 29.5 %collective-permute-start.1 = (bf16[4,128,256]{2,1,0:T(8,128)(2,1)S(1)}, bf16[4,128,256]{2,1,0:T(8,128)(2,1)}, u32[]{:S(2)}, u32[]{:S(2)}) collective-permute-start(bf16[4,128,256]{2,1,0:T(8,128)(2,1)S(1)} %slice_select_fusion), channel_id=1, source_target_pairs={{0,224},{32,0},{64,32},{96,64},{128,96},{160,128},{192,160},{224,1... | collective-permute-start | bytes 786440 | tf_op jit(solution)/shard_map/ppermute | solution.py:349
  23.0 5.8 %copy-start.9 = (bf16[4,128,256]{2,1,0:T(8,128)(2,1)}, bf16[4,128,256]{2,1,0:T(8,128)(2,1)S(1)}, u32[]{:S(2)}) copy-start(bf16[4,128,256]{2,1,0:T(8,128)(2,1)S(1)} %collective-permute-done.q_t_next_in) | copy-start | bytes 786436
  37.3 11.9 %collective-permute-start.3 = (bf16[4,144,256]{2,1,0:T(8,128)(2,1)}, bf16[4,144,256]{2,1,0:T(8,128)(2,1)S(1)}, u32[]{:S(2)}, u32[]{:S(2)}) collective-permute-start(bf16[4,144,256]{2,1,0:T(8,128)(2,1)} %get-tuple-element.15.mine_in), channel_id=1, source_target_pairs={{0,224},{32,0},{64,32},{96,64},{128,96},{160,128},{192,160},{224,1... | collective-permute-start | bytes 884744 | tf_op jit(solution)/shard_map/ppermute | solution.py:375
  42.9 9.3 %collective-permute-start.2 = (bf16[4,144,256]{2,1,0:T(8,128)(2,1)}, bf16[4,144,256]{2,1,0:T(8,128)(2,1)S(1)}, u32[]{:S(2)}, u32[]{:S(2)}) collective-permute-start(bf16[4,144,256]{2,1,0:T(8,128)(2,1)} %get-tuple-element.16.next_in), channel_id=1, source_target_pairs={{0,32},{32,64},{64,96},{96,128},{128,160},{160,192},{192,224},{224... | collective-permute-start | bytes 884744 | tf_op jit(solution)/shard_map/ppermute | solution.py:374
  49.2 3.0 %copy-start.7 = (bf16[4,144,256]{2,1,0:T(8,128)(2,1)}, bf16[4,144,256]{2,1,0:T(8,128)(2,1)S(1)}, u32[]{:S(2)}) copy-start(bf16[4,144,256]{2,1,0:T(8,128)(2,1)S(1)} %collective-permute-done.3.after_in) | copy-start | bytes 884740
  52.2 0.7 copy-start.8
  63.8 11.7 %copy-start.10 = (bf16[4,128,256]{2,1,0:T(8,128)(2,1)S(1)}, bf16[4,128,256]{2,1,0:T(8,128)(2,1)}, u32[]{:S(2)}) copy-start(bf16[4,128,256]{2,1,0:T(8,128)(2,1)} %get-tuple-element.24) | copy-start | bytes 786436
  63.8 11.8 %copy-start.4 = (bf16[8,128,256]{2,1,0:T(8,128)(2,1)S(1)}, bf16[8,128,256]{2,1,0:T(8,128)(2,1)}, u32[]{:S(2)}) copy-start(bf16[8,128,256]{2,1,0:T(8,128)(2,1)} %get-tuple-element.21) | copy-start | bytes 1572868
  63.8 20.7 %copy-start.5 = (bf16[4,128,256]{2,1,0:T(8,128)(2,1)S(1)}, bf16[4,128,256]{2,1,0:T(8,128)(2,1)}, u32[]{:S(2)}) copy-start(bf16[4,128,256]{2,1,0:T(8,128)(2,1)} %get-tuple-element.22) | copy-start | bytes 786436
  63.9 20.6 %copy-start.6 = (bf16[4,128,256]{2,1,0:T(8,128)(2,1)S(1)}, bf16[4,128,256]{2,1,0:T(8,128)(2,1)}, u32[]{:S(2)}) copy-start(bf16[4,128,256]{2,1,0:T(8,128)(2,1)} %get-tuple-element.23) | copy-start | bytes 786436
  63.9 28.8 %all-to-all-start.1 = ((bf16[32,64,256]{2,1,0:T(8,128)(2,1)}), bf16[32,64,256]{2,1,0:T(8,128)(2,1)S(1)}, u32[]{:S(2)}, u32[]{:S(2)}) async-start(bf16[32,64,256]{2,1,0:T(8,128)(2,1)} %bitcast.27), calls=%async_computation.1 | async-start | bytes 2097152 | tf_op jit(solution)/shard_map/all_to_all | solution.py:324
  75.6 8.9 %collective-permute-start.4 = (bf16[4,128,256]{2,1,0:T(8,128)(2,1)S(1)}, bf16[4,128,256]{2,1,0:T(8,128)(2,1)S(1)}, u32[]{:S(2)}, u32[]{:S(2)}) collective-permute-start(bf16[4,128,256]{2,1,0:T(8,128)(2,1)S(1)} %copy-done.10), channel_id=1, source_target_pairs={{0,32},{32,64},{64,96},{96,128},{128,160},{160,192},{192,224},{224... | collective-permute-start | bytes 786440 | tf_op jit(solution)/shard_map/ppermute | solution.py:408

commit v5 on v4

--- a/solution.py
+++ b/solution.py
@@ -59,7 +59,8 @@
 
 
 def backward_tile(
-    place, kv, lo, hi, q_t, q, g_t, g, log_total, delta, dq_t, scores, grads, probs, ds, masked, ready=None
+    place, kv, lo, hi, q_t, q, g_t, g, log_total, delta, dq_t, scores, grads, probs, ds, masked,
+    ready=None,
 ):
     key = kv[:, :DIM]
     value = kv[:, DIM:]
@@ -124,9 +125,9 @@
 
 
 def forward(
-    place, kv_in, q_t_in, q_t_next_in, g_t_in,
-    out_out, mine_out, next_out, log_narrow, delta_narrow,
-    kv, q_t, g_t, acc, out, mine, nexts, top, total, scores, sems, out_sems,
+    place, kv_in, q_t_in, q_t_next_in,
+    mine_out, next_out, narrow_out,
+    kv, q_t, acc, mine, nexts, narrows, top, total, scores, sems, out_sems,
 ):
     rank = place[0]
     wide = place[1]
@@ -136,11 +137,10 @@
             (q_t_in, q_t.at[pl.ds(0, HEADS)]),
             (q_t_next_in, q_t.at[pl.ds(HEADS, HALF)]),
             (kv_in, kv),
-            (g_t_in.at[pl.ds(narrow, HALF)], g_t),
         ],
         sems,
     )
-    wait_all(loads[:3])
+    wait_all(loads)
     every = HEADS + HALF
     mine_at = lax.div(rank, TILE // BLOCK)
     forward_tile(place, kv[mine_at], 0, every, q_t, acc, top, total, scores, True, HEADS)
@@ -163,31 +163,34 @@
     for h in range(HALF):
         nexts[h] = pack(*result(HEADS + h))
         mine[h] = pack(*result(wide + h))
-    stores = start_all([(nexts, next_out), (mine, mine_out)], out_sems)
-    loads[3].wait()
-    for h in range(HALF):
-        o, log_h = result(narrow + h)
-        out[h], delta_narrow[h : h + 1, :] = finish(o, g_t[h])
-        log_narrow[h : h + 1, :] = log_h
-    last = pltpu.make_async_copy(out, out_out.at[pl.ds(narrow, HALF)], out_sems.at[2])
-    last.start()
-    wait_all(stores)
-    last.wait()
+        narrows[h] = pack(*result(narrow + h))
+    wait_all(start_all([(nexts, next_out), (mine, mine_out), (narrows, narrow_out)], out_sems))
 
 
 def backward_narrow(
-    place, kv_in, q_t_in, q_in, g_t_in, g_in, log_narrow, delta_narrow,
-    dq_out, dkv_out,
-    kv, q_t, q, g_t, g, dq_t, dq, dkv, scores, grads, probs, ds, sems, tile_sems,
+    place, kv_in, q_t_in, q_in, g_t_in, g_in, packed_in,
+    out_out, dq_out, dkv_out,
+    kv, q_t, q, g_t, g, packed, out, dq_t, dq, dkv, log_narrow, delta_narrow, scores, grads, probs, ds,
+    sems, out_sems, tile_sems,
 ):
     mine_at = lax.div(place[0], TILE // BLOCK)
     part = pl.ds(HALF - place[1], HALF)
     loads = start_all(
-        [(q_t_in.at[part], q_t), (kv_in, kv), (g_t_in.at[part], g_t), (g_in.at[part], g), (q_in.at[part], q)],
+        [
+            (packed_in, packed), (g_t_in.at[part], g_t), (q_t_in.at[part], q_t), (kv_in, kv),
+            (g_in.at[part], g), (q_in.at[part], q),
+        ],
         sems,
     )
+    out_store = pltpu.make_async_copy(out, out_out.at[part], out_sems.at[0])
+
     dq_t[...] = jnp.zeros_like(dq_t)
-    wait_all(loads[:3])
+    wait_all(loads[:2])
+    for h in range(HALF):
+        out[h], delta_narrow[h : h + 1, :] = finish(packed[h, :DIM].astype(F32), g_t[h])
+        log_narrow[h : h + 1, :] = log_of(packed[h])
+    out_store.start()
+    wait_all(loads[2:4])
 
     def store(b):
         return pltpu.make_async_copy(dkv.at[b], dkv_out.at[b], tile_sems.at[b])
@@ -199,7 +202,7 @@
         )
         store(b).start()
 
-    tile(mine_at, HALF, lambda: wait_all(loads[3:]))
+    tile(mine_at, HALF, lambda: wait_all(loads[4:]))
 
     def below(b, carry):
         tile(b, 0)
@@ -207,7 +210,7 @@
 
     lax.fori_loop(0, mine_at, below, 0)
     dq[...] = (dq_t[...] * SCALE).astype(BF16)
-    last = pltpu.make_async_copy(dq, dq_out, sems.at[5])
+    last = pltpu.make_async_copy(dq, dq_out, out_sems.at[1])
     last.start()
 
     def settle(b, carry):
@@ -216,6 +219,7 @@
 
     lax.fori_loop(0, mine_at + 1, settle, 0)
     last.wait()
+    out_store.wait()
 
 
 def backward_wide(
@@ -359,32 +363,30 @@
     square = (HEADS, TILE, BLOCK)
     small = (HALF, TILE, BLOCK)
     kv_shape = (TILES, TILE, 2 * DIM)
-    out_t, mine, nexts, log_narrow, delta_narrow = call(
+    mine, nexts, narrows = call(
         forward,
-        [(full_t, BF16, FAR), (packed, BF16, FAR), (packed, BF16, FAR), (few, F32, NEAR), (few, F32, NEAR)],
-        [(place, None), (own, FAR), (q_t, FAR), (q_t_next, FAR), (g_t, FAR)],
-        [
-            (kv_shape, BF16), ((every, DIM, BLOCK), BF16), (half_t, BF16), ((every, DIM, BLOCK), F32),
-            (half_t, BF16), (packed, BF16), (packed, BF16), ((2 * HEADS, BLOCK), F32), ((2 * HEADS, BLOCK), F32),
+        [(packed, BF16, FAR), (packed, BF16, FAR), (packed, BF16, FAR)],
+        [(place, None), (own, FAR), (q_t, FAR), (q_t_next, FAR)],
+        [
+            (kv_shape, BF16), ((every, DIM, BLOCK), BF16), ((every, DIM, BLOCK), F32),
+            (packed, BF16), (packed, BF16), (packed, BF16), ((2 * HEADS, BLOCK), F32), ((2 * HEADS, BLOCK), F32),
             ((every, TILE, BLOCK), F32),
         ],
-        [4, 3],
+        [3, 3],
         12 << 30,
     )
     before = lax.ppermute(nexts, "z", ring(planes, 1))
     after = lax.ppermute(mine, "z", ring(planes, -1))
-    dq_narrow, dkv_narrow = call(
+    out_t, dq_narrow, dkv_narrow = call(
         backward_narrow,
-        [(half_t, BF16, FAR), (kv_shape, F32, FAR)],
-        [
-            (place, None), (own, FAR), (q_t, FAR), (q, FAR), (g_t, FAR), (g, FAR),
-            (log_narrow, NEAR), (delta_narrow, NEAR),
-        ],
-        [
-            (kv_shape, BF16), (half_t, BF16), (half, BF16), (half_t, BF16), (half, BF16), (half_t, F32),
-            (half_t, BF16), (kv_shape, F32), (small, F32), (small, F32), (small, BF16), (small, BF16),
-        ],
-        [6, TILES],
+        [(full_t, BF16, FAR), (half_t, BF16, FAR), (kv_shape, F32, FAR)],
+        [(place, None), (own, FAR), (q_t, FAR), (q, FAR), (g_t, FAR), (g, FAR), (narrows, FAR)],
+        [
+            (kv_shape, BF16), (half_t, BF16), (half, BF16), (half_t, BF16), (half, BF16), (packed, BF16),
+            (half_t, BF16), (half_t, F32), (half_t, BF16), (kv_shape, F32), (few, F32), (few, F32),
+            (small, F32), (small, F32), (small, BF16), (small, BF16),
+        ],
+        [6, 2, TILES],
         8 << 30,
     )
     out_t, dq_wide, dq_next, dkv = call(

time: 94.7 us -> 94.1 us (level)
  transfers between devices with their start and end apart: 7 -> 7, of which waited for: 6 -> 6; matrix products, arithmetic and copies ran while one was open for 5% -> 5% of each run, Pallas kernels for 14% -> 13%
where the time goes in v5:
time: 94.1 us; the launch traced here: 93.7 us
  starting transfers between devices  32.7 us (35%)
  waiting for transfers between devices  27.5 us (29%)
  Pallas kernels  23.4 us (25%)
  local copies, waits for them, and re-layouts  7.25 us (8%)
  other arithmetic  1.97 us (2%)
    pallas_call x3, Pallas kernels, call(): pl.pallas_call(body, out_shape=[jax.ShapeDtypeStruct(s, t) for s, t, _ in...  23.4 us
    all_to_all x1, starting transfers between devices, collect(): lax.all_to_all(grads.reshape(4 * RANKS, 64, 2 * DIM), PLANE, 0, 0, tiled=...  11.7 us
    all_to_all x1, starting transfers between devices, spread(): got = lax.all_to_all(many, PLANE, 0, 0, tiled=True)  8.76 us
    ppermute x1, waiting for transfers between devices, per_device(): dq_back = lax.ppermute(dq_next, 'z', ring(planes, 1))  7.74 us
    all_to_all x1, waiting for transfers between devices, collect(): lax.all_to_all(grads.reshape(4 * RANKS, 64, 2 * DIM), PLANE, 0, 0, tiled=...  6.93 us
    all_to_all x1, waiting for transfers between devices, spread(): got = lax.all_to_all(many, PLANE, 0, 0, tiled=True)  5.75 us
    ppermute x1, starting transfers between devices, per_device(): q_t_next = lax.ppermute(widest(q_t), 'z', ring(planes, -1))  5.65 us
    ppermute x1, starting transfers between devices, per_device(): after = lax.ppermute(mine, 'z', ring(planes, -1))  5.65 us
  transfers between devices with their start and end apart: 7, of which 6 were waited for; matrix products, arithmetic and copies ran while one was open for 5% of the time, Pallas kernels for 13%

profile of v5, /device:TPU:1, one launch (start us, length us, event | category | flops | bytes accessed | tf_op | source)
XLA Modules:
  0.0 93.7 jit_solution(5978049347862069926)
XLA Ops:
  0.6 0.0 copy-start.2
  0.6 1.0 %maximum_bitcast_fusion.1 = bf16[4,64,256]{2,0,1:T(4,128)(2,1)S(1)} fusion(bf16[64,4,128]{2,1,0:T(4,128)(2,1)} %param.6, bf16[64,4,128]{2,1,0:T(4,128)(2,1)} %param.5), kind=kLoop, calls=%fused_computation.8 | loop fusion | flops 262144 | bytes 262144 | tf_op jit(solution)/shard_map/transpose | solution.py:337
  1.7 1.1 %broadcast_in_dim.2 = bf16[8,4,64,256]{3,2,1,0:T(8,128)(2,1)} broadcast(bf16[4,64,256]{2,1,0:T(8,128)(2,1)S(1)} %copy.16), dimensions={1,2,3} | broadcast | bytes 1179648 | tf_op jit(solution)/shard_map/broadcast_in_dim | solution.py:322
  2.8 8.8 %all-to-all-start = ((bf16[32,64,256]{2,1,0:T(8,128)(2,1)}), bf16[32,64,256]{2,1,0:T(8,128)(2,1)}, u32[]{:S(2)}, u32[]{:S(2)}) async-start(bf16[32,64,256]{2,1,0:T(8,128)(2,1)} %bitcast.3), calls=%async_computation | async-start | bytes 2097152 | tf_op jit(solution)/shard_map/all_to_all | solution.py:323
  11.6 0.3 copy.17
  11.9 0.0 copy-start
  12.0 5.7 %collective-permute-start = (bf16[4,128,256]{2,1,0:T(8,128)(2,1)S(1)}, bf16[4,128,256]{2,1,0:T(8,128)(2,1)S(1)}, u32[]{:S(2)}, u32[]{:S(2)}) collective-permute-start(bf16[4,128,256]{2,1,0:T(8,128)(2,1)S(1)} %slice_select_fusion.1), channel_id=1, source_target_pairs={{0,224},{32,0},{64,32},{96,64},{128,96},{160,128},{192,160},{224,1... | collective-permute-start | bytes 786440 | tf_op jit(solution)/shard_map/ppermute | solution.py:352
  17.6 0.3 copy.19
  18.0 0.8 collective-permute-start.1
  18.8 0.6 pad_add_fusion.place
  19.4 1.2 %copy_bitcast_fusion = (bf16[8,256,128]{2,1,0:T(8,128)(2,1)}, bf16[8,256,128]{2,1,0:T(8,128)(2,1)}) fusion(bf16[256,8,128]{2,1,0:T(8,128)(2,1)S(1)} %copy-done.3, bf16[256,8,128]{2,1,0:T(8,128)(2,1)S(1)} %copy-done.2), kind=kLoop, calls=%fused_computation.1 | loop fusion | bytes 2097152 | tf_op jit(solution)/shard_map/transpose | solution.py:346
  20.6 2.4 %collective-permute-done.q_t_next_in = bf16[4,128,256]{2,1,0:T(8,128)(2,1)S(1)} collective-permute-done((bf16[4,128,256]{2,1,0:T(8,128)(2,1)S(1)}, bf16[4,128,256]{2,1,0:T(8,128)(2,1)S(1)}, u32[]{:S(2)}, u32[]{:S(2)}) %collective-permute-start) | collective-permute-done | bytes 262176 | tf_op jit(solution)/shard_map/ppermute | solution.py:352
  23.0 5.8 %all-to-all-done = bf16[32,64,256]{2,1,0:T(8,128)(2,1)} async-done(((bf16[32,64,256]{2,1,0:T(8,128)(2,1)}), bf16[32,64,256]{2,1,0:T(8,128)(2,1)}, u32[]{:S(2)}, u32[]{:S(2)}) %all-to-all-start) | async-done | bytes 1048608 | tf_op jit(solution)/shard_map/all_to_all | solution.py:323
  28.7 8.0 %shard_map.75 = (bf16[4,144,256]{2,1,0:T(8,128)(2,1)}, bf16[4,144,256]{2,1,0:T(8,128)(2,1)}, bf16[4,144,256]{2,1,0:T(8,128)(2,1)}) custom-call(s32[2]{0:T(128)} %pad_add_fusion.place, bf16[4,512,256]{2,1,0:T(8,128)(2,1)} %bitcast.4.kv_in, bf16[8,128,256]{2,1,0:T(8,128)(2,1)} %bitcast.20, bf16[4,128,256]{2,1,0:T(8,128)(2,1)} %copy-done.9), custom_call_target="tpu_custom_call" | custom-call | flops 12884901888 | bytes 4194304 | tf_op jit(solution)/shard_map/pallas_call | solution.py:305
  36.7 5.7 %collective-permute-start.3 = (bf16[4,144,256]{2,1,0:T(8,128)(2,1)}, bf16[4,144,256]{2,1,0:T(8,128)(2,1)S(1)}, u32[]{:S(2)}, u32[]{:S(2)}) collective-permute-start(bf16[4,144,256]{2,1,0:T(8,128)(2,1)} %get-tuple-element.14.mine_in), channel_id=1, source_target_pairs={{0,224},{32,0},{64,32},{96,64},{128,96},{160,128},{192,160},{224,1... | collective-permute-start | bytes 884744 | tf_op jit(solution)/shard_map/ppermute | solution.py:379
  42.4 0.0 collective-permute-start.2
  42.4 4.6 %shard_map.76 = (bf16[8,128,256]{2,1,0:T(8,128)(2,1)}, bf16[4,128,256]{2,1,0:T(8,128)(2,1)}, f32[4,512,256]{2,1,0:T(8,128)}) custom-call(s32[2]{0:T(128)} %pad_add_fusion.place, bf16[4,512,256]{2,1,0:T(8,128)(2,1)} %bitcast.4.kv_in, bf16[8,128,256]{2,1,0:T(8,128)(2,1)} %bitcast.21, bf16[8,256,128]{2,1,0:T(8,128)(2,1)} %get-tuple-element.37.q_in, ...), custom_call_target="tpu_custom_call" | custom-call | flops 8589934592 | bytes 4194304 | tf_op jit(solution)/shard_map/pallas_call | solution.py:305
  47.0 0.0 collective-permute-done.1.g_t_next_in
  47.0 1.6 %collective-permute-done.3.after_in = bf16[4,144,256]{2,1,0:T(8,128)(2,1)S(1)} collective-permute-done((bf16[4,144,256]{2,1,0:T(8,128)(2,1)}, bf16[4,144,256]{2,1,0:T(8,128)(2,1)S(1)}, u32[]{:S(2)}, u32[]{:S(2)}) %collective-permute-start.3) | collective-permute-done | bytes 294944 | tf_op jit(solution)/shard_map/ppermute | solution.py:379
  48.6 3.0 %collective-permute-done.2.before_in = bf16[4,144,256]{2,1,0:T(8,128)(2,1)S(1)} collective-permute-done((bf16[4,144,256]{2,1,0:T(8,128)(2,1)}, bf16[4,144,256]{2,1,0:T(8,128)(2,1)S(1)}, u32[]{:S(2)}, u32[]{:S(2)}) %collective-permute-start.2) | collective-permute-done | bytes 294944 | tf_op jit(solution)/shard_map/ppermute | solution.py:378
  51.7 0.7 copy-done.8
  52.4 10.9 %shard_map.77 = (bf16[8,128,256]{2,1,0:T(8,128)(2,1)}, bf16[4,128,256]{2,1,0:T(8,128)(2,1)}, bf16[4,128,256]{2,1,0:T(8,128)(2,1)}, bf16[4,512,256]{2,1,0:T(8,128)(2,1)}) custom-call(s32[2]{0:T(128)} %pad_add_fusion.place, bf16[4,512,256]{2,1,0:T(8,128)(2,1)} %bitcast.4.kv_in, bf16[8,128,256]{2,1,0:T(8,128)(2,1)} %bitcast.22, ...), custom_call_target="tpu_custom_call", output_to_operand_aliasing={{0}: (13, {})} | custom-call | flops 17179869184 | bytes 4194304 | tf_op jit(solution)/shard_map/pallas_call | solution.py:305
  63.3 11.7 %all-to-all-start.1 = ((bf16[32,64,256]{2,1,0:T(8,128)(2,1)}), bf16[32,64,256]{2,1,0:T(8,128)(2,1)S(1)}, u32[]{:S(2)}, u32[]{:S(2)}) async-start(bf16[32,64,256]{2,1,0:T(8,128)(2,1)} %bitcast.26), calls=%async_computation.1 | async-start | bytes 2097152 | tf_op jit(solution)/shard_map/all_to_all | solution.py:328
  75.0 0.1 collective-permute-start.4
  75.1 1.1 %copy.21 = bf16[256,8,128]{2,1,0:T(8,128)(2,1)} copy(bf16[256,8,128]{0,2,1:T(8,128)(2,1)S(1)} %bitcast.28) | data formatting | bytes 1048576
  76.2 7.7 %collective-permute-done.4 = bf16[4,128,256]{2,1,0:T(8,128)(2,1)S(1)} collective-permute-done((bf16[4,128,256]{2,1,0:T(8,128)(2,1)S(1)}, bf16[4,128,256]{2,1,0:T(8,128)(2,1)S(1)}, u32[]{:S(2)}, u32[]{:S(2)}) %collective-permute-start.4) | collective-permute-done | bytes 262176 | tf_op jit(solution)/shard_map/ppermute | solution.py:410
  83.9 0.1 broadcast_select_fusion.1
  84.1 1.1 %copy.22 = bf16[256,8,128]{2,1,0:T(8,128)(2,1)} copy(bf16[256,8,128]{0,2,1:T(8,128)(2,1)S(1)} %maximum_bitcast_fusion) | data formatting | bytes 1048576
  85.2 6.9 %all-to-all-done.1 = bf16[32,64,256]{2,1,0:T(8,128)(2,1)S(1)} async-done(((bf16[32,64,256]{2,1,0:T(8,128)(2,1)}), bf16[32,64,256]{2,1,0:T(8,128)(2,1)S(1)}, u32[]{:S(2)}, u32[]{:S(2)}) %all-to-all-start.1) | async-done | bytes 1048608 | tf_op jit(solution)/shard_map/all_to_all | solution.py:328
  92.1 0.1 reduce_sum.12
  92.3 0.7 copy.24
  93.0 0.7 copy.23
  (24 shorter events, 0.2 us)
Async XLA Ops:
  0.6 10.9 %copy-start.2 = (bf16[256,8,128]{2,1,0:T(8,128)(2,1)S(1)}, bf16[256,8,128]{2,1,0:T(8,128)(2,1)}, u32[]{:S(2)}) copy-start(bf16[256,8,128]{2,1,0:T(8,128)(2,1)} %param.4) | copy-start | bytes 1572868
  2.8 14.8 %copy-start.3 = (bf16[256,8,128]{2,1,0:T(8,128)(2,1)S(1)}, bf16[256,8,128]{2,1,0:T(8,128)(2,1)}, u32[]{:S(2)}) copy-start(bf16[256,8,128]{2,1,0:T(8,128)(2,1)} %param.7) | copy-start | bytes 1572868
  2.8 25.9 %all-to-all-start = ((bf16[32,64,256]{2,1,0:T(8,128)(2,1)}), bf16[32,64,256]{2,1,0:T(8,128)(2,1)}, u32[]{:S(2)}, u32[]{:S(2)}) async-start(bf16[32,64,256]{2,1,0:T(8,128)(2,1)} %bitcast.3), calls=%async_computation | async-start | bytes 2097152 | tf_op jit(solution)/shard_map/all_to_all | solution.py:323
  11.9 8.7 %copy-start = (bf16[256,8,128]{0,2,1:T(8,128)(2,1)}, bf16[256,8,128]{0,2,1:T(8,128)(2,1)S(1)}, u32[]{:S(2)}) copy-start(bf16[256,8,128]{0,2,1:T(8,128)(2,1)S(1)} %copy.17) | copy-start | bytes 1572868
  12.0 11.0 %collective-permute-start = (bf16[4,128,256]{2,1,0:T(8,128)(2,1)S(1)}, bf16[4,128,256]{2,1,0:T(8,128)(2,1)S(1)}, u32[]{:S(2)}, u32[]{:S(2)}) collective-permute-start(bf16[4,128,256]{2,1,0:T(8,128)(2,1)S(1)} %slice_select_fusion.1), channel_id=1, source_target_pairs={{0,224},{32,0},{64,32},{96,64},{128,96},{160,128},{192,160},{224,1... | collective-permute-start | bytes 786440 | tf_op jit(solution)/shard_map/ppermute | solution.py:352
  17.9 5.0 %copy-start.1 = (bf16[256,8,128]{0,2,1:T(8,128)(2,1)}, bf16[256,8,128]{0,2,1:T(8,128)(2,1)S(1)}, u32[]{:S(2)}) copy-start(bf16[256,8,128]{0,2,1:T(8,128)(2,1)S(1)} %copy.19) | copy-start | bytes 1572868
  18.0 29.0 %collective-permute-start.1 = (bf16[4,128,256]{2,1,0:T(8,128)(2,1)S(1)}, bf16[4,128,256]{2,1,0:T(8,128)(2,1)}, u32[]{:S(2)}, u32[]{:S(2)}) collective-permute-start(bf16[4,128,256]{2,1,0:T(8,128)(2,1)S(1)} %slice_select_fusion), channel_id=1, source_target_pairs={{0,224},{32,0},{64,32},{96,64},{128,96},{160,128},{192,160},{224,1... | collective-permute-start | bytes 786440 | tf_op jit(solution)/shard_map/ppermute | solution.py:353
  23.0 5.8 %copy-start.9 = (bf16[4,128,256]{2,1,0:T(8,128)(2,1)}, bf16[4,128,256]{2,1,0:T(8,128)(2,1)S(1)}, u32[]{:S(2)}) copy-start(bf16[4,128,256]{2,1,0:T(8,128)(2,1)S(1)} %collective-permute-done.q_t_next_in) | copy-start | bytes 786436
  36.7 11.9 %collective-permute-start.3 = (bf16[4,144,256]{2,1,0:T(8,128)(2,1)}, bf16[4,144,256]{2,1,0:T(8,128)(2,1)S(1)}, u32[]{:S(2)}, u32[]{:S(2)}) collective-permute-start(bf16[4,144,256]{2,1,0:T(8,128)(2,1)} %get-tuple-element.14.mine_in), channel_id=1, source_target_pairs={{0,224},{32,0},{64,32},{96,64},{128,96},{160,128},{192,160},{224,1... | collective-permute-start | bytes 884744 | tf_op jit(solution)/shard_map/ppermute | solution.py:379
  42.4 9.3 %collective-permute-start.2 = (bf16[4,144,256]{2,1,0:T(8,128)(2,1)}, bf16[4,144,256]{2,1,0:T(8,128)(2,1)S(1)}, u32[]{:S(2)}, u32[]{:S(2)}) collective-permute-start(bf16[4,144,256]{2,1,0:T(8,128)(2,1)} %get-tuple-element.15.next_in), channel_id=1, source_target_pairs={{0,32},{32,64},{64,96},{96,128},{128,160},{160,192},{192,224},{224... | collective-permute-start | bytes 884744 | tf_op jit(solution)/shard_map/ppermute | solution.py:378
  48.6 3.0 %copy-start.7 = (bf16[4,144,256]{2,1,0:T(8,128)(2,1)}, bf16[4,144,256]{2,1,0:T(8,128)(2,1)S(1)}, u32[]{:S(2)}) copy-start(bf16[4,144,256]{2,1,0:T(8,128)(2,1)S(1)} %collective-permute-done.3.after_in) | copy-start | bytes 884740
  51.7 0.7 copy-start.8
  63.2 11.8 %copy-start.10 = (bf16[4,128,256]{2,1,0:T(8,128)(2,1)S(1)}, bf16[4,128,256]{2,1,0:T(8,128)(2,1)}, u32[]{:S(2)}) copy-start(bf16[4,128,256]{2,1,0:T(8,128)(2,1)} %get-tuple-element.22) | copy-start | bytes 786436
  63.3 11.8 %copy-start.4 = (bf16[8,128,256]{2,1,0:T(8,128)(2,1)S(1)}, bf16[8,128,256]{2,1,0:T(8,128)(2,1)}, u32[]{:S(2)}) copy-start(bf16[8,128,256]{2,1,0:T(8,128)(2,1)} %get-tuple-element.19) | copy-start | bytes 1572868
  63.3 20.7 %copy-start.5 = (bf16[4,128,256]{2,1,0:T(8,128)(2,1)S(1)}, bf16[4,128,256]{2,1,0:T(8,128)(2,1)}, u32[]{:S(2)}) copy-start(bf16[4,128,256]{2,1,0:T(8,128)(2,1)} %get-tuple-element.20) | copy-start | bytes 786436
  63.3 20.7 %copy-start.6 = (bf16[4,128,256]{2,1,0:T(8,128)(2,1)S(1)}, bf16[4,128,256]{2,1,0:T(8,128)(2,1)}, u32[]{:S(2)}) copy-start(bf16[4,128,256]{2,1,0:T(8,128)(2,1)} %get-tuple-element.21) | copy-start | bytes 786436
  63.3 28.8 %all-to-all-start.1 = ((bf16[32,64,256]{2,1,0:T(8,128)(2,1)}), bf16[32,64,256]{2,1,0:T(8,128)(2,1)S(1)}, u32[]{:S(2)}, u32[]{:S(2)}) async-start(bf16[32,64,256]{2,1,0:T(8,128)(2,1)} %bitcast.26), calls=%async_computation.1 | async-start | bytes 2097152 | tf_op jit(solution)/shard_map/all_to_all | solution.py:328
  75.0 8.9 %collective-permute-start.4 = (bf16[4,128,256]{2,1,0:T(8,128)(2,1)S(1)}, bf16[4,128,256]{2,1,0:T(8,128)(2,1)S(1)}, u32[]{:S(2)}, u32[]{:S(2)}) collective-permute-start(bf16[4,128,256]{2,1,0:T(8,128)(2,1)S(1)} %copy-done.10), channel_id=1, source_target_pairs={{0,32},{32,64},{64,96},{96,128},{128,160},{160,192},{192,224},{224... | collective-permute-start | bytes 786440 | tf_op jit(solution)/shard_map/ppermute | solution.py:410
